TPU v7x, 32 devices: a whole 2x2x4 slice. The times are simulated.
32 devices in a mesh: dp: 8 (over y, x, core), tensor: 4 (over z).
Axes of the slice: x: 2, y: 2, z: 4, core: 2. Of those that a mesh axis runs over, the one named last changes fastest.
Arguments:
- tokens: bfloat16 [128, 196, 768], P(('dp', 'tensor')), may hold values from -6 to 6
- space_gain: float32 [768], replicated, may hold values from 0.5 to 1.5
- space_shift: float32 [768], replicated, may hold values from -3 to 3
- space_inproj: bfloat16 [768, 3, 768], P(None, None, 'tensor'), may hold values from -0.21875 to 0.21875
- space_bias: bfloat16 [2, 768], P(None, 'tensor'), may hold values from -3 to 3
- space_outproj: bfloat16 [768, 768], P('tensor'), may hold values from -1.75 to 1.75
- space_outbias: bfloat16 [768], replicated, may hold values from -3 to 3
- time_gain: float32 [768], replicated, may hold values from 0.5 to 1.5
- time_shift: float32 [768], replicated, may hold values from -3 to 3
- time_inproj: bfloat16 [768, 3, 768], P(None, None, 'tensor'), may hold values from -0.21875 to 0.21875
- time_bias: bfloat16 [2, 768], P(None, 'tensor'), may hold values from -3 to 3
- time_outproj: bfloat16 [768, 768], P('tensor'), may hold values from -0.5 to 0.5
- time_outbias: bfloat16 [768], replicated, may hold values from -3 to 3
- feed_gain: float32 [768], replicated, may hold values from 0.5 to 1.5
- feed_shift: float32 [768], replicated, may hold values from -3 to 3
- up_weight: bfloat16 [3072, 768], P('tensor'), may hold values from -0.21875 to 0.21875
- up_bias: bfloat16 [3072], P('tensor'), may hold values from -3 to 3
- down_weight: bfloat16 [3072, 768], P('tensor'), may hold values from -0.15625 to 0.15625
- down_bias: bfloat16 [768], replicated, may hold values from -3 to 3
- cotangent: bfloat16 [128, 196, 768], P(('dp', 'tensor')), may hold values from -6 to 6
Outputs:
- layer_out: bfloat16 [128, 196, 768], P(('dp', 'tensor'))
- input_gradient: float32 [128, 196, 768], P(('dp', 'tensor'))
- space_gain_gradient: float32 [768], replicated
- space_shift_gradient: float32 [768], replicated
- space_inproj_gradient: float32 [768, 3, 768], P(None, None, 'tensor')
- space_bias_gradient: float32 [2, 768], P(None, 'tensor')
- space_outproj_gradient: float32 [768, 768], P('tensor')
- space_outbias_gradient: float32 [768], replicated
- time_gain_gradient: float32 [768], replicated
- time_shift_gradient: float32 [768], replicated
- time_inproj_gradient: float32 [768, 3, 768], P(None, None, 'tensor')
- time_bias_gradient: float32 [2, 768], P(None, 'tensor')
- time_outproj_gradient: float32 [768, 768], P('tensor')
- time_outbias_gradient: float32 [768], replicated
- feed_gain_gradient: float32 [768], replicated
- feed_shift_gradient: float32 [768], replicated
- up_weight_gradient: float32 [3072, 768], P('tensor')
- up_bias_gradient: float32 [3072], P('tensor')
- down_weight_gradient: float32 [3072, 768], P('tensor')
- down_bias_gradient: float32 [768], replicated
All inputs are finite; a program needn't handle non-finite values.
Results may differ from a plain program's by a relative error of at most 0.013.
The roundings to bfloat16 on the way count: a program that leaves them out, or rounds other values in their place, can miss the bound.
Values may be sent and summed in bfloat16 or wider, within the bound.
A program may use at most 192 MiB of HBM per device.

v0:
```python
import jax
import jax.numpy as jnp
from jax import lax
from jax.sharding import PartitionSpec as P

HS = 64
PATCH = 196
TIMES = 16


EPSILON = 1e-06
ROOT_HALF = 0.7071067811865476
INV_ROOT_TAU = 0.3989422804014327


def layer_norm(values, gain, shift):
    center = values - jnp.mean(values, axis=-1, keepdims=True)
    second = jnp.mean(center * center, axis=-1, keepdims=True)
    return center * lax.rsqrt(second + EPSILON) * gain + shift


def gelu_exact(values):
    return 0.5 * values * (1.0 + lax.erf(values * ROOT_HALF))


def gelu_slope(values):
    return (
        0.5 * (1.0 + lax.erf(values * ROOT_HALF))
        + values * jnp.exp(-0.5 * values * values) * INV_ROOT_TAU
    )


def head_forms(batch_first):
    if batch_first:
        return ("blhe", "bmhe", "bhlm")
    return ("lbhe", "mbhe", "bhlm")


def attend(queries, keys, values, batch_first):
    query_form, key_form, score_form = head_forms(batch_first)
    qk_scale = HS ** (-0.5)
    scores = (
        jnp.einsum(
            query_form + "," + key_form + "->" + score_form,
            queries,
            keys,
            preferred_element_type=jnp.float32,
        )
        * qk_scale
    )
    top = jnp.max(scores, axis=-1, keepdims=True)
    weights = jnp.exp(scores - top)
    total = jnp.sum(weights, axis=-1, keepdims=True)
    probs = (weights / total).astype(jnp.bfloat16)
    mixed = jnp.einsum(
        score_form + "," + key_form + "->" + query_form,
        probs,
        values,
        preferred_element_type=jnp.float32,
    )
    return (mixed, top + jnp.log(total))


def attend_back(queries, keys, values, log_total, mixed_grad, batch_first):
    query_form, key_form, score_form = head_forms(batch_first)
    qk_scale = HS ** (-0.5)
    to_scores = query_form + "," + key_form + "->" + score_form
    scores = jnp.einsum(to_scores, queries, keys, preferred_element_type=jnp.float32) * qk_scale
    probs = jnp.exp(scores - log_total)
    value_grad = jnp.einsum(
        score_form + "," + query_form + "->" + key_form,
        probs.astype(jnp.bfloat16),
        mixed_grad,
        preferred_element_type=jnp.float32,
    )
    prob_grad = jnp.einsum(to_scores, mixed_grad, values, preferred_element_type=jnp.float32)
    inner = jnp.sum(prob_grad * probs, axis=-1, keepdims=True)
    score_grad = (probs * (prob_grad - inner)).astype(jnp.bfloat16)
    query_grad = (
        jnp.einsum(
            score_form + "," + key_form + "->" + query_form,
            score_grad,
            keys,
            preferred_element_type=jnp.float32,
        )
        * qk_scale
    )
    key_grad = (
        jnp.einsum(
            score_form + "," + query_form + "->" + key_form,
            score_grad,
            queries,
            preferred_element_type=jnp.float32,
        )
        * qk_scale
    )
    return (query_grad, key_grad, value_grad)


def full_rows(shard):
    return lax.all_gather(shard, "tensor", axis=0, tiled=True)


def partial_rows(make_term, own_rows):
    return lax.psum_scatter(
        make_term(jnp.int32(0), own_rows * lax.axis_size("tensor")),
        "tensor",
        scatter_dimension=0,
        tiled=True,
    )


def to_patches(frame_major, times_local):
    width = frame_major.shape[-1]
    grouped = frame_major.reshape(times_local, -1, width)
    moved = lax.all_to_all(grouped, "dp", split_axis=1, concat_axis=0, tiled=True)
    return moved.reshape(TIMES, -1, width)


def to_frames(patch_major, times_local):
    width = patch_major.shape[-1]
    grouped = patch_major.reshape(lax.axis_size("dp") * times_local, -1, width)
    moved = lax.all_to_all(grouped, "dp", split_axis=0, concat_axis=1, tiled=True)
    return moved.reshape(-1, width)


def in_weights(inproj, bias_pair):
    width = inproj.shape[2]
    weight = inproj.reshape(inproj.shape[0], 3 * width)
    zero_part = jnp.zeros((width,), jnp.float32)
    bias = jnp.concatenate(
        [bias_pair[0].astype(jnp.float32), zero_part, bias_pair[1].astype(jnp.float32)]
    )
    return (weight, bias)


def attention_forward(resid, gain, shift, weight_set, outbias, temporal, times_local):
    inproj, bias_pair, outproj = weight_set
    normed, norm_pull = jax.vjp(layer_norm, resid, gain, shift)
    rows_in = full_rows(normed.astype(jnp.bfloat16))
    weight, bias = in_weights(inproj, bias_pair)
    width = inproj.shape[2]
    projected = (jnp.dot(rows_in, weight, preferred_element_type=jnp.float32) + bias).astype(
        jnp.bfloat16
    )
    heads_here = projected.shape[-1] // (3 * HS)
    if temporal:
        projected = to_patches(projected, times_local)
        split_heads = projected.reshape(TIMES, -1, 3, heads_here, HS)
    else:
        split_heads = projected.reshape(-1, PATCH, 3, heads_here, HS)
    mixed, log_total = attend(
        split_heads[:, :, 0], split_heads[:, :, 1], split_heads[:, :, 2], not temporal
    )
    if temporal:
        mixed_low = to_frames(
            mixed.astype(jnp.bfloat16).reshape(TIMES, -1, heads_here * HS), times_local
        )
    else:
        mixed_low = mixed.astype(jnp.bfloat16).reshape(-1, width)

    def out_term(start, count):
        return jnp.dot(
            lax.dynamic_slice_in_dim(mixed_low, start, count, 0),
            outproj,
            preferred_element_type=jnp.float32,
        )

    branch = partial_rows(out_term, resid.shape[0]) + outbias.astype(jnp.float32)
    kept = (norm_pull, rows_in, split_heads, log_total, mixed_low)
    return (resid + branch, kept)


def attention_backward(upstream, kept, weight_set, temporal, times_local):
    inproj, bias_pair, outproj = weight_set
    norm_pull, rows_in, split_heads, log_total, mixed_low = kept
    contract_rows = (((0,), (0,)), ((), ()))
    contract_cols = (((1,), (1,)), ((), ()))
    branch_low = upstream.astype(jnp.bfloat16)
    outbias_grad = jnp.sum(branch_low, axis=0, dtype=jnp.float32)
    branch_rows = full_rows(branch_low)
    outproj_grad = lax.dot_general(
        mixed_low, branch_rows, contract_rows, preferred_element_type=jnp.float32
    )
    mixed_grad = lax.dot_general(
        branch_rows, outproj, contract_cols, preferred_element_type=jnp.float32
    ).astype(jnp.bfloat16)
    width = inproj.shape[2]
    heads_here = split_heads.shape[3]
    if temporal:
        mixed_grad = to_patches(mixed_grad, times_local)
    mixed_grad = mixed_grad.reshape(split_heads.shape[0], split_heads.shape[1], heads_here, HS)
    query_grad, key_grad, value_grad = attend_back(
        split_heads[:, :, 0],
        split_heads[:, :, 1],
        split_heads[:, :, 2],
        log_total,
        mixed_grad,
        not temporal,
    )
    projected_grad = jnp.stack([query_grad, key_grad, value_grad], axis=2).astype(jnp.bfloat16)
    if temporal:
        projected_grad = to_frames(
            projected_grad.reshape(TIMES, -1, 3 * heads_here * HS), times_local
        )
    else:
        projected_grad = projected_grad.reshape(-1, 3 * width)
    column_sums = jnp.sum(projected_grad, axis=0, dtype=jnp.float32).reshape(3, width)
    bias_grad = jnp.stack([column_sums[0], column_sums[2]])
    weight = inproj.reshape(inproj.shape[0], 3 * width)
    inproj_grad = lax.dot_general(
        rows_in, projected_grad, contract_rows, preferred_element_type=jnp.float32
    ).reshape(inproj.shape)

    def in_term(start, count):
        return lax.dot_general(
            lax.dynamic_slice_in_dim(projected_grad, start, count, 0),
            weight,
            contract_cols,
            preferred_element_type=jnp.float32,
        )

    normed_grad = partial_rows(in_term, upstream.shape[0])
    resid_grad, gain_grad, shift_grad = norm_pull(normed_grad)
    return (
        upstream + resid_grad,
        (gain_grad, shift_grad, inproj_grad, bias_grad, outproj_grad, outbias_grad),
    )


def per_device(
    tokens,
    space_gain,
    space_shift,
    space_inproj,
    space_bias,
    space_outproj,
    space_outbias,
    time_gain,
    time_shift,
    time_inproj,
    time_bias,
    time_outproj,
    time_outbias,
    feed_gain,
    feed_shift,
    up_weight,
    up_bias,
    down_weight,
    down_bias,
    cotangent,
):
    clips_local = min(TIMES, lax.axis_size("dp"))
    times_local = TIMES // clips_local
    own_rows = tokens.shape[0] * tokens.shape[1]
    contract_rows = (((0,), (0,)), ((), ()))
    contract_cols = (((1,), (1,)), ((), ()))
    time_set = (time_inproj, time_bias, time_outproj)
    space_set = (space_inproj, space_bias, space_outproj)
    resid = tokens.reshape(own_rows, -1).astype(jnp.float32)
    after_space, space_kept = attention_forward(
        resid, space_gain, space_shift, space_set, space_outbias, False, times_local
    )
    after_time, time_kept = attention_forward(
        after_space, time_gain, time_shift, time_set, time_outbias, True, times_local
    )
    feed_normed, feed_pull = jax.vjp(layer_norm, after_time, feed_gain, feed_shift)
    feed_low = feed_normed.astype(jnp.bfloat16)
    branch_low = cotangent.reshape(own_rows, -1)
    upstream = branch_low.astype(jnp.float32)
    down_bias_grad = jnp.sum(branch_low, axis=0, dtype=jnp.float32)
    feed_full = full_rows(feed_low)
    pre_act = lax.dot_general(
        feed_full, up_weight, contract_cols, preferred_element_type=jnp.float32
    ) + up_bias.astype(jnp.float32)
    hidden = gelu_exact(pre_act).astype(jnp.bfloat16)

    def down_term(start, count):
        return jnp.dot(hidden, down_weight, preferred_element_type=jnp.float32)

    layer_sum = after_time + partial_rows(down_term, own_rows) + down_bias.astype(jnp.float32)
    branch_full = full_rows(branch_low)
    down_grad = lax.dot_general(
        hidden, branch_full, contract_rows, preferred_element_type=jnp.float32
    )
    hidden_grad = lax.dot_general(
        branch_full, down_weight, contract_cols, preferred_element_type=jnp.float32
    )
    pre_grad = (hidden_grad * gelu_slope(pre_act)).astype(jnp.bfloat16)
    up_grad = lax.dot_general(
        pre_grad, feed_full, contract_rows, preferred_element_type=jnp.float32
    )
    up_bias_grad = jnp.sum(pre_grad, axis=0, dtype=jnp.float32)

    def up_term(start, count):
        return jnp.dot(pre_grad, up_weight, preferred_element_type=jnp.float32)

    feed_grad = partial_rows(up_term, own_rows)
    resid_part, feed_gain_grad, feed_shift_grad = feed_pull(feed_grad)
    time_upstream = upstream + resid_part
    space_upstream, time_grads = attention_backward(
        time_upstream, time_kept, time_set, True, times_local
    )
    input_grad, space_grads = attention_backward(
        space_upstream, space_kept, space_set, False, times_local
    )
    summed = lax.psum(
        (
            space_grads[2],
            space_grads[3],
            space_grads[4],
            time_grads[2],
            time_grads[3],
            time_grads[4],
            up_grad,
            up_bias_grad,
            down_grad,
        ),
        "dp",
    )
    shared = lax.psum(
        (
            space_grads[0],
            space_grads[1],
            space_grads[5],
            time_grads[0],
            time_grads[1],
            time_grads[5],
            feed_gain_grad,
            feed_shift_grad,
            down_bias_grad,
        ),
        ("dp", "tensor"),
    )
    shape_out = tokens.shape
    return (
        layer_sum.astype(jnp.bfloat16).reshape(shape_out),
        input_grad.reshape(shape_out),
        shared[0],
        shared[1],
        summed[0],
        summed[1],
        summed[2],
        shared[2],
        shared[3],
        shared[4],
        summed[3],
        summed[4],
        summed[5],
        shared[5],
        shared[6],
        shared[7],
        summed[6],
        summed[7],
        summed[8],
        shared[8],
    )


def solution(mesh):
    return jax.shard_map(
        per_device,
        mesh=mesh,
        in_specs=(
            P(("dp", "tensor"), None, None),
            P(),
            P(),
            P(None, None, "tensor"),
            P(None, "tensor"),
            P("tensor", None),
            P(),
            P(),
            P(),
            P(None, None, "tensor"),
            P(None, "tensor"),
            P("tensor", None),
            P(),
            P(),
            P(),
            P("tensor", None),
            P("tensor"),
            P("tensor", None),
            P(),
            P(("dp", "tensor"), None, None),
        ),
        out_specs=(
            P(("dp", "tensor"), None, None),
            P(("dp", "tensor"), None, None),
            P(),
            P(),
            P(None, None, "tensor"),
            P(None, "tensor"),
            P("tensor", None),
            P(),
            P(),
            P(),
            P(None, None, "tensor"),
            P(None, "tensor"),
            P("tensor", None),
            P(),
            P(),
            P(),
            P("tensor", None),
            P("tensor"),
            P("tensor", None),
            P(),
        ),
        check_vma=False,
    )
```

profile of v0, /device:TPU:0, one launch (start us, length us, event | category | flops | bytes accessed | tf_op | source)
XLA Modules:
  0.0 2200.0 jit_solution(4943705803411020907)
XLA Ops:
  19.5 93.5 %all-gather.7.cloned.1.call-done = bf16[3136,768]{1,0:T(8,128)(2,1)} async-done(((bf16[784,768]{1,0:T(8,128)(2,1)}), bf16[3136,768]{1,0:T(8,128)(2,1)}) %all-gather.7.cloned.1.call-update) | async-done | bytes 4816912 | tf_op jit(solution)/shard_map/all_gather | solution.py:101
  120.2 15.5 reshape.274
  160.2 162.2 %reduce-scatter.7.cloned.1.call-done = f32[784,768]{1,0:T(8,128)} async-done(((f32[3136,768]{1,0:T(8,128)}), f32[784,768]{1,0:T(8,128)}) %reduce-scatter.7.cloned.1.call-update) | async-done | bytes 2408464 | tf_op jit(solution)/shard_map/reduce_scatter | solution.py:105
  328.2 92.1 %all-gather.9.cloned.1.call-done = bf16[3136,768]{1,0:T(8,128)(2,1)} async-done(((bf16[784,768]{1,0:T(8,128)(2,1)}), bf16[3136,768]{1,0:T(8,128)(2,1)}) %all-gather.9.cloned.1.call-update) | async-done | bytes 4816912 | tf_op jit(solution)/shard_map/all_gather | solution.py:101
  436.5 16.3 copy.164
  452.8 51.6 %all_to_all.60 = bf16[2,1568,576]{2,0,1:T(2,128)(2,1)} all-to-all(bf16[2,1568,576]{2,0,1:T(2,128)(2,1)} %copy.164), channel_id=1, replica_groups=mesh['dp'=8,'tensor'=4] {'dp'}, dimensions={1} | all-to-all | bytes 7225344 | tf_op jit(solution)/shard_map/all_to_all | solution.py:116
  504.4 13.3 copy.199
  548.9 23.4 %all_to_all.61 = bf16[16,196,192]{1,2,0:T(8,128)(2,1)S(1)} all-to-all(bf16[16,196,192]{1,2,0:T(8,128)(2,1)S(1)} %bitcast.180), channel_id=1, replica_groups=mesh['dp'=8,'tensor'=4] {'dp'}, dimensions={0} | all-to-all | bytes 2408448 | tf_op jit(solution)/shard_map/all_to_all | solution.py:123
  583.6 160.4 %reduce-scatter.9.cloned.1.call-done = f32[784,768]{1,0:T(8,128)} async-done(((f32[3136,768]{1,0:T(8,128)}), f32[784,768]{1,0:T(8,128)}) %reduce-scatter.9.cloned.1.call-update) | async-done | bytes 2408464 | tf_op jit(solution)/shard_map/reduce_scatter | solution.py:105
  752.4 89.5 %all-gather.11.cloned.1.call-done = bf16[3136,768]{1,0:T(8,128)(2,1)} async-done(((bf16[784,768]{1,0:T(8,128)(2,1)}), bf16[3136,768]{1,0:T(8,128)(2,1)}) %all-gather.11.cloned.1.call-update) | async-done | bytes 4816912 | tf_op jit(solution)/shard_map/all_gather | solution.py:101
  851.4 81.9 %all-gather.13.cloned.1.call-done = bf16[3136,768]{1,0:T(8,128)(2,1)} async-done(((bf16[784,768]{1,0:T(8,128)(2,1)}), bf16[3136,768]{1,0:T(8,128)(2,1)}) %all-gather.13.cloned.1.call-update) | async-done | bytes 4816912 | tf_op jit(solution)/shard_map/all_gather | solution.py:101
  961.2 153.3 %reduce-scatter.13.cloned.1.call-done = f32[784,768]{1,0:T(8,128)} async-done(((f32[3136,768]{1,0:T(8,128)}), f32[784,768]{1,0:T(8,128)}) %reduce-scatter.13.cloned.1.call-update) | async-done | bytes 2408464 | tf_op jit(solution)/shard_map/reduce_scatter | solution.py:105
  1117.9 164.4 %reduce-scatter.11.cloned.1.call-done = f32[784,768]{1,0:T(8,128)} async-done(((f32[3136,768]{1,0:T(8,128)}), f32[784,768]{1,0:T(8,128)}) %reduce-scatter.11.cloned.1.call-update) | async-done | bytes 2408464 | tf_op jit(solution)/shard_map/reduce_scatter | solution.py:105
  1289.3 92.2 %all-gather.15.cloned.1.call-done = bf16[3136,768]{1,0:T(8,128)(2,1)} async-done(((bf16[784,768]{1,0:T(8,128)(2,1)}), bf16[3136,768]{1,0:T(8,128)(2,1)}) %all-gather.15.cloned.1.call-update) | async-done | bytes 4816912 | tf_op jit(solution)/shard_map/all_gather | solution.py:101
  1402.3 21.2 all-to-all-done.2
  1450.7 10.7 copy.180
  1468.8 52.0 %all_to_all.62 = bf16[16,196,576]{2,1,0:T(8,128)(2,1)S(1)} all-to-all(bf16[16,196,576]{2,1,0:T(8,128)(2,1)} %copy.181), channel_id=1, replica_groups=mesh['dp'=8,'tensor'=4] {'dp'}, dimensions={0} | all-to-all | bytes 7225344 | tf_op jit(solution)/shard_map/all_to_all | solution.py:123
  1540.6 161.0 %reduce-scatter.15.cloned.1.call-done = f32[784,768]{1,0:T(8,128)} async-done(((f32[3136,768]{1,0:T(8,128)}), f32[784,768]{1,0:T(8,128)}) %reduce-scatter.15.cloned.1.call-update) | async-done | bytes 2408464 | tf_op jit(solution)/shard_map/reduce_scatter | solution.py:105
  1709.7 92.1 %all-gather.17.cloned.1.call-done = bf16[3136,768]{1,0:T(8,128)(2,1)} async-done(((bf16[784,768]{1,0:T(8,128)(2,1)}), bf16[3136,768]{1,0:T(8,128)(2,1)}) %all-gather.17.cloned.1.call-update) | async-done | bytes 4816912 | tf_op jit(solution)/shard_map/all_gather | solution.py:101
  1830.4 11.1 multiply_convert_fusion
  1931.4 15.3 all-reduce.1
  1946.8 90.2 %reduce-scatter.17.cloned.1.call-done = f32[784,768]{1,0:T(8,128)} async-done(((f32[3136,768]{1,0:T(8,128)}), f32[784,768]{1,0:T(8,128)}) %reduce-scatter.17.cloned.1.call-update) | async-done | bytes 2408464 | tf_op jit(solution)/shard_map/reduce_scatter | solution.py:105
  2052.5 43.8 %all-reduce = (f32[768]{0:T(1024)}, f32[768]{0:T(1024)}, f32[768]{0:T(1024)}, f32[768]{0:T(1024)}, f32[768]{0:T(1024)}, /*index=5*/f32[768]{0:T(1024)}, f32[768]{0:T(1024)}, f32[768]{0:T(1024)}, f32[768]{0:T(1024)}) all-reduce(f32[768]{0:T(1024)S(1)} %get-tuple-element.124, ...), channel_id=1, replica_groups=mesh['dp'=8,'tensor'=4] {'dp','tensor'}, use_global_device_ids=true, to_apply=%region_25.0 | all-reduce | flops 6912 | bytes 55296 | tf_op jit(solution)/shard_map/psum | solution.py:321
  2096.2 86.8 %all-reduce.5.cloned.1.call-done = (f32[768,3,192]{0,2,1:T(8,128)}, f32[192,768]{1,0:T(8,128)}, f32[768,3,192]{0,2,1:T(8,128)}, f32[192,768]{1,0:T(8,128)}, f32[768,768]{1,0:T(8,128)}, /*index=5*/f32[768,768]{1,0:T(8,128)}) async-done(((f32[768,3,192]{0,2,1:T(8,128)}, f32[192,768]{1,0:T(8,128)}, f32[768,3,192]{0,2,1:T(8,128)}, f32[192,768]{1,0:T(8,128)}, f32[768,768]{1,0:T(8,128)}, ...) | async-done | bytes 9437200 | tf_op jit(solution)/shard_map/psum | solution.py:307
  (312 shorter events, 391.5 us)
Async XLA Ops:
  7.2 834.7 %copy-start = (bf16[768,768]{1,0:T(8,128)(2,1)S(1)}, bf16[768,768]{1,0:T(8,128)(2,1)}, u32[]{:S(2)}) copy-start(bf16[768,768]{1,0:T(8,128)(2,1)} %param.35) | copy-start | bytes 3538948
  7.2 105.9 %all-gather.7.cloned.1.call-start = ((), (), s32[]{:S(2)}) async-start(), calls=%async_computation.10 | async-start | bytes 6021120 | tf_op jit(solution)/shard_map/all_gather | solution.py:101
  15.9 97.2 %copy-start.74 = (bf16[768,3,192]{0,2,1:T(8,128)(2,1)S(1)}, bf16[768,3,192]{0,2,1:T(8,128)(2,1)}, u32[]{:S(2)}) copy-start(bf16[768,3,192]{0,2,1:T(8,128)(2,1)} %param.23) | copy-start | bytes 2654212
  19.2 303.2 %reduce-scatter.7.cloned.1.call-start = ((), (), s32[]{:S(2)}) async-start(), calls=%async_computation.11 | async-start | bytes 12042240 | tf_op jit(solution)/shard_map/reduce_scatter | solution.py:105
  159.5 260.8 %all-gather.9.cloned.1.call-start = ((), (), s32[]{:S(2)}) async-start(), calls=%async_computation.12 | async-start | bytes 6021120 | tf_op jit(solution)/shard_map/all_gather | solution.py:101
  328.1 415.9 %reduce-scatter.9.cloned.1.call-start = ((), (), s32[]{:S(2)}) async-start(), calls=%async_computation.13 | async-start | bytes 12042240 | tf_op jit(solution)/shard_map/reduce_scatter | solution.py:105
  583.0 259.0 %all-gather.11.cloned.1.call-start = ((), (), s32[]{:S(2)}) async-start(), calls=%async_computation.14 | async-start | bytes 6021120 | tf_op jit(solution)/shard_map/all_gather | solution.py:101
  749.7 183.6 %all-gather.13.cloned.1.call-start = ((), (), s32[]{:S(2)}) async-start(), calls=%async_computation.16 | async-start | bytes 6021120 | tf_op jit(solution)/shard_map/all_gather | solution.py:101
  752.4 362.2 %reduce-scatter.13.cloned.1.call-start = ((), (), s32[]{:S(2)}) async-start(), calls=%async_computation.17 | async-start | bytes 12042240 | tf_op jit(solution)/shard_map/reduce_scatter | solution.py:105
  752.4 180.9 %copy-start.72 = (bf16[768,768]{1,0:T(8,128)(2,1)S(1)}, bf16[768,768]{1,0:T(8,128)(2,1)}, u32[]{:S(2)}) copy-start(bf16[768,768]{1,0:T(8,128)(2,1)} %param.37) | copy-start | bytes 3538948
  951.7 330.6 %reduce-scatter.11.cloned.1.call-start = ((), (), s32[]{:S(2)}) async-start(), calls=%async_computation.15 | async-start | bytes 12042240 | tf_op jit(solution)/shard_map/reduce_scatter | solution.py:105
  960.6 420.9 %all-gather.15.cloned.1.call-start = ((), (), s32[]{:S(2)}) async-start(), calls=%async_computation.18 | async-start | bytes 6021120 | tf_op jit(solution)/shard_map/all_gather | solution.py:101
  1117.9 169.6 %copy-start.12 = (bf16[784,768]{1,0:T(8,128)(2,1)S(1)}, bf16[784,768]{1,0:T(8,128)(2,1)}, u32[]{:S(2)}) copy-start(bf16[784,768]{1,0:T(8,128)(2,1)} %reshape.282) | copy-start | bytes 3612676
  1287.5 94.0 %copy-start.45 = (bf16[192,768]{1,0:T(8,128)(2,1)S(1)}, bf16[192,768]{1,0:T(8,128)(2,1)}, u32[]{:S(2)}) copy-start(bf16[192,768]{1,0:T(8,128)(2,1)} %param.31) | copy-start | bytes 884740
  1397.8 25.7 %all-to-all-start.2 = ((bf16[2,1568,192]{2,0,1:T(2,128)(2,1)}), bf16[2,1568,192]{2,0,1:T(2,128)(2,1)}, u32[]{:S(2)}, u32[]{:S(2)}) async-start(bf16[2,1568,192]{2,0,1:T(2,128)(2,1)} %copy.174), calls=%async_computation.6 | async-start | bytes 3211264 | tf_op jit(solution)/shard_map/all_to_all | solution.py:116
  1402.1 299.5 %reduce-scatter.15.cloned.1.call-start = ((), (), s32[]{:S(2)}) async-start(), calls=%async_computation.19 | async-start | bytes 12042240 | tf_op jit(solution)/shard_map/reduce_scatter | solution.py:105
  1540.5 164.5 %copy-start.59 = (f32[784]{0:T(1024)S(1)}, f32[784]{0:T(1024)}, u32[]{:S(2)}) copy-start(f32[784]{0:T(1024)} %copy-done.58) | copy-start | bytes 9412
  1540.5 261.3 %all-gather.17.cloned.1.call-start = ((), (), s32[]{:S(2)}) async-start(), calls=%async_computation.20 | async-start | bytes 6021120 | tf_op jit(solution)/shard_map/all_gather | solution.py:101
  1707.8 94.0 %copy-start.47 = (bf16[192,768]{1,0:T(8,128)(2,1)S(1)}, bf16[192,768]{1,0:T(8,128)(2,1)}, u32[]{:S(2)}) copy-start(bf16[192,768]{1,0:T(8,128)(2,1)} %param.25) | copy-start | bytes 884740
  1709.6 327.4 %reduce-scatter.17.cloned.1.call-start = ((), (), s32[]{:S(2)}) async-start(), calls=%async_computation.21 | async-start | bytes 12042240 | tf_op jit(solution)/shard_map/reduce_scatter | solution.py:105
  1874.1 308.9 %all-reduce.5.cloned.1.call-start = ((), (), s32[]{:S(2)}) async-start(), calls=%async_computation.22 | async-start | bytes 18874368 | tf_op jit(solution)/shard_map/psum | solution.py:307
  1928.3 108.7 %copy-start.51 = (f32[784]{0:T(1024)S(1)}, f32[784]{0:T(1024)}, u32[]{:S(2)}) copy-start(f32[784]{0:T(1024)} %copy-done.50) | copy-start | bytes 9412
  1928.3 108.7 %copy-start.53 = (f32[784]{0:T(1024)S(1)}, f32[784]{0:T(1024)}, u32[]{:S(2)}) copy-start(f32[784]{0:T(1024)} %copy-done.52) | copy-start | bytes 9412
  1928.3 108.7 %copy-start.57 = (f32[768]{0:T(1024)S(1)}, f32[768]{0:T(1024)}, u32[]{:S(2)}) copy-start(f32[768]{0:T(1024)} %param.21) | copy-start | bytes 9220
  (70 other events, 444.2 us)
Sparse Core Ops, SparseCore 0:
  19.3 93.7 all-gather.6
  159.7 162.6 reduce-scatter.6
  328.2 92.0 all-gather.8
  583.1 160.8 reduce-scatter.8
  749.8 92.0 all-gather.10
  843.9 89.3 all-gather.12
  951.8 162.6 reduce-scatter.12
  1116.9 165.3 reduce-scatter.10
  1289.4 92.0 all-gather.14
  1540.6 160.8 reduce-scatter.14
  1709.7 92.0 all-gather.16
  1874.3 162.6 reduce-scatter.16
  2043.2 139.7 all-reduce.4
where the time goes:
time: 2210 us; the launch traced here: 2200 us
  waiting for transfers between devices  1540 us (70%)
  local copies, waits for them, and re-layouts  211 us (10%)
  blocking collectives  186 us (8%)
  matrix products  174 us (8%)
  other arithmetic  67.5 us (3%)
    reduce_scatter x6, waiting for transfers between devices, partial_rows(): lax.psum_scatter(make_term(jnp.int32(0), own_rows * lax.axis_size('tensor...  891 us
    all_gather x6, waiting for transfers between devices, full_rows(): return lax.all_gather(shard, 'tensor', axis=0, tiled=True)  541 us
    psum x1, waiting for transfers between devices, per_device(): lax.psum((space_grads[2], space_grads[3], space_grads[4], time_grads[2],...  86.8 us
    all_to_all x2, blocking collectives, to_frames(): lax.all_to_all(grouped, 'dp', split_axis=0, concat_axis=1, tiled=True)  75.4 us
    all_to_all x1, blocking collectives, to_patches(): lax.all_to_all(grouped, 'dp', split_axis=1, concat_axis=0, tiled=True)  51.6 us
    unnamed x174, local copies, waits for them, and re-layouts  47 us
  transfers between devices with their start and end apart: 14, of which 14 were waited for; matrix products, arithmetic and copies ran while one was open for 4% of the time, Pallas kernels for 0%

commit v1 on v0

v1 whole, which is shorter than its diff:
```python
import jax
import jax.numpy as jnp
from jax import lax
from jax.sharding import Mesh, PartitionSpec as P

HS = 64
PATCH = 196
TIMES = 16
EPSILON = 1e-06
ROOT_HALF = 0.7071067811865476
INV_ROOT_TAU = 0.3989422804014327
F32 = jnp.float32
BF16 = jnp.bfloat16
NT = (((1,), (1,)), ((), ()))
NN = (((1,), (0,)), ((), ()))
TN = (((0,), (0,)), ((), ()))


def dot(a, b, dims):
    return lax.dot_general(a, b, dims, preferred_element_type=F32)


def norm_stats(values):
    center = values - jnp.mean(values, axis=-1, keepdims=True)
    second = jnp.mean(center * center, axis=-1, keepdims=True)
    rate = lax.rsqrt(second + EPSILON)
    return center * rate, rate


def norm_back(grad, normed, rate, gain):
    e = grad * gain
    inner = jnp.mean(e * normed, axis=-1, keepdims=True)
    return rate * (e - jnp.mean(e, axis=-1, keepdims=True) - normed * inner)


def gelu_exact(values):
    return 0.5 * values * (1.0 + lax.erf(values * ROOT_HALF))


def gelu_slope(values):
    return (
        0.5 * (1.0 + lax.erf(values * ROOT_HALF))
        + values * jnp.exp(-0.5 * values * values) * INV_ROOT_TAU
    )


def forms(batch_first):
    if batch_first:
        return ("blhe", "bmhe", "bhlm")
    return ("lbhe", "mbhe", "bhlm")


def esum(form, a, b):
    return jnp.einsum(form, a, b, preferred_element_type=F32)


def attend(queries, keys, values, batch_first):
    q, k, s = forms(batch_first)
    scores = esum(q + "," + k + "->" + s, queries, keys) * (HS ** -0.5)
    top = jnp.max(scores, axis=-1, keepdims=True)
    weights = jnp.exp(scores - top)
    total = jnp.sum(weights, axis=-1, keepdims=True)
    probs = (weights / total).astype(BF16)
    return esum(s + "," + k + "->" + q, probs, values), top + jnp.log(total)


def attend_back(queries, keys, values, log_total, mixed_grad, batch_first):
    q, k, s = forms(batch_first)
    scale = HS ** -0.5
    scores = esum(q + "," + k + "->" + s, queries, keys) * scale
    probs = jnp.exp(scores - log_total)
    value_grad = esum(s + "," + q + "->" + k, probs.astype(BF16), mixed_grad)
    prob_grad = esum(q + "," + k + "->" + s, mixed_grad, values)
    inner = jnp.sum(prob_grad * probs, axis=-1, keepdims=True)
    score_grad = (probs * (prob_grad - inner)).astype(BF16)
    query_grad = esum(s + "," + k + "->" + q, score_grad, keys) * scale
    key_grad = esum(s + "," + q + "->" + k, score_grad, queries) * scale
    return query_grad, key_grad, value_grad


def build(mesh):
    dp, tp = mesh.shape["dp"], mesh.shape["tensor"]
    count = dp * tp
    groups = count // TIMES
    if groups <= tp:
        shape = (dp, tp // groups, groups)
        names = dict(time=("a", "b"), tensor=("b", "c"), dp=("a",))
    else:
        shape = (TIMES, groups // tp, tp)
        names = dict(time=("a",), tensor=("c",), dp=("a", "b"))
    inner = Mesh(mesh.devices.reshape(shape), ("a", "b", "c"))
    return inner, names, dp, tp


def make_device(names, dp, tp):
    every = ("a", "b", "c")

    def regroup(x):
        return lax.all_to_all(x, names["time"], split_axis=0, concat_axis=0, tiled=True)

    def gather_all(piece):
        full = lax.all_gather(piece, every, axis=0, tiled=False)
        return full.reshape((dp, tp) + piece.shape)

    def per_device(
        tokens, space_gain, space_shift, space_inproj, space_bias, space_outproj,
        space_outbias, time_gain, time_shift, time_inproj, time_bias, time_outproj,
        time_outbias, feed_gain, feed_shift, up_weight, up_bias, down_weight,
        down_bias, cotangent,
    ):
        width = tokens.shape[-1]
        own = tokens.shape[0] * tokens.shape[1]
        heads_width = space_inproj.shape[2]
        heads = tp * heads_width // HS
        units = up_weight.shape[0]
        d_index = lax.axis_index(names["dp"])
        k_index = lax.axis_index(names["tensor"])
        hp, up = heads_width // dp, units // dp

        def piece_of(rows, per):
            return lax.dynamic_slice_in_dim(rows, d_index * per, per, rows.ndim - 2)

        def attn_piece(inproj, outproj):
            in_piece = piece_of(inproj.transpose(1, 2, 0), hp).reshape(3 * hp, width)
            return jnp.concatenate([in_piece, piece_of(outproj, hp)], axis=0)

        def attn_full(full):
            w_in = full[:, :, : 3 * hp].reshape(dp, tp, 3, hp, width)
            w_in = w_in.transpose(2, 1, 0, 3, 4).reshape(3 * width, width)
            w_out = full[:, :, 3 * hp : 4 * hp].transpose(1, 0, 2, 3).reshape(width, width)
            return w_in, w_out

        bias_piece = jnp.concatenate(
            [
                lax.dynamic_slice_in_dim(up_bias, d_index * up, up, 0),
                lax.dynamic_slice_in_dim(space_bias, d_index * hp, hp, 1).reshape(-1),
                lax.dynamic_slice_in_dim(time_bias, d_index * hp, hp, 1).reshape(-1),
            ]
        )
        bias_row = jnp.zeros((8, width), BF16).at[0, : bias_piece.shape[0]].set(bias_piece)
        full_space = gather_all(
            jnp.concatenate([attn_piece(space_inproj, space_outproj), bias_row], axis=0)
        )
        full_time = gather_all(attn_piece(time_inproj, time_outproj))
        full_feed = gather_all(
            jnp.concatenate([piece_of(up_weight, up), piece_of(down_weight, up)], axis=0)
        )
        space_in_w, space_out_w = attn_full(full_space)
        time_in_w, time_out_w = attn_full(full_time)
        up_w = full_feed[:, :, :up].reshape(dp * tp * up, width)
        down_w = full_feed[:, :, up:].reshape(dp * tp * up, width)
        bias_all = full_space[:, :, 4 * hp].astype(F32)
        up_b = bias_all[:, :, :up].reshape(-1)

        def in_bias(start):
            pair = bias_all[:, :, start : start + 2 * hp].reshape(dp, tp, 2, hp)
            pair = pair.transpose(2, 1, 0, 3).reshape(2, width)
            return jnp.concatenate([pair[0], jnp.zeros((width,), F32), pair[1]])

        space_b, time_b = in_bias(up), in_bias(up + 2 * hp)

        cot = regroup(cotangent.reshape(TIMES, own // TIMES, width)).reshape(own, width)

        resid = tokens.reshape(own, width).astype(F32)
        space_n, space_r = norm_stats(resid)
        space_in = (space_n * space_gain + space_shift).astype(BF16)
        space_qkv = (dot(space_in, space_in_w, NT) + space_b).astype(BF16)
        split = space_qkv.reshape(-1, PATCH, 3, heads, HS)
        mixed, space_log = attend(split[:, :, 0], split[:, :, 1], split[:, :, 2], True)
        space_mix = mixed.astype(BF16).reshape(own, width)
        after_space = resid + dot(space_mix, space_out_w, NN) + space_outbias.astype(F32)
        tn, _ = norm_stats(after_space)
        time_in_own = (tn * time_gain + time_shift).astype(BF16)

        time_in = regroup(time_in_own.reshape(TIMES, own // TIMES, width)).reshape(own, width)
        after_space_p = regroup(after_space.reshape(TIMES, own // TIMES, width)).reshape(own, width)
        time_qkv = (dot(time_in, time_in_w, NT) + time_b).astype(BF16)
        tsplit = time_qkv.reshape(TIMES, -1, 3, heads, HS)
        tmixed, time_log = attend(tsplit[:, :, 0], tsplit[:, :, 1], tsplit[:, :, 2], False)
        time_mix = tmixed.astype(BF16).reshape(own, width)
        after_time = after_space_p + dot(time_mix, time_out_w, NN) + time_outbias.astype(F32)
        feed_n, feed_r = norm_stats(after_time)
        feed_in = (feed_n * feed_gain + feed_shift).astype(BF16)
        pre = dot(feed_in, up_w, NT) + up_b
        hidden = gelu_exact(pre).astype(BF16)
        layer_p = (after_time + dot(hidden, down_w, NN) + down_bias.astype(F32)).astype(BF16)
        layer_out = regroup(layer_p.reshape(TIMES, -1, width)).reshape(tokens.shape)

        upstream = cot.astype(F32)
        down_bias_g = jnp.sum(upstream, axis=0)
        down_g = dot(hidden, cot, TN)
        pre_g = (dot(cot, down_w, NT) * gelu_slope(pre)).astype(BF16)
        up_g = dot(pre_g, feed_in, TN)
        up_bias_g = jnp.sum(pre_g.astype(F32), axis=0)
        feed_g = dot(pre_g, up_w, NN)
        feed_gain_g = jnp.sum(feed_g * feed_n, axis=0)
        feed_shift_g = jnp.sum(feed_g, axis=0)
        after_time_g = upstream + norm_back(feed_g, feed_n, feed_r, feed_gain)

        def scatter(grad):
            return lax.psum_scatter(
                grad.astype(BF16), every, scatter_dimension=0, tiled=False
            )

        feed_pack = jnp.concatenate(
            [up_g.reshape(dp * tp, up, width), down_g.reshape(dp * tp, up, width)], axis=1
        )
        feed_part = scatter(feed_pack)

        def attention_back(upstream, normed_in, qkv, log_total, mix, w_in, w_out, temporal, shape):
            branch = upstream.astype(BF16)
            outbias_g = jnp.sum(branch.astype(F32), axis=0)
            out_g = dot(mix, branch, TN)
            mix_g = dot(branch, w_out, NT).astype(BF16)
            parts = qkv.reshape(shape + (3, heads, HS))
            qg, kg, vg = attend_back(
                parts[:, :, 0], parts[:, :, 1], parts[:, :, 2], log_total,
                mix_g.reshape(shape + (heads, HS)), not temporal,
            )
            qkv_g = jnp.stack([qg, kg, vg], axis=2).astype(BF16).reshape(own, 3 * width)
            sums = jnp.sum(qkv_g.astype(F32), axis=0).reshape(3, width)
            in_g = dot(qkv_g, normed_in, TN)
            normed_g = dot(qkv_g, w_in, NN)
            pack = jnp.concatenate(
                [
                    in_g.reshape(3, tp, dp, hp, width)
                    .transpose(2, 1, 0, 3, 4)
                    .reshape(dp * tp, 3 * hp, width),
                    out_g.reshape(tp, dp, hp, width)
                    .transpose(1, 0, 2, 3)
                    .reshape(dp * tp, hp, width),
                ],
                axis=1,
            )
            return normed_g, pack, outbias_g, sums

        seqs = own // TIMES
        time_in_g, time_pack, time_outbias_g, time_sums = attention_back(
            after_time_g, time_in, time_qkv, time_log, time_mix, time_in_w, time_out_w,
            True, (TIMES, seqs),
        )
        time_part = scatter(time_pack)
        tn_p, tr_p = norm_stats(after_space_p)
        time_gain_g = jnp.sum(time_in_g * tn_p, axis=0)
        time_shift_g = jnp.sum(time_in_g, axis=0)
        after_space_g_p = after_time_g + norm_back(time_in_g, tn_p, tr_p, time_gain)

        high_p = after_space_g_p.astype(BF16)
        low_p = (after_space_g_p - high_p.astype(F32)).astype(BF16)
        high = regroup(high_p.reshape(TIMES, seqs, width)).reshape(own, width)
        low = regroup(low_p.reshape(TIMES, seqs, width)).reshape(own, width)
        after_space_g = high.astype(F32) + low.astype(F32)

        space_in_g, space_pack, space_outbias_g, space_sums = attention_back(
            high, space_in, space_qkv, space_log, space_mix, space_in_w, space_out_w,
            False, (own // PATCH, PATCH),
        )
        space_part = scatter(space_pack)
        space_gain_g = jnp.sum(space_in_g * space_n, axis=0)
        space_shift_g = jnp.sum(space_in_g, axis=0)
        input_g = after_space_g + norm_back(space_in_g, space_n, space_r, space_gain)

        small = jnp.concatenate(
            [
                space_gain_g, space_shift_g, space_outbias_g, time_gain_g, time_shift_g,
                time_outbias_g, feed_gain_g, feed_shift_g, down_bias_g,
                space_sums[0], space_sums[2], time_sums[0], time_sums[2],
                up_bias_g.reshape(dp, tp, up).transpose(1, 0, 2).reshape(-1),
            ]
        )
        small = lax.psum(small, every)
        rows = small[: 13 * width].reshape(13, width)
        head_rows = lax.dynamic_slice_in_dim(rows[9:], k_index * heads_width, heads_width, 1)
        up_bias_out = lax.dynamic_slice_in_dim(small[13 * width :], k_index * units, units, 0)

        def spread(part):
            return lax.all_gather(part, names["dp"], axis=0, tiled=False)

        def attn_out(full):
            in_out = full[:, : 3 * hp].reshape(dp, 3, hp, width).transpose(1, 0, 2, 3)
            in_out = in_out.reshape(3, heads_width, width).transpose(2, 0, 1).astype(F32)
            return in_out, full[:, 3 * hp :].reshape(heads_width, width).astype(F32)

        feed_all = spread(feed_part)
        time_in_out, time_out_out = attn_out(spread(time_part))
        space_in_out, space_out_out = attn_out(spread(space_part))
        return (
            layer_out,
            input_g.reshape(tokens.shape),
            rows[0], rows[1], space_in_out, head_rows[0:2], space_out_out, rows[2],
            rows[3], rows[4], time_in_out, head_rows[2:4], time_out_out, rows[5],
            rows[6], rows[7],
            feed_all[:, :up].reshape(units, width).astype(F32),
            up_bias_out,
            feed_all[:, up:].reshape(units, width).astype(F32),
            rows[8],
        )

    return per_device


def solution(mesh):
    inner, names, dp, tp = build(mesh)
    every, tensor = ("a", "b", "c"), names["tensor"]
    frames = P(every, None, None)
    head_in = P(None, None, tensor)
    head_bias = P(None, tensor)
    row = P(tensor, None)
    return jax.shard_map(
        make_device(names, dp, tp),
        mesh=inner,
        in_specs=(
            frames, P(), P(), head_in, head_bias, row, P(),
            P(), P(), head_in, head_bias, row, P(),
            P(), P(), row, P(tensor), row, P(), frames,
        ),
        out_specs=(
            frames, frames, P(), P(), head_in, head_bias, row, P(),
            P(), P(), head_in, head_bias, row, P(),
            P(), P(), row, P(tensor), row, P(),
        ),
        check_vma=False,
    )
```

time: 2210 us -> 904 us (0.41)
  waiting for transfers between devices: 1540 us -> 384 us
  blocking collectives: 186 us -> 40.2 us
  matrix products: 174 us -> 147 us
  starting transfers between devices: 5.79 us -> 30.2 us
    reduce_scatter x6 -> x3, waiting for transfers between devices: 891 us -> 208 us  [scatter(): lax.psum_scatter(grad.astype(BF16), every, scatter_dimension=0, tiled=False)]
    all_gather x6, waiting for transfers between devices: 541 us -> 83.1 us  [the longest x3 62.6 us: gather_all(): full = lax.all_gather(piece, every, axis=0, tiled=False)]
    all_to_all x3 -> x0, blocking collectives: 127 us -> none  [the longest x2 75.4 us: to_frames(): lax.all_to_all(grouped, 'dp', split_axis=0, concat_axis=1, tiled=True)]
    psum x1 -> x0, waiting for transfers between devices: 86.8 us -> none  [per_device(): lax.psum((space_grads[2], space_grads[3], space_grads[4], time_grads[2],...]
    all_to_all x1 -> x6, waiting for transfers between devices: 21.2 us -> 93.4 us  [regroup(): lax.all_to_all(x, names['time'], split_axis=0, concat_axis=0, tiled=True)]
    convert_element_type x7 -> x15, local copies, waits for them, and re-layouts: 32.7 us -> 62.9 us  [the longest x4 38.2 us: attention_back(): qkv_g = jnp.stack([qg, kg, vg], axis=2).astype(BF16).reshape(own, 3 * width)]
    dot_general x30, matrix products: 174 us -> 147 us  [the longest x18 105 us: dot(): return lax.dot_general(a, b, dims, preferred_element_type=F32)]
    all_to_all x1 -> x6, starting transfers between devices: 4.28 us -> 29.7 us  [regroup(): lax.all_to_all(x, names['time'], split_axis=0, concat_axis=0, tiled=True)]
  transfers between devices with their start and end apart: 14 -> 15, of which waited for: 14 -> 7; matrix products, arithmetic and copies ran while one was open for 4% -> 35% of each run, Pallas kernels for 0% -> 0%
where the time goes in v1:
time: 904 us; the launch traced here: 894 us
  waiting for transfers between devices  384 us (42%)
  local copies, waits for them, and re-layouts  218 us (24%)
  matrix products  147 us (16%)
  other arithmetic  58 us (6%)
  blocking collectives  40.2 us (4%)
  starting transfers between devices  30.2 us (3%)
  between operations  15.5 us (2%)
    reduce_scatter x3, waiting for transfers between devices, scatter(): lax.psum_scatter(grad.astype(BF16), every, scatter_dimension=0, tiled=False)  208 us
    dot_general x18, matrix products, dot(): return lax.dot_general(a, b, dims, preferred_element_type=F32)  105 us
    all_to_all x6, waiting for transfers between devices, regroup(): lax.all_to_all(x, names['time'], split_axis=0, concat_axis=0, tiled=True)  93.4 us
    all_gather x3, waiting for transfers between devices, gather_all(): full = lax.all_gather(piece, every, axis=0, tiled=False)  62.6 us
    dot_general x12, matrix products, esum(): return jnp.einsum(form, a, b, preferred_element_type=F32)  42 us
    psum x1, blocking collectives, per_device(): small = lax.psum(small, every)  40.2 us
    convert_element_type x4, local copies, waits for them, and re-layouts, attention_back(): qkv_g = jnp.stack([qg, kg, vg], axis=2).astype(BF16).reshape(own, 3 * width)  38.2 us
    unnamed x154, local copies, waits for them, and re-layouts  30.1 us
  transfers between devices with their start and end apart: 15, of which 7 were waited for; matrix products, arithmetic and copies ran while one was open for 35% of the time, Pallas kernels for 0%

profile of v1, /device:TPU:0, one launch (start us, length us, event | category | flops | bytes accessed | tf_op | source)
XLA Modules:
  0.0 893.7 jit_solution(4292682229700434396)
XLA Ops:
  16.4 7.3 all-to-all-start.3
  32.6 62.6 %all-gather.16.cloned.1.call-done = bf16[3328,768]{1,0:T(8,128)(2,1)} async-done(((bf16[104,768]{1,0:T(8,128)(2,1)}), bf16[3328,768]{1,0:T(8,128)(2,1)}) %all-gather.16.cloned.1.call-update) | async-done | bytes 5111824 | tf_op jit(solution)/shard_map/all_gather | solution.py:102
  110.7 11.9 %reshape.576 = bf16[4,196,3,12,64]{4,3,2,1,0:T(8,128)(2,1)} reshape(bf16[784,2304]{1,0:T(8,128)(2,1)} %add_convert_fusion.1) | data formatting | bytes 7225344 | tf_op jit(solution)/shard_map/reshape | solution.py:168
  174.8 44.2 %all-to-all-done.1 = bf16[16,49,768]{2,1,0:T(8,128)(2,1)} async-done(((bf16[16,49,768]{2,1,0:T(8,128)(2,1)}), bf16[16,49,768]{2,1,0:T(8,128)(2,1)}, u32[]{:S(2)}, u32[]{:S(2)}) %all-to-all-start.1) | async-done | bytes 1204256 | tf_op jit(solution)/shard_map/all_to_all | solution.py:99
  240.6 11.8 %reshape.527 = bf16[16,49,3,12,64]{4,3,2,1,0:T(8,128)(2,1)} reshape(bf16[784,2304]{1,0:T(8,128)(2,1)} %add_convert_fusion) | data formatting | bytes 7225344 | tf_op jit(solution)/shard_map/reshape | solution.py:178
  275.5 36.8 %all-to-all-done = f32[16,49,768]{2,1,0:T(8,128)} async-done(((f32[16,49,768]{2,1,0:T(8,128)}), f32[16,49,768]{2,1,0:T(8,128)}, u32[]{:S(2)}, u32[]{:S(2)}) %all-to-all-start) | async-done | bytes 2408480 | tf_op jit(solution)/shard_map/all_to_all | solution.py:99
  323.9 7.2 fusion.61
  331.2 10.3 %multiply_convert_fusion.1 = (bf16[784,3072]{1,0:T(8,128)(2,1)}, f32[784,3072]{1,0:T(8,128)S(1)}) fusion(f32[3072]{0:T(1024)S(1)} %add.216, bf16[3072,768]{1,0:T(8,128)(2,1)} %bitcast.235, f32[784,768]{1,0:T(8,128)S(1)} %get-tuple-element.194, f32[768]{0:T(1024)S(1)} %copy-done.60, f32[768]{0:T(1024)S(1)} %copy-done.54, f32[784]{0:T(1024)S(1)} %add_rsqrt_fusion.2, ...), kind=kOutput, calls=%fused_computation.15 | convolution fusion | flops 3716837376 | bytes 21602432 | tf_op jit(solution)/shard_map/dot_general | solution.py:20
  341.5 8.0 convert_reduce_fusion.1
  380.5 8.9 copy.218
  389.4 12.9 %convert_element_type.255 = bf16[784,2304]{1,0:T(8,128)(2,1)} reshape(bf16[16,49,3,12,64]{4,3,2,1,0:T(8,128)(2,1)} %copy.218) | data formatting | bytes 7225344 | tf_op jit(solution)/shard_map/convert_element_type | solution.py:220
  439.3 12.4 %all-to-all-done.4 = bf16[16,49,768]{2,1,0:T(8,128)(2,1)S(1)} async-done(((bf16[16,49,768]{2,1,0:T(8,128)(2,1)}), bf16[16,49,768]{2,1,0:T(8,128)(2,1)S(1)}, u32[]{:S(2)}, u32[]{:S(2)}) %all-to-all-start.4) | async-done | bytes 1204256 | tf_op jit(solution)/shard_map/all_to_all | solution.py:99
  466.5 9.2 %multiply_reduce_fusion = (f32[4,12,196]{2,1,0:T(8,128)S(1)}, f32[4,12,196,196]{2,3,1,0:T(8,128)}) fusion(f32[4,12,196,196]{2,3,1,0:T(8,128)} %copy-done.2, f32[4,12,196]{2,1,0:T(8,128)S(1)} %log_add_fusion.1, bf16[4,196,12,64]{1,3,2,0:T(8,128)(2,1)S(1)} %copy.220, bf16[4,196,1,12,64]{1,4,3,0,2:T(8,128)(2,1)} %copy.253), kind=kOutput, calls=%fused_computation.4 | convolution fusion | flops 243394368 | bytes 17235456 | tf_op jit(solution)/shard_map/blhe,bmhe->bhlm/dot_general | solution.py:54
  475.7 11.7 %multiply_convert_fusion = bf16[4,12,196,196]{2,3,1,0:T(8,128)(2,1)} fusion(f32[4,12,196,196]{2,3,1,0:T(8,128)} %get-tuple-element.202, f32[4,12,196,196]{2,3,1,0:T(8,128)} %copy-done.2, f32[4,12,196]{2,1,0:T(8,128)S(1)} %get-tuple-element.201, f32[4,12,196]{2,1,0:T(8,128)S(1)} %log_add_fusion.1), kind=kLoop, calls=%fused_computation.3 | loop fusion | flops 9219840 | bytes 18514944 | tf_op jit(solution)/shard_map/convert_element_type | solution.py:75
  506.7 9.8 %convert_element_type.266 = bf16[784,2304]{0,1:T(8,128)(2,1)} reshape(bf16[4,196,3,12,64]{1,0,4,3,2:T(4,128)(2,1)} %copy.225) | data formatting | bytes 7225344 | tf_op jit(solution)/shard_map/convert_element_type | solution.py:220
  528.8 7.5 copy.235
  536.2 8.2 convolution_convert_fusion.1
  544.4 8.8 convolution_convert_fusion
  557.8 8.7 add_convert_fusion.2
  572.4 86.6 %reduce-scatter.4.cloned.1.call-done = bf16[1,96,768]{2,1,0:T(8,128)(2,1)} async-done(((bf16[32,96,768]{2,1,0:T(8,128)(2,1)}), bf16[1,96,768]{2,1,0:T(8,128)(2,1)}) %reduce-scatter.4.cloned.1.call-update) | async-done | bytes 147472 | tf_op jit(solution)/shard_map/reduce_scatter | solution.py:201
  667.4 8.4 multiply_reduce_fusion.7
  679.1 121.1 %reduce-scatter.8.cloned.1.call-done = bf16[1,192,768]{2,1,0:T(8,128)(2,1)} async-done(((bf16[32,192,768]{2,1,0:T(8,128)(2,1)}), bf16[1,192,768]{2,1,0:T(8,128)(2,1)}) %reduce-scatter.8.cloned.1.call-update) | async-done | bytes 294928 | tf_op jit(solution)/shard_map/reduce_scatter | solution.py:201
  800.7 40.2 %psum.7 = f32[13056]{0:T(1024)S(1)} all-reduce(f32[13056]{0:T(1024)S(1)} %constant_dynamic-update-slice_fusion), channel_id=1, replica_groups=mesh['a'=8,'b'=2,'c'=2] {'a','b','c'}, use_global_device_ids=true, to_apply=%region_32.0 | all-reduce | flops 13056 | bytes 104448 | tf_op jit(solution)/shard_map/psum | solution.py:271
  861.4 20.5 %all-gather.14.cloned.1.call-done = bf16[8,192,768]{2,1,0:T(8,128)(2,1)} async-done(((bf16[1,192,768]{2,1,0:T(8,128)(2,1)}), bf16[8,192,768]{2,1,0:T(8,128)(2,1)}) %all-gather.14.cloned.1.call-update) | async-done | bytes 2359312 | tf_op jit(solution)/shard_map/all_gather | solution.py:277
  (360 shorter events, 303.4 us)
Async XLA Ops:
  7.2 88.0 %all-gather.16.cloned.1.call-start = ((), (), s32[]{:S(2)}) async-start(), calls=%async_computation.15 | async-start | bytes 5271552 | tf_op jit(solution)/shard_map/all_gather | solution.py:102
  10.7 214.5 %all-gather.18.cloned.1.call-start = ((), (), s32[]{:S(2)}) async-start(), calls=%async_computation.16 | async-start | bytes 4866048 | tf_op jit(solution)/shard_map/all_gather | solution.py:102
  13.1 310.8 %all-gather.20.cloned.1.call-start = ((), (), s32[]{:S(2)}) async-start(), calls=%async_computation.17 | async-start | bytes 9732096 | tf_op jit(solution)/shard_map/all_gather | solution.py:102
  16.4 150.9 %all-to-all-start.3 = ((bf16[16,49,768]{2,1,0:T(8,128)(2,1)}), bf16[16,49,768]{2,1,0:T(8,128)(2,1)S(1)}, u32[]{:S(2)}, u32[]{:S(2)}) async-start(bf16[16,49,768]{2,1,0:T(8,128)(2,1)} %reshape.535), calls=%async_computation.3 | async-start | bytes 2752512 | tf_op jit(solution)/shard_map/all_to_all | solution.py:99
  105.8 54.8 %copy-start.39 = (bf16[4,8,24,768]{3,2,1,0:T(8,128)(2,1)}, bf16[4,8,24,768]{3,2,1,0:T(8,128)(2,1)S(1)}, u32[]{:S(2)}) copy-start(bf16[4,8,24,768]{3,2,1,0:T(8,128)(2,1)S(1)} %copy.205) | copy-start | bytes 3538948
  167.3 56.6 %copy-start.5 = (bf16[16,49,768]{2,1,0:T(8,128)(2,1)}, bf16[16,49,768]{2,1,0:T(8,128)(2,1)S(1)}, u32[]{:S(2)}) copy-start(bf16[16,49,768]{2,1,0:T(8,128)(2,1)S(1)} %all-to-all-done.3) | copy-start | bytes 3612676
  167.3 51.7 %all-to-all-start.1 = ((bf16[16,49,768]{2,1,0:T(8,128)(2,1)}), bf16[16,49,768]{2,1,0:T(8,128)(2,1)}, u32[]{:S(2)}, u32[]{:S(2)}) async-start(bf16[16,49,768]{2,1,0:T(8,128)(2,1)} %reshape.520), calls=%async_computation.1 | async-start | bytes 2752512 | tf_op jit(solution)/shard_map/all_to_all | solution.py:99
  219.0 93.2 %all-to-all-start = ((f32[16,49,768]{2,1,0:T(8,128)}), f32[16,49,768]{2,1,0:T(8,128)}, u32[]{:S(2)}, u32[]{:S(2)}) async-start(f32[16,49,768]{2,1,0:T(8,128)} %reshape.518), calls=%async_computation | async-start | bytes 5505024 | tf_op jit(solution)/shard_map/all_to_all | solution.py:99
  413.5 38.2 %all-to-all-start.4 = ((bf16[16,49,768]{2,1,0:T(8,128)(2,1)}), bf16[16,49,768]{2,1,0:T(8,128)(2,1)S(1)}, u32[]{:S(2)}, u32[]{:S(2)}) async-start(bf16[16,49,768]{2,1,0:T(8,128)(2,1)} %reshape.538), calls=%async_computation.4 | async-start | bytes 2752512 | tf_op jit(solution)/shard_map/all_to_all | solution.py:99
  417.4 140.3 %reduce-scatter.6.cloned.1.call-start = ((), (), s32[]{:S(2)}) async-start(), calls=%async_computation.11 | async-start | bytes 4866048 | tf_op jit(solution)/shard_map/reduce_scatter | solution.py:201
  436.8 222.2 %reduce-scatter.4.cloned.1.call-start = ((), (), s32[]{:S(2)}) async-start(), calls=%async_computation.9 | async-start | bytes 4866048 | tf_op jit(solution)/shard_map/reduce_scatter | solution.py:201
  527.0 273.2 %reduce-scatter.8.cloned.1.call-start = ((), (), s32[]{:S(2)}) async-start(), calls=%async_computation.13 | async-start | bytes 9732096 | tf_op jit(solution)/shard_map/reduce_scatter | solution.py:201
  557.1 297.1 %all-gather.12.cloned.1.call-start = ((), (), s32[]{:S(2)}) async-start(), calls=%async_computation.12 | async-start | bytes 1327104 | tf_op jit(solution)/shard_map/all_gather | solution.py:277
  566.5 92.6 %copy-start.35 = (f32[4,196]{0,1:T(8,128)S(1)}, f32[4,196]{0,1:T(8,128)}, u32[]{:S(2)}) copy-start(f32[4,196]{0,1:T(8,128)} %copy-done.34) | copy-start | bytes 9412
  566.5 92.6 %copy-start.42 = (f32[4,196]{0,1:T(8,128)S(1)}, f32[4,196]{0,1:T(8,128)}, u32[]{:S(2)}) copy-start(f32[4,196]{0,1:T(8,128)} %copy-done.41) | copy-start | bytes 9412
  567.8 91.9 %copy-start.51 = (f32[3072]{0:T(1024)S(1)}, f32[3072]{0:T(1024)}, u32[]{:S(2)}) copy-start(f32[3072]{0:T(1024)} %get-tuple-element.204) | copy-start | bytes 36868
  567.8 94.7 %all-to-all-start.2 = ((bf16[16,49,768]{2,1,0:T(8,128)(2,1)}), bf16[16,49,768]{2,1,0:T(8,128)(2,1)}, u32[]{:S(2)}, u32[]{:S(2)}) async-start(bf16[16,49,768]{2,1,0:T(8,128)(2,1)} %reshape.533), calls=%async_computation.2 | async-start | bytes 2752512 | tf_op jit(solution)/shard_map/all_to_all | solution.py:99
  572.3 285.4 %all-gather.10.cloned.1.call-start = ((), (), s32[]{:S(2)}) async-start(), calls=%async_computation.10 | async-start | bytes 1327104 | tf_op jit(solution)/shard_map/all_gather | solution.py:277
  662.5 178.5 %all-to-all-start.5 = ((bf16[16,49,768]{2,1,0:T(8,128)(2,1)}), bf16[16,49,768]{2,1,0:T(8,128)(2,1)}, u32[]{:S(2)}, u32[]{:S(2)}) async-start(bf16[16,49,768]{2,1,0:T(8,128)(2,1)} %reshape.540), calls=%async_computation.5 | async-start | bytes 2752512 | tf_op jit(solution)/shard_map/all_to_all | solution.py:99
  667.1 214.8 %all-gather.14.cloned.1.call-start = ((), (), s32[]{:S(2)}) async-start(), calls=%async_computation.14 | async-start | bytes 2654208 | tf_op jit(solution)/shard_map/all_gather | solution.py:277
  675.8 124.5 %copy-start.8 = (bf16[16,49,768]{2,1,0:T(8,128)(2,1)S(1)}, bf16[16,49,768]{2,1,0:T(8,128)(2,1)}, u32[]{:S(2)}) copy-start(bf16[16,49,768]{2,1,0:T(8,128)(2,1)} %copy-done.7) | copy-start | bytes 3612676
  677.4 123.1 %copy-start.50 = (f32[768]{0:T(1024)S(1)}, f32[768]{0:T(1024)}, u32[]{:S(2)}) copy-start(f32[768]{0:T(1024)} %get-tuple-element.148) | copy-start | bytes 9220
  677.5 123.1 %copy-start.56 = (f32[768]{0:T(1024)S(1)}, f32[768]{0:T(1024)}, u32[]{:S(2)}) copy-start(f32[768]{0:T(1024)} %get-tuple-element.132) | copy-start | bytes 9220
  677.5 123.1 %copy-start.55 = (f32[768]{0:T(1024)S(1)}, f32[768]{0:T(1024)}, u32[]{:S(2)}) copy-start(f32[768]{0:T(1024)} %get-tuple-element.141) | copy-start | bytes 9220
  (59 other events, 385.4 us)
Sparse Core Ops, SparseCore 0:
  11.4 83.7 all-gather.15
  98.0 62.0 all-gather.17
  163.5 134.0 all-gather.19
  436.9 107.8 reduce-scatter.5
  550.1 108.8 reduce-scatter.3
  664.8 135.4 reduce-scatter.7
  802.1 22.9 all-gather.11
  826.9 24.0 all-gather.9
  853.0 28.8 all-gather.13

commit v2 on v1

v2 whole, which is shorter than its diff:
```python
import functools

import jax
import jax.numpy as jnp
from jax import lax
from jax.experimental import pallas as pl
from jax.experimental.pallas import tpu as pltpu
from jax.sharding import Mesh, PartitionSpec as P

HS = 64
PATCH = 196
TIMES = 16
SLOT = 56
EPSILON = 1e-06
ROOT_HALF = 0.7071067811865476
INV_ROOT_TAU = 0.3989422804014327
F32 = jnp.float32
BF16 = jnp.bfloat16
NT = (((1,), (1,)), ((), ()))
NN = (((1,), (0,)), ((), ()))
TN = (((0,), (0,)), ((), ()))


def dot(a, b, dims):
    return lax.dot_general(a, b, dims, preferred_element_type=F32)


def norm_stats(values):
    center = values - jnp.mean(values, axis=-1, keepdims=True)
    second = jnp.mean(center * center, axis=-1, keepdims=True)
    rate = lax.rsqrt(second + EPSILON)
    return center * rate, rate


def norm_back(grad, normed, rate, gain):
    e = grad * gain
    inner = jnp.mean(e * normed, axis=-1, keepdims=True)
    return rate * (e - jnp.mean(e, axis=-1, keepdims=True) - normed * inner)


def gelu_exact(values):
    return 0.5 * values * (1.0 + lax.erf(values * ROOT_HALF))


def gelu_slope(values):
    return (
        0.5 * (1.0 + lax.erf(values * ROOT_HALF))
        + values * jnp.exp(-0.5 * values * values) * INV_ROOT_TAU
    )


def same_sequence(rows, temporal):
    r = lax.broadcasted_iota(jnp.int32, (rows, rows), 0)
    c = lax.broadcasted_iota(jnp.int32, (rows, rows), 1)
    if temporal:
        return (r % 8) == (c % 8)
    return (c % SLOT) < (PATCH // 4)


def head_lanes(rows, second):
    lane = lax.broadcasted_iota(jnp.int32, (rows, 2 * HS), 1)
    return (lane >= HS) if second else (lane < HS)


def softmax_of(q_one, k_pair, allowed):
    scores = dot(q_one, k_pair, NT) * (HS ** -0.5)
    scores = jnp.where(allowed, scores, -1e30)
    top = jnp.max(scores, axis=-1, keepdims=True)
    weights = jnp.exp(scores - top)
    return weights / jnp.sum(weights, axis=-1, keepdims=True)


def rows_of(ref, start, temporal):
    if temporal:
        block = ref[:, :, start : start + 2 * HS].astype(F32)
        return block.reshape(-1, 2 * HS).astype(BF16)
    return ref[:, start : start + 2 * HS]


def put_rows(ref, start, value, temporal):
    if temporal:
        ref[:, :, start : start + 2 * HS] = value.reshape(TIMES, 8, 2 * HS).astype(BF16)
    else:
        ref[:, start : start + 2 * HS] = value.astype(BF16)


def attend_kernel(qkv_ref, mix_ref, *, temporal):
    width = mix_ref.shape[-1]
    rows = TIMES * 8 if temporal else mix_ref.shape[0]
    allowed = same_sequence(rows, temporal)
    for pair in range(width // (2 * HS)):
        at = pair * 2 * HS
        q = rows_of(qkv_ref, at, temporal)
        k = rows_of(qkv_ref, width + at, temporal)
        v = rows_of(qkv_ref, 2 * width + at, temporal)
        mixed = None
        for second in (False, True):
            lanes = head_lanes(rows, second)
            probs = softmax_of(jnp.where(lanes, q, 0), k, allowed).astype(BF16)
            part = dot(probs, jnp.where(lanes, v, 0), NN)
            mixed = part if mixed is None else mixed + part
        put_rows(mix_ref, at, mixed, temporal)


def attend_back_kernel(qkv_ref, mix_g_ref, qkv_g_ref, *, temporal):
    width = mix_g_ref.shape[-1]
    rows = TIMES * 8 if temporal else mix_g_ref.shape[0]
    allowed = same_sequence(rows, temporal)
    scale = HS ** -0.5
    for pair in range(width // (2 * HS)):
        at = pair * 2 * HS
        q = rows_of(qkv_ref, at, temporal)
        k = rows_of(qkv_ref, width + at, temporal)
        v = rows_of(qkv_ref, 2 * width + at, temporal)
        g = rows_of(mix_g_ref, at, temporal)
        total = [None, None, None]
        for second in (False, True):
            lanes = head_lanes(rows, second)
            q_one, g_one = jnp.where(lanes, q, 0), jnp.where(lanes, g, 0)
            probs = softmax_of(q_one, k, allowed)
            prob_g = dot(g_one, v, NT)
            inner = jnp.sum(prob_g * probs, axis=-1, keepdims=True)
            score_g = (probs * (prob_g - inner)).astype(BF16)
            parts = (
                dot(score_g, jnp.where(lanes, k, 0), NN),
                dot(score_g, q_one, TN),
                dot(probs.astype(BF16), g_one, TN),
            )
            total = [p if t is None else t + p for t, p in zip(total, parts)]
        put_rows(qkv_g_ref, at, total[0] * scale, temporal)
        put_rows(qkv_g_ref, width + at, total[1] * scale, temporal)
        put_rows(qkv_g_ref, 2 * width + at, total[2], temporal)


def attention_call(kernel, operands, out_width, temporal):
    total = operands[0].shape[0]
    if temporal:
        seqs = total // TIMES
        grid = (seqs // 8,)

        def spec(cols):
            return pl.BlockSpec((TIMES, 8, cols), lambda i: (0, i, 0))

        operands = [x.reshape(TIMES, seqs, x.shape[-1]) for x in operands]
        out_shape = (TIMES, seqs, out_width)
    else:
        rows = 4 * SLOT
        grid = (total // rows,)

        def spec(cols):
            return pl.BlockSpec((rows, cols), lambda i: (i, 0))

        out_shape = (total, out_width)
    rows = 128 if temporal else 4 * SLOT
    dots = 2 if len(operands) == 1 else 5
    out = pl.pallas_call(
        functools.partial(kernel, temporal=temporal),
        grid=grid,
        in_specs=[spec(x.shape[-1]) for x in operands],
        out_specs=spec(out_width),
        out_shape=jax.ShapeDtypeStruct(out_shape, BF16),
        cost_estimate=pl.CostEstimate(
            flops=dots * grid[0] * 12 * rows * rows * 256,
            bytes_accessed=2 * total * (out_width + sum(x.shape[-1] for x in operands)),
            transcendentals=grid[0] * 12 * rows * rows,
        ),
    )(*operands)
    return out.reshape(total, out_width)


class Copies:
    def __init__(self, send_sems, recv_sems):
        self.send_sems, self.recv_sems, self.made = send_sems, recv_sems, []

    def start(self, source, target, device):
        at = len(self.made)
        copy = pltpu.make_async_remote_copy(
            src_ref=source, dst_ref=target, send_sem=self.send_sems.at[at],
            recv_sem=self.recv_sems.at[at], device_id=device,
            device_id_type=pl.DeviceIdType.MESH,
        )
        copy.start()
        self.made.append(copy)
        return copy


def here():
    a = lax.axis_index("a")
    z = 2 * lax.axis_index("b") + lax.axis_index("c")
    core, x, y = a % 2, (a // 2) % 2, a // 4
    flips = {1: 1 - 2 * core, 2: 2 - 4 * x, 4: 4 - 8 * y, 0: 0}

    def part(mask):
        return a + flips[mask & 1] + flips[mask & 2] + flips[mask & 4]

    return a, z, part


def plane(part, mask):
    return {"a": part(mask)}


def column(z):
    return {"b": z // 2, "c": z % 2}


def greet(part, z):
    barrier = pltpu.get_barrier_semaphore()
    for device in [plane(part, m) for m in (1, 2, 4)] + [column((z + j) % 4) for j in (1, 2, 3)]:
        pl.semaphore_signal(barrier, inc=1, device_id=device, device_id_type=pl.DeviceIdType.MESH)
    pl.semaphore_wait(barrier, 6)


def gather_kernel(*refs, count):
    shards, fulls = refs[:count], refs[count : 2 * count]
    staging = refs[2 * count : 3 * count]
    send_sems, recv_sems, local_sems = refs[3 * count :]
    me, z, part = here()
    loads = [
        pltpu.make_async_copy(shards[w], staging[w], local_sems.at[w]) for w in range(count)
    ]
    for load in loads:
        load.start()
    greet(part, z)
    copies = Copies(send_sems, recv_sems)
    items = []
    for w in range(count):
        for j in (1, 2, 3):
            sent = copies.start(
                shards[w].at[:, me], fulls[w].at[:, z, me], column((z + j) % 4)
            )
            items.append((w, (z + 4 - j) % 4, sent))
    stores = []
    for w in range(count):
        loads[w].wait()
        store = pltpu.make_async_copy(staging[w], fulls[w].at[:, z], local_sems.at[count + w])
        store.start()
        stores.append(store)
    total, lag = len(items), 3
    from_x, from_y, from_far, from_core = {}, {}, {}, []

    def push(w, zz, mask, to):
        at = part(mask)
        return copies.start(fulls[w].at[:, zz, at], fulls[w].at[:, zz, at], plane(part, to))

    for step in range(total + 2 * lag):
        if step < total:
            w, zz, sent = items[step]
            sent.wait_recv()
            from_x[step] = push(w, zz, 0, 2)
            from_y[step] = push(w, zz, 0, 4)
            from_core.append(push(w, zz, 0, 1))
        late = step - lag
        if 0 <= late < total:
            w, zz, _ = items[late]
            from_x[late].wait_recv()
            if late % 2 == 0:
                from_far[late] = push(w, zz, 2, 4)
            from_core.append(push(w, zz, 2, 1))
            from_y[late].wait_recv()
            if late % 2 == 1:
                from_far[late] = push(w, zz, 4, 2)
            from_core.append(push(w, zz, 4, 1))
        last = step - 2 * lag
        if 0 <= last < total:
            w, zz, _ = items[last]
            from_far[last].wait_recv()
            from_core.append(push(w, zz, 6, 1))
    for copy in from_core:
        copy.wait_recv()
    for copy in copies.made:
        copy.wait_send()
    for store in stores:
        store.wait()


def gather_weights(shards, dp, tp):
    count = len(shards)
    views = [x.reshape(x.shape[0], dp, x.shape[1] // dp, x.shape[2]) for x in shards]
    anywhere = pl.BlockSpec(memory_space=pl.ANY)
    sent = sum(x.size for x in shards) * 2
    fulls = pl.pallas_call(
        functools.partial(gather_kernel, count=count),
        out_shape=[
            jax.ShapeDtypeStruct((v.shape[0], tp) + v.shape[1:], v.dtype) for v in views
        ],
        in_specs=[anywhere] * count,
        out_specs=[anywhere] * count,
        scratch_shapes=[pltpu.VMEM(v.shape, v.dtype) for v in views]
        + [
            pltpu.SemaphoreType.DMA((count * 27,)),
            pltpu.SemaphoreType.DMA((count * 27,)),
            pltpu.SemaphoreType.DMA((2 * count,)),
        ],
        compiler_params=pltpu.CompilerParams(collective_id=0, has_side_effects=True),
        cost_estimate=pl.CostEstimate(flops=0, bytes_accessed=40 * sent, transcendentals=0),
        name="gather_weights",
    )(*views)
    return [f.reshape(f.shape[0], -1, f.shape[-1]) for f in fulls]


def build(mesh):
    dp, tp = mesh.shape["dp"], mesh.shape["tensor"]
    count = dp * tp
    groups = count // TIMES
    if groups <= tp:
        shape = (dp, tp // groups, groups)
        names = dict(time=("a", "b"), tensor=("b", "c"), dp=("a",))
    else:
        shape = (TIMES, groups // tp, tp)
        names = dict(time=("a",), tensor=("c",), dp=("a", "b"))
    inner = Mesh(mesh.devices.reshape(shape), ("a", "b", "c"))
    return inner, names, dp, tp


def make_device(names, dp, tp):
    every = ("a", "b", "c")

    def regroup(x):
        return lax.all_to_all(x, names["time"], split_axis=0, concat_axis=0, tiled=True)

    def gather_all(piece):
        full = lax.all_gather(piece, every, axis=0, tiled=False)
        return full.reshape((dp, tp) + piece.shape)

    def per_device(
        tokens, space_gain, space_shift, space_inproj, space_bias, space_outproj,
        space_outbias, time_gain, time_shift, time_inproj, time_bias, time_outproj,
        time_outbias, feed_gain, feed_shift, up_weight, up_bias, down_weight,
        down_bias, cotangent,
    ):
        width = tokens.shape[-1]
        own = tokens.shape[0] * tokens.shape[1]
        heads_width = space_inproj.shape[2]
        units = up_weight.shape[0]
        d_index = lax.axis_index(names["dp"])
        k_index = lax.axis_index(names["tensor"])
        hp, up = heads_width // dp, units // dp

        def piece_of(rows, per):
            return lax.dynamic_slice_in_dim(rows, d_index * per, per, rows.ndim - 2)

        def attn_piece(inproj, outproj):
            in_piece = piece_of(inproj.transpose(1, 2, 0), hp).reshape(3 * hp, width)
            return jnp.concatenate([in_piece, piece_of(outproj, hp)], axis=0)

        def attn_full(full):
            w_in = full[:, :, : 3 * hp].reshape(dp, tp, 3, hp, width)
            w_in = w_in.transpose(2, 1, 0, 3, 4).reshape(3 * width, width)
            w_out = full[:, :, 3 * hp : 4 * hp].transpose(1, 0, 2, 3).reshape(width, width)
            return w_in, w_out

        def in_rows(inproj):
            return inproj.transpose(1, 2, 0)

        if (dp, tp) == (8, 4):
            space_in_w, space_out_w, time_in_w, time_out_w = [
                w.reshape(-1, width)
                for w in gather_weights(
                    [in_rows(space_inproj), space_outproj[None], in_rows(time_inproj), time_outproj[None]],
                    dp, tp,
                )
            ]
        else:
            space_in_w, space_out_w = attn_full(gather_all(attn_piece(space_inproj, space_outproj)))
            time_in_w, time_out_w = attn_full(gather_all(attn_piece(time_inproj, time_outproj)))
        full_feed = gather_all(
            jnp.concatenate([piece_of(up_weight, up), piece_of(down_weight, up)], axis=0)
        )
        up_w = full_feed[:, :, :up].reshape(dp * tp * up, width)
        down_w = full_feed[:, :, up:].reshape(dp * tp * up, width)
        biases = lax.all_gather(
            jnp.concatenate([up_bias, space_bias.reshape(-1), time_bias.reshape(-1)]),
            names["tensor"], axis=0, tiled=False,
        ).astype(F32)
        up_b = biases[:, :units].reshape(tp, dp, up).transpose(1, 0, 2).reshape(-1)

        def in_bias(start):
            pair = biases[:, start : start + 2 * heads_width].reshape(tp, 2, heads_width)
            pair = pair.transpose(1, 0, 2).reshape(2, width)
            return jnp.concatenate([pair[0], jnp.zeros((width,), F32), pair[1]])

        space_b, time_b = in_bias(units), in_bias(units + 2 * heads_width)

        seqs = own // TIMES
        slots = TIMES * SLOT

        def pad_rows(x):
            x = x.reshape(TIMES, seqs, width)
            return jnp.pad(x, ((0, 0), (0, SLOT - seqs), (0, 0))).reshape(slots, width)

        def unpad(x):
            return x.reshape(TIMES, SLOT, width)[:, :seqs].reshape(tokens.shape)

        def exchange(x):
            return regroup(x.reshape(TIMES, SLOT, width)).reshape(slots, width)

        cot = exchange(pad_rows(cotangent))

        resid = pad_rows(tokens).astype(F32)
        space_n, space_r = norm_stats(resid)
        space_in = (space_n * space_gain + space_shift).astype(BF16)
        space_qkv = (dot(space_in, space_in_w, NT) + space_b).astype(BF16)
        space_mix = attention_call(attend_kernel, [space_qkv], width, False)
        after_space = resid + dot(space_mix, space_out_w, NN) + space_outbias.astype(F32)
        tn, _ = norm_stats(after_space)
        time_in_own = (tn * time_gain + time_shift).astype(BF16)

        time_in = exchange(time_in_own)
        after_space_p = exchange(after_space)
        time_qkv = (dot(time_in, time_in_w, NT) + time_b).astype(BF16)
        time_mix = attention_call(attend_kernel, [time_qkv], width, True)
        after_time = after_space_p + dot(time_mix, time_out_w, NN) + time_outbias.astype(F32)
        feed_n, feed_r = norm_stats(after_time)
        feed_in = (feed_n * feed_gain + feed_shift).astype(BF16)
        pre = dot(feed_in, up_w, NT) + up_b
        hidden = gelu_exact(pre).astype(BF16)
        layer_p = (after_time + dot(hidden, down_w, NN) + down_bias.astype(F32)).astype(BF16)
        layer_out = unpad(exchange(layer_p))

        upstream = cot.astype(F32)
        down_bias_g = jnp.sum(upstream, axis=0)
        down_g = dot(hidden, cot, TN).astype(BF16)
        pre_g = (dot(cot, down_w, NT) * gelu_slope(pre)).astype(BF16)
        up_g = dot(pre_g, feed_in, TN).astype(BF16)
        up_bias_g = jnp.sum(pre_g.astype(F32), axis=0)
        feed_g = dot(pre_g, up_w, NN)
        feed_gain_g = jnp.sum(feed_g * feed_n, axis=0)
        feed_shift_g = jnp.sum(feed_g, axis=0)
        after_time_g = upstream + norm_back(feed_g, feed_n, feed_r, feed_gain)

        def scatter(grad):
            return lax.psum_scatter(grad, every, scatter_dimension=0, tiled=False)

        feed_pack = jnp.concatenate(
            [up_g.reshape(dp * tp, up, width), down_g.reshape(dp * tp, up, width)], axis=1
        )
        feed_pack, after_time_g = lax.optimization_barrier((feed_pack, after_time_g))
        feed_part = scatter(feed_pack)

        def attention_back(branch, normed_in, qkv, mix, w_in, w_out, temporal):
            outbias_g = jnp.sum(branch.astype(F32), axis=0)
            mix_g = dot(branch, w_out, NT).astype(BF16)
            qkv_g = attention_call(attend_back_kernel, [qkv, mix_g], 3 * width, temporal)
            normed_g = dot(qkv_g, w_in, NN)
            return normed_g, qkv_g, outbias_g

        def attention_weights(branch, normed_in, mix, qkv_g):
            sums = jnp.sum(qkv_g.astype(F32), axis=0).reshape(3, width)
            out_g = dot(mix, branch, TN).astype(BF16)
            in_g = dot(qkv_g, normed_in, TN).astype(BF16)
            pack = jnp.concatenate(
                [
                    in_g.reshape(3, tp, dp, hp, width)
                    .transpose(2, 1, 0, 3, 4)
                    .reshape(dp * tp, 3 * hp, width),
                    out_g.reshape(tp, dp, hp, width)
                    .transpose(1, 0, 2, 3)
                    .reshape(dp * tp, hp, width),
                ],
                axis=1,
            )
            return pack, sums

        time_branch = after_time_g.astype(BF16)
        time_in_g, time_qkv_g, time_outbias_g = attention_back(
            time_branch, time_in, time_qkv, time_mix, time_in_w, time_out_w, True
        )
        tn_p, tr_p = norm_stats(after_space_p)
        time_gain_g = jnp.sum(time_in_g * tn_p, axis=0)
        time_shift_g = jnp.sum(time_in_g, axis=0)
        after_space_g_p = after_time_g + norm_back(time_in_g, tn_p, tr_p, time_gain)

        high_p = after_space_g_p.astype(BF16)
        low_p = (after_space_g_p - high_p.astype(F32)).astype(BF16)
        high = exchange(high_p)
        low = exchange(low_p)
        time_pack, time_sums = attention_weights(time_branch, time_in, time_mix, time_qkv_g)
        after_space_g = high.astype(F32) + low.astype(F32)

        space_in_g, space_qkv_g, space_outbias_g = attention_back(
            high, space_in, space_qkv, space_mix, space_in_w, space_out_w, False
        )
        space_pack, space_sums = attention_weights(high, space_in, space_mix, space_qkv_g)
        attn_part = scatter(jnp.concatenate([time_pack, space_pack], axis=1))
        space_gain_g = jnp.sum(space_in_g * space_n, axis=0)
        space_shift_g = jnp.sum(space_in_g, axis=0)
        input_g = unpad(after_space_g + norm_back(space_in_g, space_n, space_r, space_gain))

        small = jnp.concatenate(
            [
                space_gain_g, space_shift_g, space_outbias_g, time_gain_g, time_shift_g,
                time_outbias_g, feed_gain_g, feed_shift_g, down_bias_g,
                space_sums[0], space_sums[2], time_sums[0], time_sums[2],
                up_bias_g.reshape(dp, tp, up).transpose(1, 0, 2).reshape(-1),
            ]
        )
        small = lax.psum(small, every)
        rows = small[: 13 * width].reshape(13, width)
        head_rows = lax.dynamic_slice_in_dim(rows[9:], k_index * heads_width, heads_width, 1)
        up_bias_out = lax.dynamic_slice_in_dim(small[13 * width :], k_index * units, units, 0)

        def spread(part):
            return lax.all_gather(part, names["dp"], axis=0, tiled=False)

        def attn_out(full):
            in_out = full[:, : 3 * hp].reshape(dp, 3, hp, width).transpose(1, 0, 2, 3)
            in_out = in_out.reshape(3, heads_width, width).transpose(2, 0, 1).astype(F32)
            return in_out, full[:, 3 * hp :].reshape(heads_width, width).astype(F32)

        feed_all = spread(feed_part)
        attn_all = spread(attn_part)
        time_in_out, time_out_out = attn_out(attn_all[:, : 4 * hp])
        space_in_out, space_out_out = attn_out(attn_all[:, 4 * hp :])
        return (
            layer_out,
            input_g,
            rows[0], rows[1], space_in_out, head_rows[0:2], space_out_out, rows[2],
            rows[3], rows[4], time_in_out, head_rows[2:4], time_out_out, rows[5],
            rows[6], rows[7],
            feed_all[:, :up].reshape(units, width).astype(F32),
            up_bias_out,
            feed_all[:, up:].reshape(units, width).astype(F32),
            rows[8],
        )

    return per_device


def solution(mesh):
    inner, names, dp, tp = build(mesh)
    every, tensor = ("a", "b", "c"), names["tensor"]
    frames = P(every, None, None)
    head_in = P(None, None, tensor)
    head_bias = P(None, tensor)
    row = P(tensor, None)
    return jax.shard_map(
        make_device(names, dp, tp),
        mesh=inner,
        in_specs=(
            frames, P(), P(), head_in, head_bias, row, P(),
            P(), P(), head_in, head_bias, row, P(),
            P(), P(), row, P(tensor), row, P(), frames,
        ),
        out_specs=(
            frames, frames, P(), P(), head_in, head_bias, row, P(),
            P(), P(), head_in, head_bias, row, P(),
            P(), P(), row, P(tensor), row, P(),
        ),
        check_vma=False,
    )
```

time: 904 us -> 704 us (0.78)
  local copies, waits for them, and re-layouts: 218 us -> 49.3 us
  waiting for transfers between devices: 384 us -> 229 us
  Pallas kernels: 0 us -> 131 us
  blocking collectives: 40.2 us -> 98.3 us
  matrix products: 147 us -> 116 us
  other arithmetic: 58 us -> 35.8 us
    pallas_call x0 -> x5, Pallas kernels: none -> 131 us  [the longest x4 71.4 us: attention_call(): pl.pallas_call(functools.partial(kernel, temporal=temporal), grid=grid, i...]
    reduce_scatter x3 -> x2, waiting for transfers between devices: 208 us -> 139 us  [scatter(): return lax.psum_scatter(grad, every, scatter_dimension=0, tiled=False)]
    all_gather x3 -> x1, waiting for transfers between devices: 62.6 us -> 0.02 us  [gather_all(): full = lax.all_gather(piece, every, axis=0, tiled=False)]
    convert_element_type x13 -> x0, local copies, waits for them, and re-layouts: 60.2 us -> none  [the longest x4 38.2 us: attention_back(): qkv_g = jnp.stack([qg, kg, vg], axis=2).astype(BF16).reshape(own, 3 * width)]
    reshape x28 -> x13, local copies, waits for them, and re-layouts: 67.7 us -> 13.7 us  [the longest x2 4.59 us: unpad(): return x.reshape(TIMES, SLOT, width)[:, :seqs].reshape(tokens.shape)]
    all_to_all x0 -> x1, blocking collectives: none -> 42.8 us  [regroup(): lax.all_to_all(x, names['time'], split_axis=0, concat_axis=0, tiled=True)]
    dot_general x12 -> x0, matrix products: 42 us -> none  [esum(): return jnp.einsum(form, a, b, preferred_element_type=F32)]
    all_gather x3 -> x2, waiting for transfers between devices: 20.5 us -> 0.01 us  [spread(): return lax.all_gather(part, names['dp'], axis=0, tiled=False)]
  transfers between devices with their start and end apart: 15 -> 10, of which waited for: 7 -> 6; matrix products, arithmetic and copies ran while one was open for 35% -> 20% of each run, Pallas kernels for 0% -> 19%
where the time goes in v2:
time: 704 us; the launch traced here: 696 us
  waiting for transfers between devices  229 us (33%)
  Pallas kernels  131 us (19%)
  matrix products  116 us (16%)
  blocking collectives  98.3 us (14%)
  local copies, waits for them, and re-layouts  49.3 us (7%)
  other arithmetic  35.8 us (5%)
  starting transfers between devices  21.5 us (3%)
  between operations  14.8 us (2%)
    reduce_scatter x2, waiting for transfers between devices, scatter(): return lax.psum_scatter(grad, every, scatter_dimension=0, tiled=False)  139 us
    dot_general x18, matrix products, dot(): return lax.dot_general(a, b, dims, preferred_element_type=F32)  116 us
    all_to_all x5, waiting for transfers between devices, regroup(): lax.all_to_all(x, names['time'], split_axis=0, concat_axis=0, tiled=True)  89.5 us
    pallas_call x4, Pallas kernels, attention_call(): pl.pallas_call(functools.partial(kernel, temporal=temporal), grid=grid, i...  71.4 us
    pallas_call x1, Pallas kernels, gather_weights(): pl.pallas_call(functools.partial(gather_kernel, count=count), out_shape=[...  59.9 us
    all_to_all x1, blocking collectives, regroup(): lax.all_to_all(x, names['time'], split_axis=0, concat_axis=0, tiled=True)  42.8 us
    psum x1, blocking collectives, per_device(): small = lax.psum(small, every)  40.5 us
    all_to_all x5, starting transfers between devices, regroup(): lax.all_to_all(x, names['time'], split_axis=0, concat_axis=0, tiled=True)  21.3 us
  transfers between devices with their start and end apart: 10, of which 6 were waited for; matrix products, arithmetic and copies ran while one was open for 20% of the time, Pallas kernels for 19%

profile of v2, /device:TPU:0, one launch (start us, length us, event | category | flops | bytes accessed | tf_op | source)
XLA Modules:
  0.0 696.2 jit_solution(16658656331820894420)
XLA Ops:
  11.9 14.9 %all-gather.2 = bf16[4,1,1536]{2,1,0:T(2,128)(2,1)S(1)} all-gather(bf16[1,1,1536]{2,1,0:T(2,128)(2,1)S(1)} %reshape.440), channel_id=2, replica_groups=mesh['a'=8,'b'=2,'c'=2] {'b','c'}, dimensions={0}, use_global_device_ids=true | all-gather | bytes 15360 | tf_op jit(solution)/shard_map/all_gather | solution.py:372
  29.4 59.9 %gather_weights.1 = (bf16[3,4,8,24,768]{4,3,2,1,0:T(8,128)(2,1)}, bf16[1,4,8,24,768]{4,3,2,1,0:T(8,128)(2,1)}, bf16[3,4,8,24,768]{4,3,2,1,0:T(8,128)(2,1)}, bf16[1,4,8,24,768]{4,3,2,1,0:T(8,128)(2,1)}) custom-call(bf16[3,8,24,768]{3,2,1,0:T(8,128)(2,1)} %bitcast.197, bf16[1,8,24,768]{3,2,1,0:T(8,128)(2,1)} %bitcast.199, bf16[3,8,24,768]{3,2,1,0:T(8,128)(2,1)} %bitcast.198, ...), custom_call_target="tpu_custom_call" | custom-call | bytes 94371840 | tf_op jit(solution)/shard_map/gather_weights/pallas_call | solution.py:282
  91.4 5.0 add_convert_fusion.1.qkv_ref
  96.4 9.1 %shard_map.347 = bf16[896,768]{1,0:T(8,128)(2,1)} custom-call(bf16[896,2304]{1,0:T(8,128)(2,1)} %add_convert_fusion.1.qkv_ref), custom_call_target="tpu_custom_call" | custom-call | flops 1233125376 | bytes 5505024 | tf_op jit(solution)/shard_map/pallas_call | solution.py:156
  109.8 42.8 %all_to_all.30 = bf16[16,56,768]{2,1,0:T(8,128)(2,1)} all-to-all(bf16[16,56,768]{2,1,0:T(8,128)(2,1)S(1)} %bitcast.174), channel_id=1, replica_groups=mesh['a'=8,'b'=2,'c'=2] {'a','b'}, dimensions={0} | all-to-all | bytes 2752512 | tf_op jit(solution)/shard_map/all_to_all | solution.py:320
  164.5 6.9 add_convert_fusion
  171.4 18.3 %shard_map.348 = bf16[16,56,768]{2,1,0:T(8,128)(2,1)} custom-call(bf16[16,56,2304]{2,1,0:T(8,128)(2,1)} %bitcast.165), custom_call_target="tpu_custom_call" | custom-call | flops 704643072 | bytes 5505024 | tf_op jit(solution)/shard_map/pallas_call | solution.py:156
  189.8 30.9 %all-to-all-done = f32[16,56,768]{2,1,0:T(8,128)S(1)} async-done(((f32[16,56,768]{2,1,0:T(8,128)}), f32[16,56,768]{2,1,0:T(8,128)S(1)}, u32[]{:S(2)}, u32[]{:S(2)}) %all-to-all-start) | async-done | bytes 2752544 | tf_op jit(solution)/shard_map/all_to_all | solution.py:320
  230.2 8.4 %fusion.32 = (bf16[8,4,96,768]{3,2,1,0:T(8,128)(2,1)}, bf16[8,4,96,768]{3,2,1,0:T(8,128)(2,1)}) fusion(bf16[8,4,192,768]{3,2,1,0:T(8,128)(2,1)} %bitcast.172), kind=kLoop, calls=%fused_computation.123 | loop fusion | bytes 18874368 | tf_op jit(solution)/shard_map/slice | solution.py:371
  238.6 11.5 %multiply_convert_fusion = (bf16[896,3072]{1,0:T(8,128)(2,1)}, f32[896,3072]{1,0:T(8,128)}) fusion(f32[3072]{0:T(1024)S(1)} %add.185, bf16[3072,768]{1,0:T(8,128)(2,1)} %bitcast.179, f32[896,768]{1,0:T(8,128)S(1)} %copy-done.6, f32[768]{0:T(1024)S(1)} %copy-done.31, f32[768]{0:T(1024)S(1)} %copy-done.22, f32[896]{0:T(1024)S(1)} %add_rsqrt_fusion.2, ...), kind=kOutput, calls=%fused_computation.8 | convolution fusion | flops 4247814144 | bytes 24011776 | tf_op jit(solution)/shard_map/dot_general | solution.py:25
  250.1 8.7 %all-to-all-done.3 = bf16[16,56,768]{2,1,0:T(8,128)(2,1)} async-done(((bf16[16,56,768]{2,1,0:T(8,128)(2,1)}), bf16[16,56,768]{2,1,0:T(8,128)(2,1)}, u32[]{:S(2)}, u32[]{:S(2)}) %all-to-all-start.3) | async-done | bytes 1376288 | tf_op jit(solution)/shard_map/all_to_all | solution.py:320
  258.8 11.1 %convert_reduce_fusion = (f32[3072]{0:T(1024)S(1)}, bf16[896,3072]{1,0:T(8,128)(2,1)S(1)}) fusion(f32[896,3072]{1,0:T(8,128)} %get-tuple-element.143, f32[3072]{0:T(1024)S(1)} %add.185, bf16[896,768]{1,0:T(8,128)(2,1)} %bitcast.25, bf16[3072,768]{1,0:T(8,128)(2,1)} %bitcast.177), kind=kOutput, calls=%fused_computation.7 | convolution fusion | flops 4263638016 | bytes 22634496 | tf_op jit(solution)/shard_map/dot_general | solution.py:25
  269.9 6.3 multiply_reduce_fusion
  276.2 6.1 convolution_convert_fusion.1
  282.4 16.2 %convolution_convert_fusion = bf16[3072,768]{1,0:T(8,128)(2,1)S(1)} fusion(bf16[896,3072]{1,0:T(8,128)(2,1)S(1)} %bitcast.216, bf16[896,768]{1,0:T(8,128)(2,1)} %bitcast.25), kind=kOutput, calls=%fused_computation.17 | convolution fusion | flops 4230217728 | bytes 11599872 | tf_op jit(solution)/shard_map/dot_general | solution.py:25
  312.4 23.8 %shard_map.349 = bf16[16,56,2304]{2,1,0:T(8,128)(2,1)} custom-call(bf16[16,56,2304]{2,1,0:T(8,128)(2,1)} %bitcast.166, bf16[16,56,768]{2,1,0:T(8,128)(2,1)} %bitcast.189), custom_call_target="tpu_custom_call" | custom-call | flops 1761607680 | bytes 9633792 | tf_op jit(solution)/shard_map/pallas_call | solution.py:156
  336.2 7.5 %multiply_reduce_fusion.1 = (f32[768]{0:T(1024)S(1)}, f32[896]{0:T(1024)S(1)}, f32[896]{0:T(1024)S(1)}, f32[768]{0:T(1024)S(1)}, f32[896,768]{1,0:T(8,128)S(1)}) fusion(f32[16,56,768]{2,1,0:T(8,128)S(1)} %all-to-all-done, f32[896]{0:T(1024)S(1)} %div.57, f32[896]{0:T(1024)S(1)} %rsqrt.43, f32[768]{0:T(1024)S(1)} %copy-done.21, ...), kind=kOutput, calls=%fused_computation.51 | convolution fusion | flops 3177083648 | bytes 13196288 | tf_op jit(solution)/shard_map/dot_general | solution.py:25
  361.9 46.6 %all-to-all-done.4 = bf16[16,56,768]{2,1,0:T(8,128)(2,1)S(1)} async-done(((bf16[16,56,768]{2,1,0:T(8,128)(2,1)}), bf16[16,56,768]{2,1,0:T(8,128)(2,1)S(1)}, u32[]{:S(2)}, u32[]{:S(2)}) %all-to-all-start.4) | async-done | bytes 1376288 | tf_op jit(solution)/shard_map/all_to_all | solution.py:320
  413.4 20.2 %shard_map.350 = bf16[896,2304]{1,0:T(8,128)(2,1)} custom-call(bf16[896,2304]{1,0:T(8,128)(2,1)} %add_convert_fusion.1.qkv_ref, bf16[896,768]{1,0:T(8,128)(2,1)} %convolution_convert_fusion.3.mix_g_ref), custom_call_target="tpu_custom_call" | custom-call | flops 3082813440 | bytes 9633792 | tf_op jit(solution)/shard_map/pallas_call | solution.py:156
  433.6 8.8 %fusion.24 = (f32[768]{0:T(1024)S(1)}, f32[896]{0:T(1024)S(1)}, f32[896]{0:T(1024)S(1)}, f32[768]{0:T(1024)S(1)}, bf16[896,768]{1,0:T(8,128)(2,1)S(1)}, /*index=5*/f32[896,768]{1,0:T(8,128)}) fusion(f32[896]{0:T(1024)S(1)} %div.60, f32[896]{0:T(1024)S(1)} %rsqrt.44, bf16[16,49,768]{2,1,0:T(8,128)(2,1)S(1)} %copy-done.1, f32[768]{0:T(1024)S(1)} %copy-done.20, ...), kind=kOutput, calls=%fused_computation.45 | convolution fusion | flops 3179836160 | bytes 13027328 | tf_op jit(solution)/shard_map/dot_general | solution.py:25
  458.2 20.9 %reduce-scatter.5.cloned.1.call-done = bf16[1,192,768]{2,1,0:T(8,128)(2,1)} async-done(((bf16[32,192,768]{2,1,0:T(8,128)(2,1)}), bf16[1,192,768]{2,1,0:T(8,128)(2,1)}) %reduce-scatter.5.cloned.1.call-update) | async-done | bytes 294928 | tf_op jit(solution)/shard_map/reduce_scatter | solution.py:433
  479.2 10.3 %add_convert_fusion.2 = bf16[896,768]{1,0:T(8,128)(2,1)} fusion(f32[896,768]{1,0:T(8,128)} %copy-done.5, bf16[896,3072]{1,0:T(8,128)(2,1)} %get-tuple-element.142, bf16[3072,768]{1,0:T(8,128)(2,1)} %bitcast.178, f32[768]{0:T(1024)S(1)} %convert_element_type.190), kind=kOutput, calls=%fused_computation.59 | convolution fusion | flops 4229922816 | bytes 14355456 | tf_op jit(solution)/shard_map/dot_general | solution.py:25
  502.0 118.5 %reduce-scatter.3.cloned.1.call-done = bf16[1,192,768]{2,1,0:T(8,128)(2,1)} async-done(((bf16[32,192,768]{2,1,0:T(8,128)(2,1)}), bf16[1,192,768]{2,1,0:T(8,128)(2,1)}) %reduce-scatter.3.cloned.1.call-update) | async-done | bytes 294928 | tf_op jit(solution)/shard_map/reduce_scatter | solution.py:433
  635.8 40.5 %psum.7 = f32[13056]{0:T(1024)S(1)} all-reduce(f32[13056]{0:T(1024)S(1)} %constant_dynamic-update-slice_fusion), channel_id=1, replica_groups=mesh['a'=8,'b'=2,'c'=2] {'a','b','c'}, use_global_device_ids=true, to_apply=%region_26.27 | all-reduce | flops 13056 | bytes 104448 | tf_op jit(solution)/shard_map/psum | solution.py:498
  (206 shorter events, 128.0 us)
Async XLA Ops:
  7.2 223.0 %all-gather.11.cloned.1.call-start = ((), (), s32[]{:S(2)}) async-start(), calls=%async_computation.12 | async-start | bytes 9732096 | tf_op jit(solution)/shard_map/all_gather | solution.py:323
  29.2 60.9 %copy-start = (bf16[16,49,768]{2,1,0:T(8,128)(2,1)}, bf16[16,49,768]{2,1,0:T(8,128)(2,1)S(1)}, u32[]{:S(2)}) copy-start(bf16[16,49,768]{2,1,0:T(8,128)(2,1)S(1)} %reshape.386) | copy-start | bytes 3612676
  29.3 60.8 %copy-start.19 = (f32[768]{0:T(1024)S(1)}, f32[768]{0:T(1024)}, u32[]{:S(2)}) copy-start(f32[768]{0:T(1024)} %param.21) | copy-start | bytes 9220
  29.4 60.8 %copy-start.23 = (f32[768]{0:T(1024)S(1)}, f32[768]{0:T(1024)}, u32[]{:S(2)}) copy-start(f32[768]{0:T(1024)} %param.22) | copy-start | bytes 9220
  96.4 9.1 %copy-start.29 = (bf16[1,4,8,24,768]{4,3,2,1,0:T(8,128)(2,1)S(1)}, bf16[1,4,8,24,768]{4,3,2,1,0:T(8,128)(2,1)}, u32[]{:S(2)}) copy-start(bf16[1,4,8,24,768]{4,3,2,1,0:T(8,128)(2,1)} %get-tuple-element.27) | copy-start | bytes 3538948
  152.6 68.0 %all-to-all-start = ((f32[16,56,768]{2,1,0:T(8,128)}), f32[16,56,768]{2,1,0:T(8,128)S(1)}, u32[]{:S(2)}, u32[]{:S(2)}) async-start(f32[16,56,768]{2,1,0:T(8,128)} %bitcast.163), calls=%async_computation | async-start | bytes 5505024 | tf_op jit(solution)/shard_map/all_to_all | solution.py:320
  220.7 38.1 %all-to-all-start.3 = ((bf16[16,56,768]{2,1,0:T(8,128)(2,1)}), bf16[16,56,768]{2,1,0:T(8,128)(2,1)}, u32[]{:S(2)}, u32[]{:S(2)}) async-start(bf16[16,56,768]{2,1,0:T(8,128)(2,1)} %pad.8), calls=%async_computation.3 | async-start | bytes 2752512 | tf_op jit(solution)/shard_map/all_to_all | solution.py:320
  225.1 254.0 %reduce-scatter.5.cloned.1.call-start = ((), (), s32[]{:S(2)}) async-start(), calls=%async_computation.10 | async-start | bytes 9732096 | tf_op jit(solution)/shard_map/reduce_scatter | solution.py:433
  230.2 8.4 %copy-start.6 = (f32[896,768]{1,0:T(8,128)S(1)}, f32[896,768]{1,0:T(8,128)}, u32[]{:S(2)}) copy-start(f32[896,768]{1,0:T(8,128)} %copy-done.5) | copy-start | bytes 8257540
  258.8 11.1 %copy-start.7 = (f32[896,768]{1,0:T(8,128)S(1)}, f32[896,768]{1,0:T(8,128)}, u32[]{:S(2)}) copy-start(f32[896,768]{1,0:T(8,128)} %copy-done.5) | copy-start | bytes 8257540
  258.8 11.2 %copy-start.11 = (bf16[8,4,96,768]{3,2,1,0:T(8,128)(2,1)S(1)}, bf16[8,4,96,768]{3,2,1,0:T(8,128)(2,1)}, u32[]{:S(2)}) copy-start(bf16[8,4,96,768]{3,2,1,0:T(8,128)(2,1)} %get-tuple-element.111) | copy-start | bytes 14155780
  269.9 12.4 %slice-start = ((s8[5505024]{0:T(1024)(128)(4,1)}), s8[4194304]{0:T(1024)(128)(4,1)S(1)}, s32[]{:S(2)}) async-start(s8[5505024]{0:T(1024)(128)(4,1)} %bitcast.215), calls=%async_computation.13 | async-start | bytes 8388608
  346.8 61.7 %all-to-all-start.4 = ((bf16[16,56,768]{2,1,0:T(8,128)(2,1)}), bf16[16,56,768]{2,1,0:T(8,128)(2,1)S(1)}, u32[]{:S(2)}, u32[]{:S(2)}) async-start(bf16[16,56,768]{2,1,0:T(8,128)(2,1)} %bitcast.30), calls=%async_computation.4 | async-start | bytes 2752512 | tf_op jit(solution)/shard_map/all_to_all | solution.py:320
  350.7 269.9 %reduce-scatter.3.cloned.1.call-start = ((), (), s32[]{:S(2)}) async-start(), calls=%async_computation.8 | async-start | bytes 9732096 | tf_op jit(solution)/shard_map/reduce_scatter | solution.py:433
  359.8 48.7 %copy-start.15 = (bf16[896,768]{1,0:T(8,128)(2,1)S(1)}, bf16[896,768]{1,0:T(8,128)(2,1)}, u32[]{:S(2)}) copy-start(bf16[896,768]{1,0:T(8,128)(2,1)} %shard_map.347) | copy-start | bytes 4128772
  413.4 20.2 %copy-start.1 = (bf16[16,49,768]{2,1,0:T(8,128)(2,1)S(1)}, bf16[16,49,768]{2,1,0:T(8,128)(2,1)}, u32[]{:S(2)}) copy-start(bf16[16,49,768]{2,1,0:T(8,128)(2,1)} %copy-done) | copy-start | bytes 3612676
  413.4 20.2 %copy-start.20 = (f32[768]{0:T(1024)S(1)}, f32[768]{0:T(1024)}, u32[]{:S(2)}) copy-start(f32[768]{0:T(1024)} %param.21) | copy-start | bytes 9220
  413.4 20.2 %copy-start.24 = (f32[768]{0:T(1024)S(1)}, f32[768]{0:T(1024)}, u32[]{:S(2)}) copy-start(f32[768]{0:T(1024)} %param.22) | copy-start | bytes 9220
  433.6 8.9 %copy-start.12 = (bf16[896,2304]{1,0:T(8,128)(2,1)S(1)}, bf16[896,2304]{1,0:T(8,128)(2,1)}, u32[]{:S(2)}) copy-start(bf16[896,2304]{1,0:T(8,128)(2,1)} %shard_map.350) | copy-start | bytes 12386308
  453.8 25.4 %copy-start.27 = (bf16[768]{0:T(1024)(128)(2,1)S(1)}, bf16[768]{0:T(1024)(128)(2,1)}, u32[]{:S(2)}) copy-start(bf16[768]{0:T(1024)(128)(2,1)} %param.38) | copy-start | bytes 4612
  453.8 39.0 %all-to-all-start.5 = ((bf16[16,56,768]{2,1,0:T(8,128)(2,1)}), bf16[16,56,768]{2,1,0:T(8,128)(2,1)}, u32[]{:S(2)}, u32[]{:S(2)}) async-start(bf16[16,56,768]{2,1,0:T(8,128)(2,1)} %bitcast.173), calls=%async_computation.5 | async-start | bytes 2752512 | tf_op jit(solution)/shard_map/all_to_all | solution.py:320
  458.2 220.1 %all-gather.9.cloned.1.call-start = ((), (), s32[]{:S(2)}) async-start(), calls=%async_computation.11 | async-start | bytes 2654208 | tf_op jit(solution)/shard_map/all_gather | solution.py:504
  492.7 131.7 %all-to-all-start.2 = ((bf16[16,56,768]{2,1,0:T(8,128)(2,1)}), bf16[16,56,768]{2,1,0:T(8,128)(2,1)}, u32[]{:S(2)}, u32[]{:S(2)}) async-start(bf16[16,56,768]{2,1,0:T(8,128)(2,1)} %bitcast.193), calls=%async_computation.2 | async-start | bytes 2752512 | tf_op jit(solution)/shard_map/all_to_all | solution.py:320
  497.1 186.2 %all-gather.7.cloned.1.call-start = ((), (), s32[]{:S(2)}) async-start(), calls=%async_computation.9 | async-start | bytes 2654208 | tf_op jit(solution)/shard_map/all_gather | solution.py:504
  (20 other events, 74.2 us)
Sparse Core Ops, SparseCore 0:
  11.4 101.0 all-gather.10
  307.2 171.8 reduce-scatter.4
  485.0 135.4 reduce-scatter.2
  622.3 28.1 all-gather.8
  652.2 29.1 all-gather.6

commit v3 on v2

--- a/solution.py
+++ b/solution.py
@@ -299,6 +299,126 @@
     return [f.reshape(f.shape[0], -1, f.shape[-1]) for f in fulls]
 
 
+BLOCKS = (6, 2, 4, 0)
+
+
+def add_into(target, source):
+    def step(i, carry):
+        target[i] = (target[i].astype(F32) + source[i].astype(F32)).astype(BF16)
+        return carry
+
+    lax.fori_loop(0, target.shape[0], step, 0)
+
+
+def scatter_kernel(*refs):
+    packs, outs = refs[0:2], refs[2:4]
+    accs, cores, firsts, seconds, columns = (refs[4 + 2 * i : 6 + 2 * i] for i in range(5))
+    send_sems, recv_sems, local_sems = refs[14:]
+    me, z, part = here()
+    loads = {}
+    for b, mask in enumerate(BLOCKS):
+        for s in (0, 1):
+            loads[s, mask] = pltpu.make_async_copy(
+                packs[s].at[part(mask)], accs[s].at[b], local_sems.at[2 * b + s]
+            )
+            loads[s, mask].start()
+    greet(part, z)
+    copies = Copies(send_sems, recv_sems)
+    first_core = {}
+    for b, mask in enumerate(BLOCKS):
+        for s in (0, 1):
+            first_core[s, mask] = copies.start(
+                packs[s].at[part(mask ^ 1)], cores[s].at[b], plane(part, 1)
+            )
+    near, far = (2, 4), (4, 2)
+    hop = {}
+    for b, mask in enumerate(BLOCKS):
+        for s in (0, 1):
+            loads[s, mask].wait()
+            first_core[s, mask].wait_recv()
+            add_into(accs[s].at[b], cores[s].at[b])
+        for s in (0, 1):
+            if mask & near[s]:
+                slot = 0 if mask == 6 else 1
+                hop[s, slot] = copies.start(
+                    accs[s].at[b], firsts[s].at[slot], plane(part, near[s])
+                )
+    for s in (0, 1):
+        b = BLOCKS.index(far[s])
+        hop[s, 0].wait_recv()
+        add_into(accs[s].at[b], firsts[s].at[0])
+    for s in (0, 1):
+        b = BLOCKS.index(far[s])
+        hop[s, 2] = copies.start(accs[s].at[b], seconds[s], plane(part, far[s]))
+    for s in (0, 1):
+        hop[s, 1].wait_recv()
+        add_into(accs[s].at[3], firsts[s].at[1])
+    lines = {}
+    for s in (0, 1):
+        hop[s, 2].wait_recv()
+        add_into(accs[s].at[3], seconds[s])
+    for s in (0, 1):
+        for j in (1, 2, 3):
+            to = (z + j) % 4
+            lines[s, j] = copies.start(accs[s].at[3, to], columns[s].at[j - 1], column(to))
+    for s in (0, 1):
+        total = accs[s][3, z].astype(F32)
+        for j in (1, 2, 3):
+            lines[s, j].wait_recv()
+            total = total + columns[s][j - 1].astype(F32)
+        outs[s][me] = total.astype(BF16)
+
+    def push(s, mask, to):
+        at = part(mask)
+        return copies.start(outs[s].at[at], outs[s].at[at], plane(part, to))
+
+    ends = []
+    along = {}
+    for s in (0, 1):
+        along[s, 2] = push(s, 0, 2)
+        along[s, 4] = push(s, 0, 4)
+        ends.append(push(s, 0, 1))
+    relays = []
+    for s in (0, 1):
+        for mask in (2, 4):
+            along[s, mask].wait_recv()
+            if mask == near[s]:
+                relays.append((s, push(s, mask, far[s])))
+            ends.append(push(s, mask, 1))
+    for s, copy in relays:
+        copy.wait_recv()
+        ends.append(push(s, 6, 1))
+    for copy in ends:
+        copy.wait_recv()
+    for copy in copies.made:
+        copy.wait_send()
+
+
+def scatter_sum(packs):
+    count = 2 * (4 + 3 + 3 + 3 + 4)
+    anywhere = pl.BlockSpec(memory_space=pl.ANY)
+    rows = [p.shape[2:] for p in packs]
+
+    def scratch(*lead):
+        return [pltpu.VMEM(lead + r, BF16) for r in rows]
+
+    return pl.pallas_call(
+        scatter_kernel,
+        out_shape=[jax.ShapeDtypeStruct((8,) + r, BF16) for r in rows],
+        in_specs=[anywhere] * 2,
+        out_specs=[pl.BlockSpec(memory_space=pltpu.VMEM)] * 2,
+        scratch_shapes=scratch(4, 4) + scratch(4, 4) + scratch(2, 4) + scratch(4) + scratch(3)
+        + [
+            pltpu.SemaphoreType.DMA((count,)),
+            pltpu.SemaphoreType.DMA((count,)),
+            pltpu.SemaphoreType.DMA((8,)),
+        ],
+        compiler_params=pltpu.CompilerParams(collective_id=1, has_side_effects=True),
+        cost_estimate=pl.CostEstimate(flops=0, bytes_accessed=300000000, transcendentals=0),
+        name="scatter_sum",
+    )(*packs)
+
+
 def build(mesh):
     dp, tp = mesh.shape["dp"], mesh.shape["tensor"]
     count = dp * tp
@@ -353,26 +473,34 @@
         def in_rows(inproj):
             return inproj.transpose(1, 2, 0)
 
-        if (dp, tp) == (8, 4):
-            space_in_w, space_out_w, time_in_w, time_out_w = [
+        direct = (dp, tp) == (8, 4)
+        bias_shard = jnp.concatenate([up_bias, space_bias.reshape(-1), time_bias.reshape(-1)])
+        per_row = bias_shard.shape[0] // dp
+        if direct:
+            bias_rows = jnp.pad(
+                bias_shard.reshape(dp, 1, per_row), ((0, 0), (0, 7), (0, width - per_row))
+            )
+            space_in_w, space_out_w, time_in_w, time_out_w, bias_full = [
                 w.reshape(-1, width)
                 for w in gather_weights(
-                    [in_rows(space_inproj), space_outproj[None], in_rows(time_inproj), time_outproj[None]],
+                    [
+                        in_rows(space_inproj), space_outproj[None], in_rows(time_inproj),
+                        time_outproj[None], bias_rows.reshape(1, -1, width),
+                    ],
                     dp, tp,
                 )
             ]
+            biases = bias_full.reshape(tp, dp, 8, width)[:, :, 0, :per_row].reshape(tp, -1)
         else:
             space_in_w, space_out_w = attn_full(gather_all(attn_piece(space_inproj, space_outproj)))
             time_in_w, time_out_w = attn_full(gather_all(attn_piece(time_inproj, time_outproj)))
+            biases = lax.all_gather(bias_shard, names["tensor"], axis=0, tiled=False)
+        biases = biases.astype(F32)
         full_feed = gather_all(
             jnp.concatenate([piece_of(up_weight, up), piece_of(down_weight, up)], axis=0)
         )
         up_w = full_feed[:, :, :up].reshape(dp * tp * up, width)
         down_w = full_feed[:, :, up:].reshape(dp * tp * up, width)
-        biases = lax.all_gather(
-            jnp.concatenate([up_bias, space_bias.reshape(-1), time_bias.reshape(-1)]),
-            names["tensor"], axis=0, tiled=False,
-        ).astype(F32)
         up_b = biases[:, :units].reshape(tp, dp, up).transpose(1, 0, 2).reshape(-1)
 
         def in_bias(start):
@@ -403,11 +531,10 @@
         space_qkv = (dot(space_in, space_in_w, NT) + space_b).astype(BF16)
         space_mix = attention_call(attend_kernel, [space_qkv], width, False)
         after_space = resid + dot(space_mix, space_out_w, NN) + space_outbias.astype(F32)
-        tn, _ = norm_stats(after_space)
-        time_in_own = (tn * time_gain + time_shift).astype(BF16)
-
-        time_in = exchange(time_in_own)
-        after_space_p = exchange(after_space)
+
+        after_space_p = exchange(after_space.astype(BF16)).astype(F32)
+        tn_p, tr_p = norm_stats(after_space_p)
+        time_in = (tn_p * time_gain + time_shift).astype(BF16)
         time_qkv = (dot(time_in, time_in_w, NT) + time_b).astype(BF16)
         time_mix = attention_call(attend_kernel, [time_qkv], width, True)
         after_time = after_space_p + dot(time_mix, time_out_w, NN) + time_outbias.astype(F32)
@@ -466,52 +593,68 @@
         time_in_g, time_qkv_g, time_outbias_g = attention_back(
             time_branch, time_in, time_qkv, time_mix, time_in_w, time_out_w, True
         )
-        tn_p, tr_p = norm_stats(after_space_p)
         time_gain_g = jnp.sum(time_in_g * tn_p, axis=0)
         time_shift_g = jnp.sum(time_in_g, axis=0)
         after_space_g_p = after_time_g + norm_back(time_in_g, tn_p, tr_p, time_gain)
 
-        high_p = after_space_g_p.astype(BF16)
-        low_p = (after_space_g_p - high_p.astype(F32)).astype(BF16)
-        high = exchange(high_p)
-        low = exchange(low_p)
+        high = exchange(after_space_g_p.astype(BF16))
         time_pack, time_sums = attention_weights(time_branch, time_in, time_mix, time_qkv_g)
-        after_space_g = high.astype(F32) + low.astype(F32)
+        after_space_g = high.astype(F32)
 
         space_in_g, space_qkv_g, space_outbias_g = attention_back(
             high, space_in, space_qkv, space_mix, space_in_w, space_out_w, False
         )
         space_pack, space_sums = attention_weights(high, space_in, space_mix, space_qkv_g)
-        attn_part = scatter(jnp.concatenate([time_pack, space_pack], axis=1))
         space_gain_g = jnp.sum(space_in_g * space_n, axis=0)
         space_shift_g = jnp.sum(space_in_g, axis=0)
         input_g = unpad(after_space_g + norm_back(space_in_g, space_n, space_r, space_gain))
 
-        small = jnp.concatenate(
+        shared = jnp.concatenate(
             [
                 space_gain_g, space_shift_g, space_outbias_g, time_gain_g, time_shift_g,
                 time_outbias_g, feed_gain_g, feed_shift_g, down_bias_g,
-                space_sums[0], space_sums[2], time_sums[0], time_sums[2],
-                up_bias_g.reshape(dp, tp, up).transpose(1, 0, 2).reshape(-1),
             ]
         )
-        small = lax.psum(small, every)
-        rows = small[: 13 * width].reshape(13, width)
-        head_rows = lax.dynamic_slice_in_dim(rows[9:], k_index * heads_width, heads_width, 1)
-        up_bias_out = lax.dynamic_slice_in_dim(small[13 * width :], k_index * units, units, 0)
+        headed = jnp.stack([space_sums[0], space_sums[2], time_sums[0], time_sums[2]])
+        headed = headed.reshape(4, tp, heads_width).transpose(1, 0, 2).reshape(tp, -1)
+        upped = up_bias_g.reshape(dp, tp, up).transpose(1, 0, 2).reshape(tp, -1)
+        sharded = jnp.concatenate([headed, upped], axis=1)
+        many, few = 9 * width // dp, sharded.shape[1] // dp
+        small = jnp.concatenate(
+            [
+                jnp.broadcast_to(shared.reshape(dp, 1, many), (dp, tp, many)),
+                sharded.reshape(tp, dp, few).transpose(1, 0, 2),
+                jnp.zeros((dp, tp, 2 * width - many - few), F32),
+            ],
+            axis=2,
+        ).astype(BF16)
+        small = jnp.pad(small.reshape(dp * tp, 2, width), ((0, 0), (0, 14), (0, 0)))
+        space_pack = jnp.concatenate([space_pack, small], axis=1)
 
         def spread(part):
             return lax.all_gather(part, names["dp"], axis=0, tiled=False)
+
+        if direct:
+            time_all, space_all = scatter_sum(
+                [x.reshape((dp, tp) + x.shape[1:]) for x in (time_pack, space_pack)]
+            )
+        else:
+            both = spread(scatter(jnp.concatenate([time_pack, space_pack], axis=1)))
+            time_all, space_all = both[:, : 4 * hp], both[:, 4 * hp :]
 
         def attn_out(full):
             in_out = full[:, : 3 * hp].reshape(dp, 3, hp, width).transpose(1, 0, 2, 3)
             in_out = in_out.reshape(3, heads_width, width).transpose(2, 0, 1).astype(F32)
-            return in_out, full[:, 3 * hp :].reshape(heads_width, width).astype(F32)
+            return in_out, full[:, 3 * hp : 4 * hp].reshape(heads_width, width).astype(F32)
 
         feed_all = spread(feed_part)
-        attn_all = spread(attn_part)
-        time_in_out, time_out_out = attn_out(attn_all[:, : 4 * hp])
-        space_in_out, space_out_out = attn_out(attn_all[:, 4 * hp :])
+        time_in_out, time_out_out = attn_out(time_all)
+        space_in_out, space_out_out = attn_out(space_all)
+        sums = space_all[:, 4 * hp : 4 * hp + 2].reshape(dp, 2 * width).astype(F32)
+        rows = sums[:, :many].reshape(9, width)
+        own_sums = sums[:, many : many + few].reshape(-1)
+        head_rows = own_sums[: 4 * heads_width].reshape(4, heads_width)
+        up_bias_out = own_sums[4 * heads_width :]
         return (
             layer_out,
             input_g,

time: 704 us -> 580 us (0.82)
  waiting for transfers between devices: 229 us -> 93.6 us
  Pallas kernels: 131 us -> 231 us
  blocking collectives: 98.3 us -> 0 us
  other arithmetic: 35.8 us -> 44.7 us
  local copies, waits for them, and re-layouts: 49.3 us -> 57.4 us
  matrix products: 116 us -> 108 us
    reduce_scatter x2 -> x1, waiting for transfers between devices: 139 us -> 28.8 us  [scatter(): return lax.psum_scatter(grad, every, scatter_dimension=0, tiled=False)]
    pallas_call x0 -> x1, Pallas kernels: none -> 92.2 us  [scatter_sum(): pl.pallas_call(scatter_kernel, out_shape=[jax.ShapeDtypeStruct((8,) + r,...]
    all_to_all x1 -> x0, blocking collectives: 42.8 us -> none  [regroup(): lax.all_to_all(x, names['time'], split_axis=0, concat_axis=0, tiled=True)]
    psum x1 -> x0, blocking collectives: 40.5 us -> none  [per_device(): small = lax.psum(small, every)]
    all_to_all x5 -> x4, waiting for transfers between devices: 89.5 us -> 64.7 us  [regroup(): lax.all_to_all(x, names['time'], split_axis=0, concat_axis=0, tiled=True)]
    all_gather x1 -> x0, blocking collectives: 14.9 us -> none  [per_device(): lax.all_gather(jnp.concatenate([up_bias, space_bias.reshape(-1), time_bia...]
    dot_general x18, matrix products: 116 us -> 108 us  [dot(): return lax.dot_general(a, b, dims, preferred_element_type=F32)]
    unnamed x87 -> x101, local copies, waits for them, and re-layouts: 14.7 us -> 12.8 us
  transfers between devices with their start and end apart: 10 -> 7, of which waited for: 6 -> 3; matrix products, arithmetic and copies ran while one was open for 20% -> 28% of each run, Pallas kernels for 19% -> 40%
where the time goes in v3:
time: 580 us; the launch traced here: 570 us
  Pallas kernels  231 us (40%)
  matrix products  108 us (19%)
  waiting for transfers between devices  93.6 us (16%)
  local copies, waits for them, and re-layouts  57.4 us (10%)
  other arithmetic  44.7 us (8%)
  starting transfers between devices  20.7 us (4%)
  between operations  15.1 us (3%)
    dot_general x18, matrix products, dot(): return lax.dot_general(a, b, dims, preferred_element_type=F32)  108 us
    pallas_call x1, Pallas kernels, scatter_sum(): pl.pallas_call(scatter_kernel, out_shape=[jax.ShapeDtypeStruct((8,) + r,...  92.2 us
    pallas_call x4, Pallas kernels, attention_call(): pl.pallas_call(functools.partial(kernel, temporal=temporal), grid=grid, i...  71.8 us
    pallas_call x1, Pallas kernels, gather_weights(): pl.pallas_call(functools.partial(gather_kernel, count=count), out_shape=[...  66.7 us
    all_to_all x4, waiting for transfers between devices, regroup(): lax.all_to_all(x, names['time'], split_axis=0, concat_axis=0, tiled=True)  64.7 us
    reduce_scatter x1, waiting for transfers between devices, scatter(): return lax.psum_scatter(grad, every, scatter_dimension=0, tiled=False)  28.8 us
    all_to_all x4, starting transfers between devices, regroup(): lax.all_to_all(x, names['time'], split_axis=0, concat_axis=0, tiled=True)  20.4 us
    unnamed x101, local copies, waits for them, and re-layouts  12.8 us
  transfers between devices with their start and end apart: 7, of which 3 were waited for; matrix products, arithmetic and copies ran while one was open for 28% of the time, Pallas kernels for 40%

profile of v3, /device:TPU:0, one launch (start us, length us, event | category | flops | bytes accessed | tf_op | source)
XLA Modules:
  0.0 570.0 jit_solution(16675002005675361926)
XLA Ops:
  14.5 66.7 %gather_weights.1 = (bf16[3,4,8,24,768]{4,3,2,1,0:T(8,128)(2,1)}, bf16[1,4,8,24,768]{4,3,2,1,0:T(8,128)(2,1)}, bf16[3,4,8,24,768]{4,3,2,1,0:T(8,128)(2,1)}, bf16...) custom-call(bf16[3,8,24,768]{3,2,1,0:T(8,128)(2,1)} %bitcast.212, bf16[1,8,24,768]{3,2,1,0:T(8,128)(2,1)} %bitcast.214, ...), custom_call_target="tpu_custom_call" | custom-call | bytes 98304000 | tf_op jit(solution)/shard_map/gather_weights/pallas_call | solution.py:282
  85.0 5.0 add_convert_fusion.1.qkv_ref
  90.0 9.1 %shard_map.347 = bf16[896,768]{1,0:T(8,128)(2,1)} custom-call(bf16[896,2304]{1,0:T(8,128)(2,1)} %add_convert_fusion.1.qkv_ref), custom_call_target="tpu_custom_call" | custom-call | flops 1233125376 | bytes 5505024 | tf_op jit(solution)/shard_map/pallas_call | solution.py:156
  102.8 5.9 %all-to-all-start = ((bf16[16,56,768]{2,1,0:T(8,128)(2,1)}), bf16[16,56,768]{2,1,0:T(8,128)(2,1)S(1)}, u32[]{:S(2)}, u32[]{:S(2)}) async-start(bf16[16,56,768]{2,1,0:T(8,128)(2,1)} %bitcast.208), calls=%async_computation | async-start | bytes 2752512 | tf_op jit(solution)/shard_map/all_to_all | solution.py:440
  112.7 29.5 %all-to-all-done = bf16[16,56,768]{2,1,0:T(8,128)(2,1)S(1)} async-done(((bf16[16,56,768]{2,1,0:T(8,128)(2,1)}), bf16[16,56,768]{2,1,0:T(8,128)(2,1)S(1)}, u32[]{:S(2)}, u32[]{:S(2)}) %all-to-all-start) | async-done | bytes 1376288 | tf_op jit(solution)/shard_map/all_to_all | solution.py:440
  148.2 5.0 add_convert_fusion
  153.2 18.3 %shard_map.348 = bf16[16,56,768]{2,1,0:T(8,128)(2,1)} custom-call(bf16[16,56,2304]{2,1,0:T(8,128)(2,1)} %bitcast.181), custom_call_target="tpu_custom_call" | custom-call | flops 704643072 | bytes 5505024 | tf_op jit(solution)/shard_map/pallas_call | solution.py:156
  176.7 8.3 %fusion.49 = (bf16[8,4,96,768]{3,2,1,0:T(8,128)(2,1)}, bf16[8,4,96,768]{3,2,1,0:T(8,128)(2,1)}) fusion(bf16[8,4,192,768]{3,2,1,0:T(8,128)(2,1)} %bitcast.188), kind=kLoop, calls=%fused_computation.139 | loop fusion | bytes 18874368 | tf_op jit(solution)/shard_map/slice | solution.py:503
  185.0 11.5 %multiply_convert_fusion = (bf16[896,3072]{1,0:T(8,128)(2,1)}, f32[896,3072]{1,0:T(8,128)}) fusion(f32[3072]{0:T(1024)S(1)} %add.168, bf16[3072,768]{1,0:T(8,128)(2,1)} %bitcast.193, f32[896,768]{1,0:T(8,128)S(1)} %copy-done.5, f32[768]{0:T(1024)S(1)} %copy-done.41, f32[768]{0:T(1024)S(1)} %copy-done.28, f32[896]{0:T(1024)S(1)} %add_rsqrt_fusion.2, ...), kind=kOutput, calls=%fused_computation.7 | convolution fusion | flops 4247814144 | bytes 24011776 | tf_op jit(solution)/shard_map/dot_general | solution.py:25
  196.6 11.1 %fusion.56 = (bf16[3072]{0:T(1024)(128)(2,1)S(1)}, bf16[896,3072]{1,0:T(8,128)(2,1)S(1)}) fusion(f32[896,3072]{1,0:T(8,128)} %get-tuple-element.144, f32[3072]{0:T(1024)S(1)} %add.168, bf16[896,768]{1,0:T(8,128)(2,1)S(1)} %bitcast.185, bf16[3072,768]{1,0:T(8,128)(2,1)} %bitcast.191), kind=kOutput, calls=%fused_computation.146 | convolution fusion | flops 4260885504 | bytes 22628352 | tf_op jit(solution)/shard_map/dot_general | solution.py:25
  207.7 6.9 %multiply_reduce_fusion = (f32[768]{0:T(1024)}, f32[896]{0:T(1024)S(1)}, f32[896]{0:T(1024)S(1)}, f32[768]{0:T(1024)}, f32[896,768]{1,0:T(8,128)}) fusion(f32[896,768]{1,0:T(8,128)S(1)} %copy-done.6, f32[896]{0:T(1024)S(1)} %add_rsqrt_fusion.2, f32[896]{0:T(1024)S(1)} %broadcast_multiply_fusion.8, f32[768]{0:T(1024)S(1)} %copy-done.28, ...), kind=kOutput, calls=%fused_computation.64 | convolution fusion | flops 4234048256 | bytes 15752192 | tf_op jit(solution)/shard_map/dot_general | solution.py:25
  214.7 6.1 %convolution_convert_fusion.1 = bf16[3072,768]{1,0:T(8,128)(2,1)S(1)} fusion(bf16[896,3072]{1,0:T(8,128)(2,1)S(1)} %get-tuple-element.149, f32[896,768]{1,0:T(8,128)S(1)} %copy-done.6, f32[768]{0:T(1024)S(1)} %copy-done.41, f32[768]{0:T(1024)S(1)} %copy-done.28, f32[896]{0:T(1024)S(1)} %add_rsqrt_fusion.2, f32[896]{0:T(1024)S(1)} %broadcast_multiply_fusion.8), kind=kOutput, calls=%fused_computation.15 | convolution fusion | flops 4233658368 | bytes 12989440 | tf_op jit(solution)/shard_map/dot_general | solution.py:25
  220.8 5.5 convolution_convert_fusion
  244.4 23.8 %shard_map.349 = bf16[16,56,2304]{2,1,0:T(8,128)(2,1)} custom-call(bf16[16,56,2304]{2,1,0:T(8,128)(2,1)} %bitcast.182, bf16[16,56,768]{2,1,0:T(8,128)(2,1)} %bitcast.204), custom_call_target="tpu_custom_call" | custom-call | flops 1761607680 | bytes 9633792 | tf_op jit(solution)/shard_map/pallas_call | solution.py:156
  272.4 8.2 %fusion.22 = (f32[768]{0:T(1024)}, f32[896]{0:T(1024)S(1)}, f32[896]{0:T(1024)S(1)}, f32[768]{0:T(1024)}, f32[896,768]{1,0:T(8,128)S(1)}) fusion(bf16[16,56,768]{2,1,0:T(8,128)(2,1)S(1)} %all-to-all-done, f32[896]{0:T(1024)S(1)} %div.49, f32[896]{0:T(1024)S(1)} %rsqrt.35, f32[768]{0:T(1024)S(1)} %copy-done.20, bf16[896,2304]{1,0:T(8,128)(2,1)} %bitcast.180, ...), kind=kOutput, calls=%fused_computation.38 | convolution fusion | flops 3177771776 | bytes 11820032 | tf_op jit(solution)/shard_map/dot_general | solution.py:25
  282.7 6.4 %all-to-all-start.3 = ((bf16[16,56,768]{2,1,0:T(8,128)(2,1)}), bf16[16,56,768]{2,1,0:T(8,128)(2,1)}, u32[]{:S(2)}, u32[]{:S(2)}) async-start(bf16[16,56,768]{2,1,0:T(8,128)(2,1)} %bitcast.31), calls=%async_computation.3 | async-start | bytes 2752512 | tf_op jit(solution)/shard_map/all_to_all | solution.py:440
  289.1 6.5 %bitcast_convert_fusion = bf16[2304,768]{1,0:T(8,128)(2,1)S(1)} fusion(bf16[16,56,2304]{2,1,0:T(8,128)(2,1)} %shard_map.349, bf16[16,56,768]{2,1,0:T(8,128)(2,1)S(1)} %copy-done.15), kind=kOutput, calls=%fused_computation.12 | convolution fusion | flops 3172663296 | bytes 9043968 | tf_op jit(solution)/shard_map/dot_general | solution.py:25
  301.4 9.5 %add_convert_fusion.2 = bf16[896,768]{1,0:T(8,128)(2,1)} fusion(f32[896,768]{1,0:T(8,128)S(1)} %copy-done.7, bf16[896,3072]{1,0:T(8,128)(2,1)} %get-tuple-element.143, bf16[3072,768]{1,0:T(8,128)(2,1)} %bitcast.192, f32[768]{0:T(1024)S(1)} %copy-done.29), kind=kOutput, calls=%fused_computation.69 | convolution fusion | flops 4229922816 | bytes 14355456 | tf_op jit(solution)/shard_map/dot_general | solution.py:25
  311.0 35.2 %all-to-all-done.3 = bf16[16,56,768]{2,1,0:T(8,128)(2,1)} async-done(((bf16[16,56,768]{2,1,0:T(8,128)(2,1)}), bf16[16,56,768]{2,1,0:T(8,128)(2,1)}, u32[]{:S(2)}, u32[]{:S(2)}) %all-to-all-start.3) | async-done | bytes 1376288 | tf_op jit(solution)/shard_map/all_to_all | solution.py:440
  354.3 20.5 %shard_map.350 = bf16[896,2304]{1,0:T(8,128)(2,1)} custom-call(bf16[896,2304]{1,0:T(8,128)(2,1)} %add_convert_fusion.1.qkv_ref, bf16[896,768]{1,0:T(8,128)(2,1)} %convolution_convert_fusion.3.mix_g_ref), custom_call_target="tpu_custom_call" | custom-call | flops 3082813440 | bytes 9633792 | tf_op jit(solution)/shard_map/pallas_call | solution.py:156
  374.9 8.6 %fusion.42 = (f32[768]{0:T(1024)S(1)}, f32[896]{0:T(1024)S(1)}, f32[896]{0:T(1024)S(1)}, f32[768]{0:T(1024)S(1)}, f32[896,768]{1,0:T(8,128)}) fusion(f32[896]{0:T(1024)S(1)} %div.52, f32[896]{0:T(1024)S(1)} %rsqrt.36, bf16[16,49,768]{2,1,0:T(8,128)(2,1)S(1)} %copy-done.1, f32[768]{0:T(1024)S(1)} %copy-done.24, bf16[896,2304]{1,0:T(8,128)(2,1)} %shard_map.350, ...), kind=kOutput, calls=%fused_computation.62 | convolution fusion | flops 3177771776 | bytes 11648000 | tf_op jit(solution)/shard_map/dot_general | solution.py:25
  388.0 28.8 %reduce-scatter.2.cloned.1.call-done = bf16[1,192,768]{2,1,0:T(8,128)(2,1)} async-done(((bf16[32,192,768]{2,1,0:T(8,128)(2,1)}), bf16[1,192,768]{2,1,0:T(8,128)(2,1)}) %reduce-scatter.2.cloned.1.call-update) | async-done | bytes 294928 | tf_op jit(solution)/shard_map/reduce_scatter | solution.py:560
  425.7 4.4 convolution_convert_fusion.2
  442.6 92.2 %scatter_sum.1 = (bf16[8,96,768]{2,1,0:T(8,128)(2,1)}, bf16[8,112,768]{2,1,0:T(8,128)(2,1)}) custom-call(bf16[8,4,96,768]{3,2,1,0:T(8,128)(2,1)} %pad_maximum_fusion.2.refs_0_, bf16[8,4,112,768]{3,2,1,0:T(8,128)(2,1)} %pad_maximum_fusion.1.refs_1_), custom_call_target="tpu_custom_call" | custom-call | bytes 300000000 | tf_op jit(solution)/shard_map/scatter_sum/pallas_call | solution.py:405
  (232 shorter events, 121.6 us)
Async XLA Ops:
  7.2 169.4 %all-gather.6.cloned.1.call-start = ((), (), s32[]{:S(2)}) async-start(), calls=%async_computation.7 | async-start | bytes 9732096 | tf_op jit(solution)/shard_map/all_gather | solution.py:443
  13.8 70.0 %copy-start = (bf16[16,49,768]{2,1,0:T(8,128)(2,1)}, bf16[16,49,768]{2,1,0:T(8,128)(2,1)S(1)}, u32[]{:S(2)}) copy-start(bf16[16,49,768]{2,1,0:T(8,128)(2,1)S(1)} %reshape.436) | copy-start | bytes 3612676
  82.3 26.4 %copy-start.18 = (f32[4,1536]{1,0:T(4,128)}, f32[4,1536]{1,0:T(4,128)S(1)}, u32[]{:S(2)}) copy-start(f32[4,1536]{1,0:T(4,128)S(1)} %reshape.470) | copy-start | bytes 73732
  90.0 9.1 %copy-start.38 = (bf16[1,4,8,24,768]{4,3,2,1,0:T(8,128)(2,1)S(1)}, bf16[1,4,8,24,768]{4,3,2,1,0:T(8,128)(2,1)}, u32[]{:S(2)}) copy-start(bf16[1,4,8,24,768]{4,3,2,1,0:T(8,128)(2,1)} %get-tuple-element.31) | copy-start | bytes 3538948
  102.8 39.4 %all-to-all-start = ((bf16[16,56,768]{2,1,0:T(8,128)(2,1)}), bf16[16,56,768]{2,1,0:T(8,128)(2,1)S(1)}, u32[]{:S(2)}, u32[]{:S(2)}) async-start(bf16[16,56,768]{2,1,0:T(8,128)(2,1)} %bitcast.208), calls=%async_computation | async-start | bytes 2752512 | tf_op jit(solution)/shard_map/all_to_all | solution.py:440
  112.7 34.3 %copy-start.20 = (f32[768]{0:T(1024)S(1)}, f32[768]{0:T(1024)}, u32[]{:S(2)}) copy-start(f32[768]{0:T(1024)} %param.27) | copy-start | bytes 9220
  112.7 34.3 %copy-start.27 = (f32[768]{0:T(1024)S(1)}, f32[768]{0:T(1024)}, u32[]{:S(2)}) copy-start(f32[768]{0:T(1024)} %param.28) | copy-start | bytes 9220
  142.2 54.3 %all-to-all-start.2 = ((bf16[16,56,768]{2,1,0:T(8,128)(2,1)}), bf16[16,56,768]{2,1,0:T(8,128)(2,1)S(1)}, u32[]{:S(2)}, u32[]{:S(2)}) async-start(bf16[16,56,768]{2,1,0:T(8,128)(2,1)} %pad.17), calls=%async_computation.2 | async-start | bytes 2752512 | tf_op jit(solution)/shard_map/all_to_all | solution.py:440
  145.9 270.9 %reduce-scatter.2.cloned.1.call-start = ((), (), s32[]{:S(2)}) async-start(), calls=%async_computation.5 | async-start | bytes 9732096 | tf_op jit(solution)/shard_map/reduce_scatter | solution.py:560
  196.6 11.1 %copy-start.6 = (f32[896,768]{1,0:T(8,128)S(1)}, f32[896,768]{1,0:T(8,128)}, u32[]{:S(2)}) copy-start(f32[896,768]{1,0:T(8,128)} %copy-done.4) | copy-start | bytes 8257540
  196.6 11.1 %copy-start.9 = (bf16[8,4,96,768]{3,2,1,0:T(8,128)(2,1)S(1)}, bf16[8,4,96,768]{3,2,1,0:T(8,128)(2,1)}, u32[]{:S(2)}) copy-start(bf16[8,4,96,768]{3,2,1,0:T(8,128)(2,1)} %get-tuple-element.124) | copy-start | bytes 14155780
  207.7 13.1 %slice-start.1 = ((s8[5505024]{0:T(1024)(128)(4,1)}), s8[4194304]{0:T(1024)(128)(4,1)S(1)}, s32[]{:S(2)}) async-start(s8[5505024]{0:T(1024)(128)(4,1)} %bitcast.232), calls=%async_computation.9 | async-start | bytes 8388608
  282.7 63.5 %all-to-all-start.3 = ((bf16[16,56,768]{2,1,0:T(8,128)(2,1)}), bf16[16,56,768]{2,1,0:T(8,128)(2,1)}, u32[]{:S(2)}, u32[]{:S(2)}) async-start(bf16[16,56,768]{2,1,0:T(8,128)(2,1)} %bitcast.31), calls=%async_computation.3 | async-start | bytes 2752512 | tf_op jit(solution)/shard_map/all_to_all | solution.py:440
  311.0 39.7 %copy-start.39 = (bf16[1,4,8,24,768]{4,3,2,1,0:T(8,128)(2,1)S(1)}, bf16[1,4,8,24,768]{4,3,2,1,0:T(8,128)(2,1)}, u32[]{:S(2)}) copy-start(bf16[1,4,8,24,768]{4,3,2,1,0:T(8,128)(2,1)} %get-tuple-element.31) | copy-start | bytes 3538948
  346.2 193.9 %all-to-all-start.1 = ((bf16[16,56,768]{2,1,0:T(8,128)(2,1)}), bf16[16,56,768]{2,1,0:T(8,128)(2,1)}, u32[]{:S(2)}, u32[]{:S(2)}) async-start(bf16[16,56,768]{2,1,0:T(8,128)(2,1)} %bitcast.25), calls=%async_computation.1 | async-start | bytes 2752512 | tf_op jit(solution)/shard_map/all_to_all | solution.py:440
  350.6 207.3 %all-gather.4.cloned.1.call-start = ((), (), s32[]{:S(2)}) async-start(), calls=%async_computation.6 | async-start | bytes 2654208 | tf_op jit(solution)/shard_map/all_gather | solution.py:635
  354.3 20.5 %copy-start.1 = (bf16[16,49,768]{2,1,0:T(8,128)(2,1)S(1)}, bf16[16,49,768]{2,1,0:T(8,128)(2,1)}, u32[]{:S(2)}) copy-start(bf16[16,49,768]{2,1,0:T(8,128)(2,1)} %copy-done) | copy-start | bytes 3612676
  354.3 20.5 %copy-start.24 = (f32[768]{0:T(1024)S(1)}, f32[768]{0:T(1024)}, u32[]{:S(2)}) copy-start(f32[768]{0:T(1024)} %param.21) | copy-start | bytes 9220
  374.8 8.7 %copy-start.19 = (f32[6912]{0:T(1024)S(1)}, f32[6912]{0:T(1024)}, u32[]{:S(2)}) copy-start(f32[6912]{0:T(1024)} %custom-call) | copy-start | bytes 82948
  374.8 10.3 %copy-start.33 = (f32[768]{0:T(1024)S(1)}, f32[768]{0:T(1024)}, u32[]{:S(2)}) copy-start(f32[768]{0:T(1024)} %get-tuple-element.100) | copy-start | bytes 9220
  374.8 10.3 %copy-start.32 = (f32[768]{0:T(1024)S(1)}, f32[768]{0:T(1024)}, u32[]{:S(2)}) copy-start(f32[768]{0:T(1024)} %get-tuple-element.108) | copy-start | bytes 9220
  374.8 10.3 %copy-start.31 = (f32[768]{0:T(1024)S(1)}, f32[768]{0:T(1024)}, u32[]{:S(2)}) copy-start(f32[768]{0:T(1024)} %get-tuple-element.98) | copy-start | bytes 9220
  374.8 10.3 %copy-start.30 = (f32[768]{0:T(1024)S(1)}, f32[768]{0:T(1024)}, u32[]{:S(2)}) copy-start(f32[768]{0:T(1024)} %get-tuple-element.107) | copy-start | bytes 9220
  374.9 10.3 %copy-start.13 = (bf16[896,768]{1,0:T(8,128)(2,1)S(1)}, bf16[896,768]{1,0:T(8,128)(2,1)}, u32[]{:S(2)}) copy-start(bf16[896,768]{1,0:T(8,128)(2,1)} %shard_map.347) | copy-start | bytes 4128772
  (28 other events, 118.9 us)
Sparse Core Ops, SparseCore 0:
  11.4 101.3 all-gather.5
  234.7 182.0 reduce-scatter.1
  418.7 27.9 all-gather.3

commit v4 on v3

--- a/solution.py
+++ b/solution.py
@@ -310,84 +310,112 @@
     lax.fori_loop(0, target.shape[0], step, 0)
 
 
-def scatter_kernel(*refs):
-    packs, outs = refs[0:2], refs[2:4]
-    accs, cores, firsts, seconds, columns = (refs[4 + 2 * i : 6 + 2 * i] for i in range(5))
-    send_sems, recv_sems, local_sems = refs[14:]
+def scatter_kernel(*refs, cuts):
+    count = len(cuts)
+    held = max(c[0] for c in cuts) + 1
+    packs, outs = refs[:held], refs[held : 2 * held]
+    refs = refs[2 * held :]
+    accs, cores, firsts, seconds, columns = (
+        refs[i * count : (i + 1) * count] for i in range(5)
+    )
+    send_sems, recv_sems, local_sems = refs[5 * count :]
     me, z, part = here()
+    near, far = (2, 4), (4, 2)
+
+    def pack_of(s, at):
+        w, low, high = cuts[s]
+        return packs[w].at[at, :, low:high]
+
+    def out_of(s, at):
+        w, low, high = cuts[s]
+        return outs[w].at[at, low:high]
+
     loads = {}
-    for b, mask in enumerate(BLOCKS):
-        for s in (0, 1):
-            loads[s, mask] = pltpu.make_async_copy(
-                packs[s].at[part(mask)], accs[s].at[b], local_sems.at[2 * b + s]
+    for s in range(count):
+        for b, mask in enumerate(BLOCKS):
+            loads[s, b] = pltpu.make_async_copy(
+                pack_of(s, part(mask)), accs[s].at[b], local_sems.at[4 * s + b]
             )
-            loads[s, mask].start()
+            loads[s, b].start()
     greet(part, z)
     copies = Copies(send_sems, recv_sems)
-    first_core = {}
-    for b, mask in enumerate(BLOCKS):
-        for s in (0, 1):
-            first_core[s, mask] = copies.start(
-                packs[s].at[part(mask ^ 1)], cores[s].at[b], plane(part, 1)
-            )
-    near, far = (2, 4), (4, 2)
-    hop = {}
-    for b, mask in enumerate(BLOCKS):
-        for s in (0, 1):
-            loads[s, mask].wait()
-            first_core[s, mask].wait_recv()
-            add_into(accs[s].at[b], cores[s].at[b])
-        for s in (0, 1):
-            if mask & near[s]:
-                slot = 0 if mask == 6 else 1
-                hop[s, slot] = copies.start(
-                    accs[s].at[b], firsts[s].at[slot], plane(part, near[s])
+    first_core, hop, lines, along, relays, ends = {}, {}, {}, {}, {}, []
+    for g in range(count // 2):
+        for b, mask in enumerate(BLOCKS):
+            for s in (2 * g, 2 * g + 1):
+                first_core[s, b] = copies.start(
+                    pack_of(s, part(mask ^ 1)), cores[s].at[b], plane(part, 1)
                 )
-    for s in (0, 1):
-        b = BLOCKS.index(far[s])
-        hop[s, 0].wait_recv()
-        add_into(accs[s].at[b], firsts[s].at[0])
-    for s in (0, 1):
-        b = BLOCKS.index(far[s])
-        hop[s, 2] = copies.start(accs[s].at[b], seconds[s], plane(part, far[s]))
-    for s in (0, 1):
-        hop[s, 1].wait_recv()
-        add_into(accs[s].at[3], firsts[s].at[1])
-    lines = {}
-    for s in (0, 1):
-        hop[s, 2].wait_recv()
-        add_into(accs[s].at[3], seconds[s])
-    for s in (0, 1):
-        for j in (1, 2, 3):
-            to = (z + j) % 4
-            lines[s, j] = copies.start(accs[s].at[3, to], columns[s].at[j - 1], column(to))
-    for s in (0, 1):
-        total = accs[s][3, z].astype(F32)
-        for j in (1, 2, 3):
-            lines[s, j].wait_recv()
-            total = total + columns[s][j - 1].astype(F32)
-        outs[s][me] = total.astype(BF16)
 
     def push(s, mask, to):
         at = part(mask)
-        return copies.start(outs[s].at[at], outs[s].at[at], plane(part, to))
-
-    ends = []
-    along = {}
-    for s in (0, 1):
-        along[s, 2] = push(s, 0, 2)
-        along[s, 4] = push(s, 0, 4)
-        ends.append(push(s, 0, 1))
-    relays = []
-    for s in (0, 1):
-        for mask in (2, 4):
-            along[s, mask].wait_recv()
-            if mask == near[s]:
-                relays.append((s, push(s, mask, far[s])))
-            ends.append(push(s, mask, 1))
-    for s, copy in relays:
-        copy.wait_recv()
-        ends.append(push(s, 6, 1))
+        return copies.start(out_of(s, at), out_of(s, at), plane(part, to))
+
+    def add_cores(pair):
+        for b, mask in enumerate(BLOCKS):
+            for s in pair:
+                loads[s, b].wait()
+                first_core[s, b].wait_recv()
+                add_into(accs[s].at[b], cores[s].at[b])
+            for s in pair:
+                if mask & near[s % 2]:
+                    slot = 0 if mask == 6 else 1
+                    hop[s, slot] = copies.start(
+                        accs[s].at[b], firsts[s].at[slot], plane(part, near[s % 2])
+                    )
+
+    def add_first(pair):
+        for s in pair:
+            hop[s, 0].wait_recv()
+            add_into(accs[s].at[BLOCKS.index(far[s % 2])], firsts[s].at[0])
+        for s in pair:
+            hop[s, 2] = copies.start(
+                accs[s].at[BLOCKS.index(far[s % 2])], seconds[s], plane(part, far[s % 2])
+            )
+
+    def add_second(pair):
+        for s in pair:
+            hop[s, 1].wait_recv()
+            add_into(accs[s].at[3], firsts[s].at[1])
+        for s in pair:
+            hop[s, 2].wait_recv()
+            add_into(accs[s].at[3], seconds[s])
+        for s in pair:
+            for j in (1, 2, 3):
+                to = (z + j) % 4
+                lines[s, j] = copies.start(accs[s].at[3, to], columns[s].at[j - 1], column(to))
+
+    def add_columns(pair):
+        for s in pair:
+            total = accs[s][3, z].astype(F32)
+            for j in (1, 2, 3):
+                lines[s, j].wait_recv()
+                total = total + columns[s][j - 1].astype(F32)
+            w, low, high = cuts[s]
+            outs[w][me, low:high] = total.astype(BF16)
+        for s in pair:
+            along[s, 2] = push(s, 0, 2)
+            along[s, 4] = push(s, 0, 4)
+            ends.append(push(s, 0, 1))
+
+    def relay(pair):
+        for s in pair:
+            for mask in (2, 4):
+                along[s, mask].wait_recv()
+                if mask == near[s % 2]:
+                    relays[s] = push(s, mask, far[s % 2])
+                ends.append(push(s, mask, 1))
+
+    def finish(pair):
+        for s in pair:
+            relays[s].wait_recv()
+            ends.append(push(s, 6, 1))
+
+    stages = (add_cores, add_first, add_second, add_columns, relay, finish)
+    for step in range(count // 2 + len(stages) - 1):
+        for i, stage in enumerate(stages):
+            if 0 <= step - i < count // 2:
+                stage((2 * (step - i), 2 * (step - i) + 1))
     for copy in ends:
         copy.wait_recv()
     for copy in copies.made:
@@ -395,23 +423,27 @@
 
 
 def scatter_sum(packs):
-    count = 2 * (4 + 3 + 3 + 3 + 4)
+    cuts = []
+    for w, pack in enumerate(packs):
+        rows = pack.shape[2]
+        half = rows // 32 * 16
+        cuts += [(w, 0, half), (w, half, rows)]
+    width = packs[0].shape[3]
     anywhere = pl.BlockSpec(memory_space=pl.ANY)
-    rows = [p.shape[2:] for p in packs]
 
     def scratch(*lead):
-        return [pltpu.VMEM(lead + r, BF16) for r in rows]
+        return [pltpu.VMEM(lead + (high - low, width), BF16) for _, low, high in cuts]
 
     return pl.pallas_call(
-        scatter_kernel,
-        out_shape=[jax.ShapeDtypeStruct((8,) + r, BF16) for r in rows],
-        in_specs=[anywhere] * 2,
-        out_specs=[pl.BlockSpec(memory_space=pltpu.VMEM)] * 2,
+        functools.partial(scatter_kernel, cuts=tuple(cuts)),
+        out_shape=[jax.ShapeDtypeStruct((8,) + p.shape[2:], BF16) for p in packs],
+        in_specs=[anywhere] * len(packs),
+        out_specs=[pl.BlockSpec(memory_space=pltpu.VMEM)] * len(packs),
         scratch_shapes=scratch(4, 4) + scratch(4, 4) + scratch(2, 4) + scratch(4) + scratch(3)
         + [
-            pltpu.SemaphoreType.DMA((count,)),
-            pltpu.SemaphoreType.DMA((count,)),
-            pltpu.SemaphoreType.DMA((8,)),
+            pltpu.SemaphoreType.DMA((17 * len(cuts),)),
+            pltpu.SemaphoreType.DMA((17 * len(cuts),)),
+            pltpu.SemaphoreType.DMA((4 * len(cuts),)),
         ],
         compiler_params=pltpu.CompilerParams(collective_id=1, has_side_effects=True),
         cost_estimate=pl.CostEstimate(flops=0, bytes_accessed=300000000, transcendentals=0),
@@ -523,7 +555,7 @@
         def exchange(x):
             return regroup(x.reshape(TIMES, SLOT, width)).reshape(slots, width)
 
-        cot = exchange(pad_rows(cotangent))
+        cot_slots = pad_rows(cotangent)
 
         resid = pad_rows(tokens).astype(F32)
         space_n, space_r = norm_stats(resid)
@@ -532,7 +564,10 @@
         space_mix = attention_call(attend_kernel, [space_qkv], width, False)
         after_space = resid + dot(space_mix, space_out_w, NN) + space_outbias.astype(F32)
 
-        after_space_p = exchange(after_space.astype(BF16)).astype(F32)
+        moved = exchange(after_space.astype(BF16))
+        moved, up_w, down_w, cot_slots = lax.optimization_barrier((moved, up_w, down_w, cot_slots))
+        cot = exchange(cot_slots)
+        after_space_p = moved.astype(F32)
         tn_p, tr_p = norm_stats(after_space_p)
         time_in = (tn_p * time_gain + time_shift).astype(BF16)
         time_qkv = (dot(time_in, time_in_w, NT) + time_b).astype(BF16)
@@ -636,7 +671,7 @@
 
         if direct:
             time_all, space_all = scatter_sum(
-                [x.reshape((dp, tp) + x.shape[1:]) for x in (time_pack, space_pack)]
+                [x.reshape((dp, tp, -1, width)) for x in (time_pack, space_pack)]
             )
         else:
             both = spread(scatter(jnp.concatenate([time_pack, space_pack], axis=1)))

time: 580 us -> 546 us (0.941)
  waiting for transfers between devices: 93.6 us -> 59.4 us
  matrix products: 108 us -> 120 us
  Pallas kernels: 231 us -> 224 us
  local copies, waits for them, and re-layouts: 57.4 us -> 51.4 us
    all_to_all x4, waiting for transfers between devices: 64.7 us -> 42 us  [regroup(): lax.all_to_all(x, names['time'], split_axis=0, concat_axis=0, tiled=True)]
    dot_general x18, matrix products: 108 us -> 120 us  [dot(): return lax.dot_general(a, b, dims, preferred_element_type=F32)]
    reduce_scatter x1, waiting for transfers between devices: 28.8 us -> 17.3 us  [scatter(): return lax.psum_scatter(grad, every, scatter_dimension=0, tiled=False)]
    pallas_call x1, Pallas kernels: 92.2 us -> 86.3 us  [scatter_sum(): pl.pallas_call(functools.partial(scatter_kernel, cuts=tuple(cuts)), out_s...]
    unnamed x101 -> x59, local copies, waits for them, and re-layouts: 12.8 us -> 13.1 us
  transfers between devices with their start and end apart: 7 -> 7, of which waited for: 3 -> 3; matrix products, arithmetic and copies ran while one was open for 28% -> 30% of each run, Pallas kernels for 40% -> 42%
where the time goes in v4:
time: 546 us; the launch traced here: 537 us
  Pallas kernels  224 us (41%)
  matrix products  120 us (22%)
  waiting for transfers between devices  59.4 us (11%)
  local copies, waits for them, and re-layouts  51.4 us (9%)
  other arithmetic  43.7 us (8%)
  starting transfers between devices  22.9 us (4%)
  between operations  14.9 us (3%)
    dot_general x18, matrix products, dot(): return lax.dot_general(a, b, dims, preferred_element_type=F32)  120 us
    pallas_call x1, Pallas kernels, scatter_sum(): pl.pallas_call(functools.partial(scatter_kernel, cuts=tuple(cuts)), out_s...  86.3 us
    pallas_call x4, Pallas kernels, attention_call(): pl.pallas_call(functools.partial(kernel, temporal=temporal), grid=grid, i...  71.5 us
    pallas_call x1, Pallas kernels, gather_weights(): pl.pallas_call(functools.partial(gather_kernel, count=count), out_shape=[...  66.7 us
    all_to_all x4, waiting for transfers between devices, regroup(): lax.all_to_all(x, names['time'], split_axis=0, concat_axis=0, tiled=True)  42 us
    all_to_all x4, starting transfers between devices, regroup(): lax.all_to_all(x, names['time'], split_axis=0, concat_axis=0, tiled=True)  22.6 us
    reduce_scatter x1, waiting for transfers between devices, scatter(): return lax.psum_scatter(grad, every, scatter_dimension=0, tiled=False)  17.3 us
    unnamed x59, local copies, waits for them, and re-layouts  13.1 us
  transfers between devices with their start and end apart: 7, of which 3 were waited for; matrix products, arithmetic and copies ran while one was open for 30% of the time, Pallas kernels for 42%

profile of v4, /device:TPU:0, one launch (start us, length us, event | category | flops | bytes accessed | tf_op | source)
XLA Modules:
  0.0 536.7 jit_solution(18161438703250194707)
XLA Ops:
  14.4 66.7 %gather_weights.1 = (bf16[3,4,8,24,768]{4,3,2,1,0:T(8,128)(2,1)}, bf16[1,4,8,24,768]{4,3,2,1,0:T(8,128)(2,1)}, bf16[3,4,8,24,768]{4,3,2,1,0:T(8,128)(2,1)}, bf16...) custom-call(bf16[3,8,24,768]{3,2,1,0:T(8,128)(2,1)} %bitcast.194, bf16[1,8,24,768]{3,2,1,0:T(8,128)(2,1)} %bitcast.196, ...), custom_call_target="tpu_custom_call" | custom-call | bytes 98304000 | tf_op jit(solution)/shard_map/gather_weights/pallas_call | solution.py:282
  89.9 9.0 %shard_map.347 = bf16[896,768]{1,0:T(8,128)(2,1)} custom-call(bf16[896,2304]{1,0:T(8,128)(2,1)} %add_convert_fusion.1.qkv_ref), custom_call_target="tpu_custom_call" | custom-call | flops 1233125376 | bytes 5505024 | tf_op jit(solution)/shard_map/pallas_call | solution.py:156
  103.0 5.9 %all-to-all-start = ((bf16[16,56,768]{2,1,0:T(8,128)(2,1)}), bf16[16,56,768]{2,1,0:T(8,128)(2,1)S(1)}, u32[]{:S(2)}, u32[]{:S(2)}) async-start(bf16[16,56,768]{2,1,0:T(8,128)(2,1)} %bitcast.190), calls=%async_computation | async-start | bytes 2752512 | tf_op jit(solution)/shard_map/all_to_all | solution.py:472
  116.4 8.2 %fusion.50 = (bf16[8,4,96,768]{3,2,1,0:T(8,128)(2,1)}, bf16[8,4,96,768]{3,2,1,0:T(8,128)(2,1)}) fusion(bf16[8,4,192,768]{3,2,1,0:T(8,128)(2,1)} %bitcast.167), kind=kLoop, calls=%fused_computation.137 | loop fusion | bytes 18874368 | tf_op jit(solution)/shard_map/slice | solution.py:535
  124.6 17.8 %all-to-all-done = bf16[16,56,768]{2,1,0:T(8,128)(2,1)S(1)} async-done(((bf16[16,56,768]{2,1,0:T(8,128)(2,1)}), bf16[16,56,768]{2,1,0:T(8,128)(2,1)S(1)}, u32[]{:S(2)}, u32[]{:S(2)}) %all-to-all-start) | async-done | bytes 1376288 | tf_op jit(solution)/shard_map/all_to_all | solution.py:472
  147.9 7.3 %add_convert_fusion = bf16[896,2304]{1,0:T(8,128)(2,1)} fusion(bf16[2304,768]{1,0:T(8,128)(2,1)} %bitcast.208, f32[2304]{0:T(1024)S(1)} %get-tuple-element.147, bf16[896,768]{1,0:T(8,128)(2,1)S(1)} %bitcast.155, f32[768]{0:T(1024)S(1)} %copy-done.18, f32[768]{0:T(1024)S(1)} %copy-done.12, f32[896]{0:T(1024)S(1)} %add_rsqrt_fusion.2, ...), kind=kOutput, calls=%fused_computation.10 | convolution fusion | flops 3179151360 | bytes 9066496 | tf_op jit(solution)/shard_map/dot_general | solution.py:25
  155.3 18.3 %shard_map.348 = bf16[16,56,768]{2,1,0:T(8,128)(2,1)} custom-call(bf16[16,56,2304]{2,1,0:T(8,128)(2,1)} %bitcast.162), custom_call_target="tpu_custom_call" | custom-call | flops 704643072 | bytes 5505024 | tf_op jit(solution)/shard_map/pallas_call | solution.py:156
  178.4 13.4 %multiply_convert_fusion = (bf16[896,3072]{1,0:T(8,128)(2,1)}, f32[896,3072]{1,0:T(8,128)}) fusion(f32[3072]{0:T(1024)S(1)} %add.164, bf16[3072,768]{1,0:T(8,128)(2,1)S(1)} %bitcast.176, f32[896,768]{1,0:T(8,128)S(1)} %get-tuple-element.150, f32[768]{0:T(1024)S(1)} %copy-done.17, f32[768]{0:T(1024)S(1)} %copy-done.11, f32[896]{0:T(1024)S(1)} %add_rsqrt_fusion.1, ...), kind=kOutput, calls=%fused_computation.7 | convolution fusion | flops 4247814144 | bytes 24011776 | tf_op jit(solution)/shard_map/dot_general | solution.py:25
  191.8 11.1 %fusion.57 = (bf16[3072]{0:T(1024)(128)(2,1)S(1)}, bf16[896,3072]{1,0:T(8,128)(2,1)S(1)}) fusion(f32[896,3072]{1,0:T(8,128)} %get-tuple-element.152, f32[3072]{0:T(1024)S(1)} %add.164, bf16[896,768]{1,0:T(8,128)(2,1)} %bitcast.27, bf16[3072,768]{1,0:T(8,128)(2,1)} %bitcast.171), kind=kOutput, calls=%fused_computation.144 | convolution fusion | flops 4260885504 | bytes 22628352 | tf_op jit(solution)/shard_map/dot_general | solution.py:25
  203.0 8.8 %multiply_reduce_fusion = (f32[768]{0:T(1024)S(1)}, f32[896]{0:T(1024)S(1)}, f32[896]{0:T(1024)S(1)}, f32[768]{0:T(1024)S(1)}, f32[896,768]{1,0:T(8,128)}) fusion(f32[896,768]{1,0:T(8,128)S(1)} %copy-done.2, f32[896]{0:T(1024)S(1)} %add_rsqrt_fusion.1, f32[896]{0:T(1024)S(1)} %broadcast_multiply_fusion.7, f32[768]{0:T(1024)S(1)} %copy-done.11, ...), kind=kOutput, calls=%fused_computation.62 | convolution fusion | flops 4234048256 | bytes 15752192 | tf_op jit(solution)/shard_map/dot_general | solution.py:25
  211.8 6.5 %convolution_convert_fusion.1 = bf16[3072,768]{1,0:T(8,128)(2,1)S(1)} fusion(bf16[896,3072]{1,0:T(8,128)(2,1)S(1)} %get-tuple-element.157, f32[896,768]{1,0:T(8,128)S(1)} %copy-done.2, f32[768]{0:T(1024)S(1)} %copy-done.17, f32[768]{0:T(1024)S(1)} %copy-done.11, f32[896]{0:T(1024)S(1)} %add_rsqrt_fusion.1, f32[896]{0:T(1024)S(1)} %broadcast_multiply_fusion.7), kind=kOutput, calls=%fused_computation.14 | convolution fusion | flops 4233658368 | bytes 12989440 | tf_op jit(solution)/shard_map/dot_general | solution.py:25
  218.4 6.8 %convolution_convert_fusion = bf16[3072,768]{1,0:T(8,128)(2,1)S(1)} fusion(bf16[896,3072]{1,0:T(8,128)(2,1)S(1)} %bitcast.215, bf16[896,768]{1,0:T(8,128)(2,1)} %bitcast.27), kind=kOutput, calls=%fused_computation.13 | convolution fusion | flops 4230217728 | bytes 11599872 | tf_op jit(solution)/shard_map/dot_general | solution.py:25
  234.4 10.3 %add_convert_fusion.2 = bf16[896,768]{1,0:T(8,128)(2,1)} fusion(f32[896,768]{1,0:T(8,128)} %copy-done.1, bf16[896,3072]{1,0:T(8,128)(2,1)} %get-tuple-element.151, bf16[3072,768]{1,0:T(8,128)(2,1)} %bitcast.172, f32[768]{0:T(1024)S(1)} %convert_element_type.205), kind=kOutput, calls=%fused_computation.67 | convolution fusion | flops 4229922816 | bytes 14355456 | tf_op jit(solution)/shard_map/dot_general | solution.py:25
  244.7 6.1 %all-to-all-start.1 = ((bf16[16,56,768]{2,1,0:T(8,128)(2,1)}), bf16[16,56,768]{2,1,0:T(8,128)(2,1)}, u32[]{:S(2)}, u32[]{:S(2)}) async-start(bf16[16,56,768]{2,1,0:T(8,128)(2,1)} %bitcast.189), calls=%async_computation.1 | async-start | bytes 2752512 | tf_op jit(solution)/shard_map/all_to_all | solution.py:472
  255.5 23.8 %shard_map.349 = bf16[16,56,2304]{2,1,0:T(8,128)(2,1)} custom-call(bf16[16,56,2304]{2,1,0:T(8,128)(2,1)} %bitcast.163, bf16[16,56,768]{2,1,0:T(8,128)(2,1)} %bitcast.186), custom_call_target="tpu_custom_call" | custom-call | flops 1761607680 | bytes 9633792 | tf_op jit(solution)/shard_map/pallas_call | solution.py:156
  279.2 7.3 %fusion.19 = (f32[768]{0:T(1024)S(1)}, f32[896]{0:T(1024)S(1)}, f32[896]{0:T(1024)S(1)}, f32[768]{0:T(1024)S(1)}, f32[896,768]{1,0:T(8,128)S(1)}) fusion(bf16[896,768]{1,0:T(8,128)(2,1)S(1)} %bitcast.157, f32[896]{0:T(1024)S(1)} %add_rsqrt_fusion.2, f32[896]{0:T(1024)S(1)} %broadcast_multiply_fusion.8, f32[768]{0:T(1024)S(1)} %copy-done.12, ...), kind=kOutput, calls=%fused_computation.34 | convolution fusion | flops 3177771776 | bytes 11820032 | tf_op jit(solution)/shard_map/dot_general | solution.py:25
  288.6 6.2 %all-to-all-start.3 = ((bf16[16,56,768]{2,1,0:T(8,128)(2,1)}), bf16[16,56,768]{2,1,0:T(8,128)(2,1)}, u32[]{:S(2)}, u32[]{:S(2)}) async-start(bf16[16,56,768]{2,1,0:T(8,128)(2,1)} %bitcast.168), calls=%async_computation.3 | async-start | bytes 2752512 | tf_op jit(solution)/shard_map/all_to_all | solution.py:472
  308.3 7.3 %convolution_convert_fusion.3 = bf16[2304,768]{1,0:T(8,128)(2,1)S(1)} fusion(bf16[896,2304]{1,0:T(8,128)(2,1)} %bitcast.161, bf16[896,768]{1,0:T(8,128)(2,1)S(1)} %bitcast.159, f32[768]{0:T(1024)S(1)} %copy-done.18, f32[768]{0:T(1024)S(1)} %copy-done.12, f32[896]{0:T(1024)S(1)} %add_rsqrt_fusion.2, f32[896]{0:T(1024)S(1)} %broadcast_multiply_fusion.8), kind=kOutput, calls=%fused_computation.16 | convolution fusion | flops 3176792064 | bytes 9057280 | tf_op jit(solution)/shard_map/dot_general | solution.py:25
  320.4 24.2 %all-to-all-done.3 = bf16[16,56,768]{2,1,0:T(8,128)(2,1)} async-done(((bf16[16,56,768]{2,1,0:T(8,128)(2,1)}), bf16[16,56,768]{2,1,0:T(8,128)(2,1)}, u32[]{:S(2)}, u32[]{:S(2)}) %all-to-all-start.3) | async-done | bytes 1376288 | tf_op jit(solution)/shard_map/all_to_all | solution.py:472
  348.3 20.3 %shard_map.350 = bf16[896,2304]{1,0:T(8,128)(2,1)} custom-call(bf16[896,2304]{1,0:T(8,128)(2,1)} %add_convert_fusion.1.qkv_ref, bf16[896,768]{1,0:T(8,128)(2,1)} %convolution_convert_fusion.4.mix_g_ref), custom_call_target="tpu_custom_call" | custom-call | flops 3082813440 | bytes 9633792 | tf_op jit(solution)/shard_map/pallas_call | solution.py:156
  368.7 8.7 %fusion.41 = (f32[768]{0:T(1024)S(1)}, f32[896]{0:T(1024)S(1)}, f32[896]{0:T(1024)S(1)}, f32[768]{0:T(1024)S(1)}, f32[896,768]{1,0:T(8,128)}) fusion(f32[896]{0:T(1024)S(1)} %div.49, f32[896]{0:T(1024)S(1)} %rsqrt.31, bf16[16,49,768]{2,1,0:T(8,128)(2,1)S(1)} %reshape.382, f32[768]{0:T(1024)S(1)} %copy-done.10, bf16[896,2304]{1,0:T(8,128)(2,1)} %shard_map.350, ...), kind=kOutput, calls=%fused_computation.60 | convolution fusion | flops 3177771776 | bytes 11648000 | tf_op jit(solution)/shard_map/dot_general | solution.py:25
  382.9 17.3 %reduce-scatter.2.cloned.1.call-done = bf16[1,192,768]{2,1,0:T(8,128)(2,1)} async-done(((bf16[32,192,768]{2,1,0:T(8,128)(2,1)}), bf16[1,192,768]{2,1,0:T(8,128)(2,1)}) %reduce-scatter.2.cloned.1.call-update) | async-done | bytes 294928 | tf_op jit(solution)/shard_map/reduce_scatter | solution.py:595
  415.5 5.2 pad_maximum_fusion.1.refs_1_
  420.7 86.3 %scatter_sum.1 = (bf16[8,96,768]{2,1,0:T(8,128)(2,1)}, bf16[8,112,768]{2,1,0:T(8,128)(2,1)}) custom-call(bf16[8,4,96,768]{3,2,1,0:T(8,128)(2,1)} %pad_maximum_fusion.2.refs_0_, bf16[8,4,112,768]{3,2,1,0:T(8,128)(2,1)} %pad_maximum_fusion.1.refs_1_), custom_call_target="tpu_custom_call" | custom-call | bytes 300000000 | tf_op jit(solution)/shard_map/scatter_sum/pallas_call | solution.py:437
  (188 shorter events, 118.7 us)
Async XLA Ops:
  7.2 109.2 %all-gather.6.cloned.1.call-start = ((), (), s32[]{:S(2)}) async-start(), calls=%async_computation.7 | async-start | bytes 9732096 | tf_op jit(solution)/shard_map/all_gather | solution.py:475
  82.2 26.7 %copy-start.7 = (f32[4,1536]{1,0:T(4,128)}, f32[4,1536]{1,0:T(4,128)S(1)}, u32[]{:S(2)}) copy-start(f32[4,1536]{1,0:T(4,128)S(1)} %reshape.419) | copy-start | bytes 73732
  82.9 2.0 copy-start.15
  103.0 5.9 %copy-start.13 = (bf16[768]{0:T(1024)(128)(2,1)S(1)}, bf16[768]{0:T(1024)(128)(2,1)}, u32[]{:S(2)}) copy-start(bf16[768]{0:T(1024)(128)(2,1)} %param.32) | copy-start | bytes 4612
  103.0 39.4 %all-to-all-start = ((bf16[16,56,768]{2,1,0:T(8,128)(2,1)}), bf16[16,56,768]{2,1,0:T(8,128)(2,1)S(1)}, u32[]{:S(2)}, u32[]{:S(2)}) async-start(bf16[16,56,768]{2,1,0:T(8,128)(2,1)} %bitcast.190), calls=%async_computation | async-start | bytes 2752512 | tf_op jit(solution)/shard_map/all_to_all | solution.py:472
  111.4 4.8 slice-start.2
  142.4 5.5 %copy-start.12 = (f32[768]{0:T(1024)S(1)}, f32[768]{0:T(1024)}, u32[]{:S(2)}) copy-start(f32[768]{0:T(1024)} %param.27) | copy-start | bytes 9220
  142.4 5.5 %copy-start.18 = (f32[768]{0:T(1024)S(1)}, f32[768]{0:T(1024)}, u32[]{:S(2)}) copy-start(f32[768]{0:T(1024)} %param.28) | copy-start | bytes 9220
  143.2 48.6 %all-to-all-start.2 = ((bf16[16,56,768]{2,1,0:T(8,128)(2,1)}), bf16[16,56,768]{2,1,0:T(8,128)(2,1)}, u32[]{:S(2)}, u32[]{:S(2)}) async-start(bf16[16,56,768]{2,1,0:T(8,128)(2,1)} %pad.17), calls=%async_computation.2 | async-start | bytes 2752512 | tf_op jit(solution)/shard_map/all_to_all | solution.py:472
  147.7 252.5 %reduce-scatter.2.cloned.1.call-start = ((), (), s32[]{:S(2)}) async-start(), calls=%async_computation.5 | async-start | bytes 9732096 | tf_op jit(solution)/shard_map/reduce_scatter | solution.py:595
  173.6 4.8 slice-start
  173.6 4.8 slice-start.1
  191.8 11.1 %copy-start.2 = (f32[896,768]{1,0:T(8,128)S(1)}, f32[896,768]{1,0:T(8,128)}, u32[]{:S(2)}) copy-start(f32[896,768]{1,0:T(8,128)} %copy-done.1) | copy-start | bytes 8257540
  203.0 15.4 %slice-start.3 = ((s8[5505024]{0:T(1024)(128)(4,1)}), s8[4194304]{0:T(1024)(128)(4,1)S(1)}, s32[]{:S(2)}) async-start(s8[5505024]{0:T(1024)(128)(4,1)} %bitcast.214), calls=%async_computation.11 | async-start | bytes 8388608
  211.8 6.5 %slice-start.4 = ((s8[5505024]{0:T(1024)(128)(4,1)}), s8[1310720]{0:T(1024)(128)(4,1)S(1)}, s32[]{:S(2)}) async-start(s8[5505024]{0:T(1024)(128)(4,1)} %bitcast.214), calls=%async_computation.12 | async-start | bytes 2621440
  244.7 43.9 %all-to-all-start.1 = ((bf16[16,56,768]{2,1,0:T(8,128)(2,1)}), bf16[16,56,768]{2,1,0:T(8,128)(2,1)}, u32[]{:S(2)}, u32[]{:S(2)}) async-start(bf16[16,56,768]{2,1,0:T(8,128)(2,1)} %bitcast.189), calls=%async_computation.1 | async-start | bytes 2752512 | tf_op jit(solution)/shard_map/all_to_all | solution.py:472
  279.2 7.3 %copy-start = (f32[896,768]{1,0:T(8,128)S(1)}, f32[896,768]{1,0:T(8,128)}, u32[]{:S(2)}) copy-start(f32[896,768]{1,0:T(8,128)} %multiply_add_fusion) | copy-start | bytes 8257540
  288.6 56.0 %all-to-all-start.3 = ((bf16[16,56,768]{2,1,0:T(8,128)(2,1)}), bf16[16,56,768]{2,1,0:T(8,128)(2,1)}, u32[]{:S(2)}, u32[]{:S(2)}) async-start(bf16[16,56,768]{2,1,0:T(8,128)(2,1)} %bitcast.168), calls=%async_computation.3 | async-start | bytes 2752512 | tf_op jit(solution)/shard_map/all_to_all | solution.py:472
  294.8 229.8 %all-gather.4.cloned.1.call-start = ((), (), s32[]{:S(2)}) async-start(), calls=%async_computation.6 | async-start | bytes 2654208 | tf_op jit(solution)/shard_map/all_gather | solution.py:670
  317.6 27.1 %copy-start.16 = (bf16[1,4,8,24,768]{4,3,2,1,0:T(8,128)(2,1)S(1)}, bf16[1,4,8,24,768]{4,3,2,1,0:T(8,128)(2,1)}, u32[]{:S(2)}) copy-start(bf16[1,4,8,24,768]{4,3,2,1,0:T(8,128)(2,1)} %get-tuple-element.35) | copy-start | bytes 3538948
  368.7 10.4 %copy-start.5 = (bf16[896,768]{1,0:T(8,128)(2,1)S(1)}, bf16[896,768]{1,0:T(8,128)(2,1)}, u32[]{:S(2)}) copy-start(bf16[896,768]{1,0:T(8,128)(2,1)} %shard_map.347) | copy-start | bytes 4128772
  400.2 4.4 copy-start.9
  404.6 4.1 copy-start.4
  507.0 3.3 copy-start.6
  (7 other events, 9.2 us)
Sparse Core Ops, SparseCore 0:
  11.4 101.3 all-gather.5
  233.9 166.2 reduce-scatter.1
  402.1 29.7 all-gather.3

commit v5 on v4

--- a/solution.py
+++ b/solution.py
@@ -11,6 +11,7 @@
 PATCH = 196
 TIMES = 16
 SLOT = 56
+UNROLL = 6
 EPSILON = 1e-06
 ROOT_HALF = 0.7071067811865476
 INV_ROOT_TAU = 0.3989422804014327
@@ -63,34 +64,41 @@
 
 
 def softmax_of(q_one, k_pair, allowed):
-    scores = dot(q_one, k_pair, NT) * (HS ** -0.5)
-    scores = jnp.where(allowed, scores, -1e30)
+    scores = jnp.where(allowed, dot(q_one, k_pair, NT), -1e30)
     top = jnp.max(scores, axis=-1, keepdims=True)
     weights = jnp.exp(scores - top)
-    return weights / jnp.sum(weights, axis=-1, keepdims=True)
+    return weights * (1.0 / jnp.sum(weights, axis=-1, keepdims=True))
 
 
 def rows_of(ref, start, temporal):
     if temporal:
-        block = ref[:, :, start : start + 2 * HS].astype(F32)
+        block = ref[:, :, pl.ds(start, 2 * HS)].astype(F32)
         return block.reshape(-1, 2 * HS).astype(BF16)
-    return ref[:, start : start + 2 * HS]
+    return ref[:, pl.ds(start, 2 * HS)]
 
 
 def put_rows(ref, start, value, temporal):
     if temporal:
-        ref[:, :, start : start + 2 * HS] = value.reshape(TIMES, 8, 2 * HS).astype(BF16)
+        ref[:, :, pl.ds(start, 2 * HS)] = value.reshape(TIMES, 8, 2 * HS).astype(BF16)
     else:
-        ref[:, start : start + 2 * HS] = value.astype(BF16)
+        ref[:, pl.ds(start, 2 * HS)] = value.astype(BF16)
+
+
+def over_pairs(width, body):
+    def step(pair, carry):
+        body(pl.multiple_of(pair * 2 * HS, 2 * HS))
+        return carry
+
+    lax.fori_loop(0, width // (2 * HS), step, 0, unroll=UNROLL)
 
 
 def attend_kernel(qkv_ref, mix_ref, *, temporal):
     width = mix_ref.shape[-1]
     rows = TIMES * 8 if temporal else mix_ref.shape[0]
     allowed = same_sequence(rows, temporal)
-    for pair in range(width // (2 * HS)):
-        at = pair * 2 * HS
-        q = rows_of(qkv_ref, at, temporal)
+
+    def one_pair(at):
+        q = rows_of(qkv_ref, at, temporal) * jnp.asarray(HS ** -0.5, BF16)
         k = rows_of(qkv_ref, width + at, temporal)
         v = rows_of(qkv_ref, 2 * width + at, temporal)
         mixed = None
@@ -101,15 +109,17 @@
             mixed = part if mixed is None else mixed + part
         put_rows(mix_ref, at, mixed, temporal)
 
+    over_pairs(width, one_pair)
+
 
 def attend_back_kernel(qkv_ref, mix_g_ref, qkv_g_ref, *, temporal):
     width = mix_g_ref.shape[-1]
     rows = TIMES * 8 if temporal else mix_g_ref.shape[0]
     allowed = same_sequence(rows, temporal)
     scale = HS ** -0.5
-    for pair in range(width // (2 * HS)):
-        at = pair * 2 * HS
-        q = rows_of(qkv_ref, at, temporal)
+
+    def one_pair(at):
+        q = rows_of(qkv_ref, at, temporal) * jnp.asarray(HS ** -0.5, BF16)
         k = rows_of(qkv_ref, width + at, temporal)
         v = rows_of(qkv_ref, 2 * width + at, temporal)
         g = rows_of(mix_g_ref, at, temporal)
@@ -128,8 +138,10 @@
             )
             total = [p if t is None else t + p for t, p in zip(total, parts)]
         put_rows(qkv_g_ref, at, total[0] * scale, temporal)
-        put_rows(qkv_g_ref, width + at, total[1] * scale, temporal)
+        put_rows(qkv_g_ref, width + at, total[1], temporal)
         put_rows(qkv_g_ref, 2 * width + at, total[2], temporal)
+
+    over_pairs(width, one_pair)
 
 
 def attention_call(kernel, operands, out_width, temporal):
@@ -634,6 +646,9 @@
 
         high = exchange(after_space_g_p.astype(BF16))
         time_pack, time_sums = attention_weights(time_branch, time_in, time_mix, time_qkv_g)
+        high, time_pack, time_sums, layer_out = lax.optimization_barrier(
+            (high, time_pack, time_sums, layer_out)
+        )
         after_space_g = high.astype(F32)
 
         space_in_g, space_qkv_g, space_outbias_g = attention_back(
@@ -669,6 +684,7 @@
         def spread(part):
             return lax.all_gather(part, names["dp"], axis=0, tiled=False)
 
+        feed_part, space_pack = lax.optimization_barrier((feed_part, space_pack))
         if direct:
             time_all, space_all = scatter_sum(
                 [x.reshape((dp, tp, -1, width)) for x in (time_pack, space_pack)]

time: 546 us -> 533 us (0.976)
  waiting for transfers between devices: 59.4 us -> 49 us
    reduce_scatter x1, waiting for transfers between devices: 17.3 us -> 0.01 us  [scatter(): return lax.psum_scatter(grad, every, scatter_dimension=0, tiled=False)]
    all_to_all x4, waiting for transfers between devices: 42 us -> 48.9 us  [regroup(): lax.all_to_all(x, names['time'], split_axis=0, concat_axis=0, tiled=True)]
    unnamed x59 -> x67, local copies, waits for them, and re-layouts: 13.1 us -> 10.8 us
  transfers between devices with their start and end apart: 7 -> 7, of which waited for: 3 -> 3; matrix products, arithmetic and copies ran while one was open for 30% -> 30% of each run, Pallas kernels for 42% -> 44%
where the time goes in v5:
time: 533 us; the launch traced here: 523 us
  Pallas kernels  229 us (43%)
  matrix products  118 us (22%)
  local copies, waits for them, and re-layouts  50.2 us (9%)
  waiting for transfers between devices  49 us (9%)
  other arithmetic  40.2 us (8%)
  starting transfers between devices  22.4 us (4%)
  between operations  14.9 us (3%)
    dot_general x18, matrix products, dot(): return lax.dot_general(a, b, dims, preferred_element_type=F32)  118 us
    pallas_call x1, Pallas kernels, scatter_sum(): pl.pallas_call(functools.partial(scatter_kernel, cuts=tuple(cuts)), out_s...  90.5 us
    pallas_call x4, Pallas kernels, attention_call(): pl.pallas_call(functools.partial(kernel, temporal=temporal), grid=grid, i...  71.7 us
    pallas_call x1, Pallas kernels, gather_weights(): pl.pallas_call(functools.partial(gather_kernel, count=count), out_shape=[...  66.7 us
    all_to_all x4, waiting for transfers between devices, regroup(): lax.all_to_all(x, names['time'], split_axis=0, concat_axis=0, tiled=True)  48.9 us
    all_to_all x4, starting transfers between devices, regroup(): lax.all_to_all(x, names['time'], split_axis=0, concat_axis=0, tiled=True)  22 us
    unnamed x67, local copies, waits for them, and re-layouts  10.8 us
  transfers between devices with their start and end apart: 7, of which 3 were waited for; matrix products, arithmetic and copies ran while one was open for 30% of the time, Pallas kernels for 44%

profile of v5, /device:TPU:0, one launch (start us, length us, event | category | flops | bytes accessed | tf_op | source)
XLA Modules:
  0.0 523.4 jit_solution(5351918217618552176)
XLA Ops:
  14.5 66.7 %gather_weights.1 = (bf16[3,4,8,24,768]{4,3,2,1,0:T(8,128)(2,1)}, bf16[1,4,8,24,768]{4,3,2,1,0:T(8,128)(2,1)}, bf16[3,4,8,24,768]{4,3,2,1,0:T(8,128)(2,1)}, bf16...) custom-call(bf16[3,8,24,768]{3,2,1,0:T(8,128)(2,1)} %bitcast.199, bf16[1,8,24,768]{3,2,1,0:T(8,128)(2,1)} %bitcast.201, ...), custom_call_target="tpu_custom_call" | custom-call | bytes 98304000 | tf_op jit(solution)/shard_map/gather_weights/pallas_call | solution.py:294
  85.0 5.0 add_convert_fusion.1.qkv_ref
  90.0 9.1 %shard_map.347 = bf16[896,768]{1,0:T(8,128)(2,1)} custom-call(bf16[896,2304]{1,0:T(8,128)(2,1)} %add_convert_fusion.1.qkv_ref), custom_call_target="tpu_custom_call" | custom-call | flops 1233125376 | bytes 5505024 | tf_op jit(solution)/shard_map/pallas_call | solution.py:168
  102.8 5.9 %all-to-all-start = ((bf16[16,56,768]{2,1,0:T(8,128)(2,1)}), bf16[16,56,768]{2,1,0:T(8,128)(2,1)S(1)}, u32[]{:S(2)}, u32[]{:S(2)}) async-start(bf16[16,56,768]{2,1,0:T(8,128)(2,1)} %bitcast.13), calls=%async_computation | async-start | bytes 2752512 | tf_op jit(solution)/shard_map/all_to_all | solution.py:484
  112.8 8.2 %fusion.51 = (bf16[8,4,96,768]{3,2,1,0:T(8,128)(2,1)}, bf16[8,4,96,768]{3,2,1,0:T(8,128)(2,1)}) fusion(bf16[8,4,192,768]{3,2,1,0:T(8,128)(2,1)} %bitcast.173), kind=kLoop, calls=%fused_computation.140 | loop fusion | bytes 18874368 | tf_op jit(solution)/shard_map/slice | solution.py:547
  121.0 21.2 %all-to-all-done = bf16[16,56,768]{2,1,0:T(8,128)(2,1)S(1)} async-done(((bf16[16,56,768]{2,1,0:T(8,128)(2,1)}), bf16[16,56,768]{2,1,0:T(8,128)(2,1)S(1)}, u32[]{:S(2)}, u32[]{:S(2)}) %all-to-all-start) | async-done | bytes 1376288 | tf_op jit(solution)/shard_map/all_to_all | solution.py:484
  147.0 7.3 %add_convert_fusion = bf16[896,2304]{1,0:T(8,128)(2,1)} fusion(bf16[2304,768]{1,0:T(8,128)(2,1)} %bitcast.214, f32[2304]{0:T(1024)S(1)} %get-tuple-element.140, bf16[896,768]{1,0:T(8,128)(2,1)S(1)} %bitcast.157, f32[768]{0:T(1024)S(1)} %copy-done.22, f32[768]{0:T(1024)S(1)} %copy-done.15, f32[896]{0:T(1024)S(1)} %add_rsqrt_fusion.2, ...), kind=kOutput, calls=%fused_computation.13 | convolution fusion | flops 3179151360 | bytes 9066496 | tf_op jit(solution)/shard_map/dot_general | solution.py:26
  154.4 18.3 %shard_map.348 = bf16[16,56,768]{2,1,0:T(8,128)(2,1)} custom-call(bf16[16,56,2304]{2,1,0:T(8,128)(2,1)} %bitcast.166), custom_call_target="tpu_custom_call" | custom-call | flops 704643072 | bytes 5505024 | tf_op jit(solution)/shard_map/pallas_call | solution.py:168
  177.4 13.4 %multiply_convert_fusion = (bf16[896,3072]{1,0:T(8,128)(2,1)}, f32[896,3072]{1,0:T(8,128)}) fusion(f32[3072]{0:T(1024)S(1)} %add.164, bf16[3072,768]{1,0:T(8,128)(2,1)S(1)} %bitcast.182, f32[896,768]{1,0:T(8,128)S(1)} %get-tuple-element.143, f32[768]{0:T(1024)S(1)} %copy-done.21, f32[768]{0:T(1024)S(1)} %copy-done.14, f32[896]{0:T(1024)S(1)} %add_rsqrt_fusion.1, ...), kind=kOutput, calls=%fused_computation.8 | convolution fusion | flops 4247814144 | bytes 24011776 | tf_op jit(solution)/shard_map/dot_general | solution.py:26
  190.9 10.7 %fusion.57 = (bf16[3072]{0:T(1024)(128)(2,1)S(1)}, bf16[896,3072]{1,0:T(8,128)(2,1)S(1)}) fusion(f32[896,3072]{1,0:T(8,128)} %get-tuple-element.145, f32[3072]{0:T(1024)S(1)} %add.164, bf16[896,768]{1,0:T(8,128)(2,1)S(1)} %bitcast.170, bf16[3072,768]{1,0:T(8,128)(2,1)} %bitcast.177), kind=kOutput, calls=%fused_computation.146 | convolution fusion | flops 4260885504 | bytes 22628352 | tf_op jit(solution)/shard_map/dot_general | solution.py:26
  201.6 8.8 %multiply_reduce_fusion = (f32[768]{0:T(1024)S(1)}, f32[896]{0:T(1024)S(1)}, f32[896]{0:T(1024)S(1)}, f32[768]{0:T(1024)S(1)}, f32[896,768]{1,0:T(8,128)}) fusion(f32[896,768]{1,0:T(8,128)S(1)} %copy-done.4, f32[896]{0:T(1024)S(1)} %add_rsqrt_fusion.1, f32[896]{0:T(1024)S(1)} %broadcast_multiply_fusion.7, f32[768]{0:T(1024)S(1)} %copy-done.14, ...), kind=kOutput, calls=%fused_computation.66 | convolution fusion | flops 4234048256 | bytes 15752192 | tf_op jit(solution)/shard_map/dot_general | solution.py:26
  210.5 6.5 %convolution_convert_fusion.1 = bf16[3072,768]{1,0:T(8,128)(2,1)S(1)} fusion(bf16[896,3072]{1,0:T(8,128)(2,1)S(1)} %get-tuple-element.150, f32[896,768]{1,0:T(8,128)S(1)} %copy-done.4, f32[768]{0:T(1024)S(1)} %copy-done.21, f32[768]{0:T(1024)S(1)} %copy-done.14, f32[896]{0:T(1024)S(1)} %add_rsqrt_fusion.1, f32[896]{0:T(1024)S(1)} %broadcast_multiply_fusion.7), kind=kOutput, calls=%fused_computation.17 | convolution fusion | flops 4233658368 | bytes 12989440 | tf_op jit(solution)/shard_map/dot_general | solution.py:26
  217.1 5.5 %convolution_convert_fusion = bf16[3072,768]{1,0:T(8,128)(2,1)S(1)} fusion(bf16[896,3072]{1,0:T(8,128)(2,1)S(1)} %bitcast.221, bf16[896,768]{1,0:T(8,128)(2,1)S(1)} %bitcast.171), kind=kOutput, calls=%fused_computation.16 | convolution fusion | flops 4230217728 | bytes 11599872 | tf_op jit(solution)/shard_map/dot_general | solution.py:26
  231.4 10.3 %add_convert_fusion.2 = bf16[896,768]{1,0:T(8,128)(2,1)} fusion(f32[896,768]{1,0:T(8,128)} %copy-done.3, bf16[896,3072]{1,0:T(8,128)(2,1)} %get-tuple-element.144, bf16[3072,768]{1,0:T(8,128)(2,1)} %bitcast.178, f32[768]{0:T(1024)S(1)} %convert_element_type.212), kind=kOutput, calls=%fused_computation.68 | convolution fusion | flops 4229922816 | bytes 14355456 | tf_op jit(solution)/shard_map/dot_general | solution.py:26
  241.6 6.2 %all-to-all-start.3 = ((bf16[16,56,768]{2,1,0:T(8,128)(2,1)}), bf16[16,56,768]{2,1,0:T(8,128)(2,1)}, u32[]{:S(2)}, u32[]{:S(2)}) async-start(bf16[16,56,768]{2,1,0:T(8,128)(2,1)} %bitcast.195), calls=%async_computation.3 | async-start | bytes 2752512 | tf_op jit(solution)/shard_map/all_to_all | solution.py:484
  252.5 24.1 %shard_map.349 = bf16[16,56,2304]{2,1,0:T(8,128)(2,1)} custom-call(bf16[16,56,2304]{2,1,0:T(8,128)(2,1)} %bitcast.167, bf16[16,56,768]{2,1,0:T(8,128)(2,1)} %bitcast.192), custom_call_target="tpu_custom_call" | custom-call | flops 1761607680 | bytes 9633792 | tf_op jit(solution)/shard_map/pallas_call | solution.py:168
  276.6 7.3 %fusion.21 = (f32[768]{0:T(1024)S(1)}, f32[896]{0:T(1024)S(1)}, f32[896]{0:T(1024)S(1)}, f32[768]{0:T(1024)S(1)}, f32[896,768]{1,0:T(8,128)S(1)}) fusion(bf16[896,768]{1,0:T(8,128)(2,1)S(1)} %bitcast.159, f32[896]{0:T(1024)S(1)} %add_rsqrt_fusion.2, f32[896]{0:T(1024)S(1)} %broadcast_multiply_fusion.8, f32[768]{0:T(1024)S(1)} %copy-done.15, ...), kind=kOutput, calls=%fused_computation.39 | convolution fusion | flops 3177771776 | bytes 11820032 | tf_op jit(solution)/shard_map/dot_general | solution.py:26
  285.9 6.2 %all-to-all-start.2 = ((bf16[16,56,768]{2,1,0:T(8,128)(2,1)}), bf16[16,56,768]{2,1,0:T(8,128)(2,1)}, u32[]{:S(2)}, u32[]{:S(2)}) async-start(bf16[16,56,768]{2,1,0:T(8,128)(2,1)} %bitcast.174), calls=%async_computation.2 | async-start | bytes 2752512 | tf_op jit(solution)/shard_map/all_to_all | solution.py:484
  303.2 7.4 %convolution_convert_fusion.3 = bf16[2304,768]{1,0:T(8,128)(2,1)S(1)} fusion(bf16[896,2304]{1,0:T(8,128)(2,1)} %bitcast.165, bf16[896,768]{1,0:T(8,128)(2,1)S(1)} %bitcast.161, f32[768]{0:T(1024)S(1)} %copy-done.22, f32[768]{0:T(1024)S(1)} %copy-done.15, f32[896]{0:T(1024)S(1)} %add_rsqrt_fusion.2, f32[896]{0:T(1024)S(1)} %broadcast_multiply_fusion.8), kind=kOutput, calls=%fused_computation.19 | convolution fusion | flops 3176792064 | bytes 9057280 | tf_op jit(solution)/shard_map/dot_general | solution.py:26
  314.6 27.6 %all-to-all-done.2 = bf16[16,56,768]{2,1,0:T(8,128)(2,1)} async-done(((bf16[16,56,768]{2,1,0:T(8,128)(2,1)}), bf16[16,56,768]{2,1,0:T(8,128)(2,1)}, u32[]{:S(2)}, u32[]{:S(2)}) %all-to-all-start.2) | async-done | bytes 1376288 | tf_op jit(solution)/shard_map/all_to_all | solution.py:484
  350.2 20.3 %shard_map.350 = bf16[896,2304]{1,0:T(8,128)(2,1)} custom-call(bf16[896,2304]{1,0:T(8,128)(2,1)} %add_convert_fusion.1.qkv_ref, bf16[896,768]{1,0:T(8,128)(2,1)} %convolution_convert_fusion.4.mix_g_ref), custom_call_target="tpu_custom_call" | custom-call | flops 3082813440 | bytes 9633792 | tf_op jit(solution)/shard_map/pallas_call | solution.py:168
  373.5 7.2 %fusion.42 = (f32[768]{0:T(1024)S(1)}, f32[896]{0:T(1024)S(1)}, f32[896]{0:T(1024)S(1)}, f32[768]{0:T(1024)S(1)}, f32[896,768]{1,0:T(8,128)S(1)}) fusion(f32[896]{0:T(1024)S(1)} %div.49, f32[896]{0:T(1024)S(1)} %rsqrt.31, bf16[16,49,768]{2,1,0:T(8,128)(2,1)S(1)} %copy-done.1, f32[768]{0:T(1024)S(1)} %copy-done.13, bf16[896,2304]{1,0:T(8,128)(2,1)} %shard_map.350, ...), kind=kOutput, calls=%fused_computation.64 | convolution fusion | flops 3177771776 | bytes 11648000 | tf_op jit(solution)/shard_map/dot_general | solution.py:26
  385.4 6.5 %convolution_convert_fusion.2 = bf16[2304,768]{1,0:T(8,128)(2,1)S(1)} fusion(bf16[896,2304]{1,0:T(8,128)(2,1)} %shard_map.350, bf16[896,768]{1,0:T(8,128)(2,1)S(1)} %get-tuple-element.131), kind=kOutput, calls=%fused_computation.18 | convolution fusion | flops 3172663296 | bytes 9043968 | tf_op jit(solution)/shard_map/dot_general | solution.py:26
  410.6 90.5 %scatter_sum.1 = (bf16[8,96,768]{2,1,0:T(8,128)(2,1)}, bf16[8,112,768]{2,1,0:T(8,128)(2,1)}) custom-call(bf16[8,4,96,768]{3,2,1,0:T(8,128)(2,1)} %bitcast.163, bf16[8,4,112,768]{3,2,1,0:T(8,128)(2,1)} %bitcast.162), custom_call_target="tpu_custom_call" | custom-call | bytes 300000000 | tf_op jit(solution)/shard_map/scatter_sum/pallas_call | solution.py:449
  (195 shorter events, 108.2 us)
Async XLA Ops:
  7.2 105.6 %all-gather.5.cloned.1.call-start = ((), (), s32[]{:S(2)}) async-start(), calls=%async_computation.6 | async-start | bytes 9732096 | tf_op jit(solution)/shard_map/all_gather | solution.py:487
  13.8 70.0 %copy-start = (bf16[16,49,768]{2,1,0:T(8,128)(2,1)}, bf16[16,49,768]{2,1,0:T(8,128)(2,1)S(1)}, u32[]{:S(2)}) copy-start(bf16[16,49,768]{2,1,0:T(8,128)(2,1)S(1)} %reshape.371) | copy-start | bytes 3612676
  82.3 26.4 %copy-start.9 = (f32[4,1536]{1,0:T(4,128)}, f32[4,1536]{1,0:T(4,128)S(1)}, u32[]{:S(2)}) copy-start(f32[4,1536]{1,0:T(4,128)S(1)} %reshape.415) | copy-start | bytes 73732
  90.0 9.1 %copy-start.19 = (bf16[1,4,8,24,768]{4,3,2,1,0:T(8,128)(2,1)S(1)}, bf16[1,4,8,24,768]{4,3,2,1,0:T(8,128)(2,1)}, u32[]{:S(2)}) copy-start(bf16[1,4,8,24,768]{4,3,2,1,0:T(8,128)(2,1)} %get-tuple-element.41) | copy-start | bytes 3538948
  102.8 5.9 %copy-start.16 = (bf16[768]{0:T(1024)(128)(2,1)S(1)}, bf16[768]{0:T(1024)(128)(2,1)}, u32[]{:S(2)}) copy-start(bf16[768]{0:T(1024)(128)(2,1)} %param.32) | copy-start | bytes 4612
  102.8 5.9 %copy-start.7 = (bf16[4,196,768]{2,0,1:T(4,128)(2,1)S(1)}, bf16[4,196,768]{2,0,1:T(4,128)(2,1)}, u32[]{:S(2)}) copy-start(bf16[4,196,768]{2,0,1:T(4,128)(2,1)} %param.39) | copy-start | bytes 3612676
  102.8 39.4 %all-to-all-start = ((bf16[16,56,768]{2,1,0:T(8,128)(2,1)}), bf16[16,56,768]{2,1,0:T(8,128)(2,1)S(1)}, u32[]{:S(2)}, u32[]{:S(2)}) async-start(bf16[16,56,768]{2,1,0:T(8,128)(2,1)} %bitcast.13), calls=%async_computation | async-start | bytes 2752512 | tf_op jit(solution)/shard_map/all_to_all | solution.py:484
  142.2 4.8 copy-start.15
  142.2 4.8 copy-start.22
  143.0 47.9 %all-to-all-start.1 = ((bf16[16,56,768]{2,1,0:T(8,128)(2,1)}), bf16[16,56,768]{2,1,0:T(8,128)(2,1)S(1)}, u32[]{:S(2)}, u32[]{:S(2)}) async-start(bf16[16,56,768]{2,1,0:T(8,128)(2,1)} %pad.17), calls=%async_computation.1 | async-start | bytes 2752512 | tf_op jit(solution)/shard_map/all_to_all | solution.py:484
  146.8 256.7 %reduce-scatter.2.cloned.1.call-start = ((), (), s32[]{:S(2)}) async-start(), calls=%async_computation.5 | async-start | bytes 9732096 | tf_op jit(solution)/shard_map/reduce_scatter | solution.py:607
  172.6 4.8 slice-start
  172.6 4.8 slice-start.1
  190.9 10.7 %copy-start.4 = (f32[896,768]{1,0:T(8,128)S(1)}, f32[896,768]{1,0:T(8,128)}, u32[]{:S(2)}) copy-start(f32[896,768]{1,0:T(8,128)} %copy-done.3) | copy-start | bytes 8257540
  201.6 15.4 %slice-start.3 = ((s8[5505024]{0:T(1024)(128)(4,1)}), s8[4194304]{0:T(1024)(128)(4,1)S(1)}, s32[]{:S(2)}) async-start(s8[5505024]{0:T(1024)(128)(4,1)} %bitcast.220), calls=%async_computation.11 | async-start | bytes 8388608
  210.5 6.6 %slice-start.4 = ((s8[5505024]{0:T(1024)(128)(4,1)}), s8[1310720]{0:T(1024)(128)(4,1)S(1)}, s32[]{:S(2)}) async-start(s8[5505024]{0:T(1024)(128)(4,1)} %bitcast.220), calls=%async_computation.12 | async-start | bytes 2621440
  241.6 44.3 %all-to-all-start.3 = ((bf16[16,56,768]{2,1,0:T(8,128)(2,1)}), bf16[16,56,768]{2,1,0:T(8,128)(2,1)}, u32[]{:S(2)}, u32[]{:S(2)}) async-start(bf16[16,56,768]{2,1,0:T(8,128)(2,1)} %bitcast.195), calls=%async_computation.3 | async-start | bytes 2752512 | tf_op jit(solution)/shard_map/all_to_all | solution.py:484
  276.6 7.3 %copy-start.2 = (f32[896,768]{1,0:T(8,128)S(1)}, f32[896,768]{1,0:T(8,128)}, u32[]{:S(2)}) copy-start(f32[896,768]{1,0:T(8,128)} %multiply_add_fusion) | copy-start | bytes 8257540
  285.9 56.3 %all-to-all-start.2 = ((bf16[16,56,768]{2,1,0:T(8,128)(2,1)}), bf16[16,56,768]{2,1,0:T(8,128)(2,1)}, u32[]{:S(2)}, u32[]{:S(2)}) async-start(bf16[16,56,768]{2,1,0:T(8,128)(2,1)} %bitcast.174), calls=%async_computation.2 | async-start | bytes 2752512 | tf_op jit(solution)/shard_map/all_to_all | solution.py:484
  292.1 219.2 %all-gather.7.cloned.1.call-start = ((), (), s32[]{:S(2)}) async-start(), calls=%async_computation.7 | async-start | bytes 2654208 | tf_op jit(solution)/shard_map/all_gather | solution.py:685
  311.9 30.4 %copy-start.6 = (bf16[896,768]{1,0:T(8,128)(2,1)S(1)}, bf16[896,768]{1,0:T(8,128)(2,1)}, u32[]{:S(2)}) copy-start(bf16[896,768]{1,0:T(8,128)(2,1)} %shard_map.347) | copy-start | bytes 4128772
  342.2 4.2 copy-start.20
  373.5 7.3 %copy-start.11 = (f32[768]{0:T(1024)S(1)}, f32[768]{0:T(1024)}, u32[]{:S(2)}) copy-start(f32[768]{0:T(1024)} %param.22) | copy-start | bytes 9220
  501.1 3.3 copy-start.8
  (11 other events, 19.3 us)
Sparse Core Ops, SparseCore 0:
  11.4 101.3 all-gather.4
  230.8 166.9 reduce-scatter.1
  403.6 34.9 all-gather.6
